TPU v7x, 32 devices: a whole 2x2x4 slice. The times are simulated.
32 devices in a mesh: freq: 2 (over x), param: 4 (over y, core), sens: 4 (over z).
Axes of the slice: x: 2, y: 2, z: 4, core: 2. Of those that a mesh axis runs over, the one named last changes fastest.
Arguments:
- series: bfloat16 [8, 600, 52], P(None, 'sens', 'freq'), may hold values from -6 to 6
- kernel: bfloat16 [2, 32, 600, 4096], P(None, 'freq', 'sens', 'param'), may hold values from -0.1875 to 0.1875
- prior_spectrum: float32 [32], P('freq'), may hold values from 0.3 to 1.5
- prior_scale: float32 [4096], P('param'), may hold values from 0.5 to 2
Outputs:
- adjoint_map: float32 [52, 8, 4096], P('freq', 'sens', 'param')
All inputs are finite; a program needn't handle non-finite values.
Results may differ from a plain program's by a relative error of at most 0.0047.
Values may be sent and summed in bfloat16 or wider, within the bound.
No kernel may reach another device: no remote copies, remote signals or barrier semaphores. Data moves between devices by JAX's collectives and lax.ppermute only.
A program may use at most 64 MiB of HBM per device.

v0:
```python
import math

import jax
import jax.numpy as jnp
from jax import lax
from jax.sharding import PartitionSpec as P

LEN = 840
FB_DEV = 16


def extended(cells, sides, width):
    for axis, dim in sides:
        count = lax.axis_size(axis)
        ends = count - 1
        head = lax.slice_in_dim(cells, 0, width, axis=dim)
        tail = lax.slice_in_dim(cells, cells.shape[dim] - width, cells.shape[dim], axis=dim)
        cells = jnp.concatenate(
            [
                lax.ppermute(tail, axis, [(i, (i + 1) % count) for i in range(ends)]),
                cells,
                lax.ppermute(head, axis, [((i + 1) % count, i) for i in range(ends)]),
            ],
            axis=dim,
        )
    return cells


def phase_tables(bin_first, bin_count, time_count):
    bin_index = bin_first + jnp.arange(bin_count, dtype=jnp.int32)
    time_index = jnp.arange(time_count, dtype=jnp.int32)
    product = time_index[:, None] * bin_index[None, :] % LEN
    phase_angle = product.astype(jnp.float32) * (2.0 * math.pi / LEN)
    return (jnp.cos(phase_angle), jnp.sin(phase_angle))


def contract(spectrum, operator):
    return jnp.einsum("bsr,bsp->brp", spectrum, operator, preferred_element_type=jnp.float32)


def local(series, kernel, prior_spectrum, prior_scale):
    highest = lax.Precision.HIGHEST
    groups = lax.axis_size("freq")
    first_bin = lax.axis_index("freq") * FB_DEV
    probes, sens_dev, time_dev = series.shape
    total_times = time_dev * groups
    cosine, sine_part = phase_tables(first_bin, FB_DEV, total_times)
    phase_table = jnp.concatenate([cosine, -sine_part], axis=1)
    series_piece = lax.all_gather(series, "freq", axis=2, tiled=True)
    row_count = series_piece.shape[2]
    flat_rows = series_piece.astype(jnp.float32).reshape(-1, row_count)
    spectra = jnp.dot(flat_rows, phase_table, precision=highest)
    spectra = (spectra * (1.0 / math.sqrt(total_times))).astype(jnp.bfloat16)
    both_parts = (
        spectra.reshape(probes, sens_dev, 2, FB_DEV)
        .transpose(3, 1, 2, 0)
        .reshape(FB_DEV, sens_dev, 2 * probes)
    )
    with_real = contract(both_parts, kernel[0])
    with_imag = contract(both_parts, kernel[1])
    real_part = with_real[:, :probes] + with_imag[:, probes:]
    imag_part = with_real[:, probes:] - with_imag[:, :probes]
    partial_value = jnp.stack([real_part, imag_part])
    summed = lax.psum_scatter(partial_value, "sens", scatter_dimension=2, tiled=True)
    weights = prior_spectrum * (1.0 / math.sqrt(FB_DEV * groups))
    scaled_spec = summed * weights[None, :, None, None]
    arrived = lax.all_to_all(scaled_spec, "freq", split_axis=3, concat_axis=1, tiled=True)
    bin_total = arrived.shape[1]
    item_count = arrived.shape[2]
    col_count = arrived.shape[3]
    cos_all, sin_all = phase_tables(0, bin_total, total_times)
    full_table = jnp.concatenate([cos_all, -sin_all], axis=1)
    flat_rows = arrived.reshape(2 * bin_total, item_count * col_count)
    arranged = jnp.dot(full_table, flat_rows, precision=highest).reshape(
        total_times, item_count, col_count
    )
    image_field = lax.all_to_all(arranged, "freq", split_axis=0, concat_axis=2, tiled=True)
    weighted = image_field * prior_scale
    padded = extended(weighted, (("param", 2),), 1)
    smooth = 0.5 * weighted + 0.25 * (padded[:, :, :-2] + padded[:, :, 2:])
    return smooth * prior_scale


def solution(mesh):
    placed = (P(None, "sens", "freq"), P(None, "freq", "sens", "param"), P("freq"), P("param"))
    return jax.shard_map(
        local, mesh=mesh, in_specs=placed, out_specs=P("freq", "sens", "param"), check_vma=False
    )
```

profile of v0, /device:TPU:1, one launch (start us, length us, event | category | flops | bytes accessed | tf_op | source)
XLA Modules:
  0.0 111.2 jit_solution(6841817095177923095)
XLA Ops:
  6.5 0.0 reduce-scatter.2.cloned.1.call-start
  6.5 0.1 fusion.32
  6.7 5.6 %all_gather.3 = bf16[8,150,52]{1,0,2:T(8,128)(2,1)S(1)} all-gather(bf16[8,150,26]{1,0,2:T(8,128)(2,1)} %param.4), channel_id=1, replica_groups=mesh['freq'=2,'param'=4,'sens'=4] {'freq'}, dimensions={2}, use_global_device_ids=true | all-gather | bytes 187200 | tf_op jit(solution)/shard_map/all_gather | solution.py:49
  12.3 0.2 reshape.21
  12.5 0.2 fusion.3
  12.8 0.2 reshape.22
  13.0 7.8 %fusion.36 = (bf16[1,16,150,1024]{3,1,2,0:T(8,128)(2,1)S(1)}, bf16[1,16,150,1024]{3,1,2,0:T(8,128)(2,1)}) fusion(bf16[2,16,150,1024]{3,1,2,0:T(8,128)(2,1)} %param.5), kind=kLoop, calls=%fused_computation.55 | loop fusion | bytes 19660800 | tf_op jit(solution)/shard_map/slice | solution.py:59
  20.8 7.8 %fusion = f32[16,16,1024]{2,1,0:T(8,128)S(1)} fusion(bf16[1,16,150,1024]{3,1,2,0:T(8,128)(2,1)} %get-tuple-element.6, bf16[8,150,2,16]{1,0,3,2:T(8,128)(2,1)S(1)} %reshape.22), kind=kOutput, calls=%fused_computation.1 | convolution fusion | flops 78643200 | bytes 6040576 | tf_op jit(solution)/shard_map/bsr,bsp->brp/dot_general | solution.py:38
  28.6 5.6 %fusion.1 = f32[16,16,1024]{2,1,0:T(8,128)S(1)} fusion(bf16[1,16,150,1024]{3,1,2,0:T(8,128)(2,1)S(1)} %get-tuple-element.5, bf16[8,150,2,16]{1,0,3,2:T(8,128)(2,1)S(1)} %reshape.22), kind=kOutput, calls=%fused_computation.3 | convolution fusion | flops 78643200 | bytes 6040576 | tf_op jit(solution)/shard_map/bsr,bsp->brp/dot_general | solution.py:38
  34.2 0.0 copy-start.1
  34.2 0.1 fusion.5
  34.3 0.1 pad_maximum_fusion
  34.4 1.6 %copy.43 = f32[2,16,8,1024]{3,1,0,2:T(8,128)} copy(f32[2,16,8,1024]{3,2,1,0:T(8,128)S(1)} %pad_maximum_fusion) | data formatting | bytes 2097152 | tf_op jit(solution)/shard_map/stack | solution.py:63
  36.0 0.0 reduce-scatter.2.cloned.1.call-update
  36.0 0.0 copy-done.1
  36.0 29.0 %reduce-scatter.2.cloned.1.call-done = f32[2,16,2,1024]{3,1,0,2:T(8,128)} async-done(((f32[2,16,8,1024]{3,1,0,2:T(8,128)}), f32[2,16,2,1024]{3,1,0,2:T(8,128)}) %reduce-scatter.2.cloned.1.call-update) | async-done | bytes 262160 | tf_op jit(solution)/shard_map/reduce_scatter | solution.py:64
  65.1 1.0 broadcast_multiply_fusion
  66.1 1.3 %copy.44 = f32[2,16,2,1024]{1,2,0,3:T(2,128)S(1)} copy(f32[2,16,2,1024]{3,1,0,2:T(8,128)S(1)} %broadcast_multiply_fusion) | data formatting | bytes 524288 | tf_op jit(solution)/shard_map/mul | solution.py:66
  67.5 0.0 copy-start
  67.5 3.6 %reshape.26 = f32[2,1,32768]{2,1,0:T(1,128)} reshape(f32[1024,2,2,16]{3,2,1,0:T(2,128)S(1)} %bitcast.53) | data formatting | bytes 524288
  71.0 3.4 %all-to-all-start = ((f32[2,1,32768]{2,1,0:T(1,128)}), f32[2,1,32768]{2,1,0:T(1,128)S(1)}, u32[]{:S(2)}, u32[]{:S(2)}) async-start(f32[2,1,32768]{2,1,0:T(1,128)} %reshape.26), calls=%async_computation.1 | async-start | bytes 524288 | tf_op jit(solution)/shard_map/all_to_all | solution.py:67
  74.5 0.1 sine_negate_fusion
  74.6 3.9 %all-to-all-done = f32[2,1,32768]{2,1,0:T(1,128)S(1)} async-done(((f32[2,1,32768]{2,1,0:T(1,128)}), f32[2,1,32768]{2,1,0:T(1,128)S(1)}, u32[]{:S(2)}, u32[]{:S(2)}) %all-to-all-start) | async-done | bytes 262176 | tf_op jit(solution)/shard_map/all_to_all | solution.py:67
  78.5 0.5 broadcast.17
  79.0 1.4 %reduce = f32[2,32768]{1,0:T(2,128)S(1)} reduce(f32[2,1,32768]{2,1,0:T(1,128)S(1)} %all-to-all-done, f32[]{:T(128)} %broadcast.17), dimensions={1}, to_apply=%all_to_all.24.reduce_sub_computation | reduce | bytes 524292 | tf_op jit(solution)/shard_map/all_to_all | solution.py:67
  80.5 2.8 %reshape.27 = f32[1024,2,2,16]{3,2,1,0:T(2,128)S(1)} reshape(f32[2,32768]{1,0:T(2,128)S(1)} %reduce) | data formatting | bytes 524288
  83.3 1.5 %copy.45 = f32[2,16,2,2,512]{4,2,1,3,0:T(2,128)S(1)} copy(f32[2,16,2,2,512]{1,2,0,4,3:T(2,128)S(1)} %bitcast.54) | data formatting | bytes 524288 | tf_op jit(solution)/shard_map/all_to_all | solution.py:67
  84.7 0.4 fusion.6
  85.1 0.2 copy.47
  85.3 6.1 %all_to_all.33 = f32[52,2,512]{2,1,0:T(2,128)S(1)} all-to-all(f32[52,2,512]{2,1,0:T(2,128)S(1)} %copy.47), channel_id=1, replica_groups=mesh['freq'=2,'param'=4,'sens'=4] {'freq'}, dimensions={0} | all-to-all | bytes 425984 | tf_op jit(solution)/shard_map/all_to_all | solution.py:77
  91.4 0.0 copy-done
  91.5 0.1 broadcast_multiply_fusion.1
  91.5 0.1 fusion.37
  91.6 6.4 %collective-permute-start = (f32[26,2,1]{2,1,0:T(2,128)S(1)}, f32[26,2,1]{2,1,0:T(2,128)S(1)}, u32[]{:S(2)}, u32[]{:S(2)}) collective-permute-start(f32[26,2,1]{2,1,0:T(2,128)S(1)} %get-tuple-element.9), channel_id=1, source_target_pairs={{0,4},{4,8},{8,12},{1,5},{5,9},{9,13},{2,6},{6,10},{10,14},{3,7},{... | collective-permute-start | bytes 632 | tf_op jit(solution)/shard_map/ppermute | solution.py:20
  98.0 1.9 %collective-permute-start.1 = (f32[26,2,1]{2,1,0:T(2,128)S(1)}, f32[26,2,1]{2,1,0:T(2,128)S(1)}, u32[]{:S(2)}, u32[]{:S(2)}) collective-permute-start(f32[26,2,1]{2,1,0:T(2,128)S(1)} %get-tuple-element.10), channel_id=1, source_target_pairs={{4,0},{8,4},{12,8},{5,1},{9,5},{13,9},{6,2},{10,6},{14,10},{7,3},{... | collective-permute-start | bytes 632 | tf_op jit(solution)/shard_map/ppermute | solution.py:22
  99.9 0.0 collective-permute-done
  99.9 3.2 %collective-permute-done.1 = f32[26,2,1]{2,1,0:T(2,128)S(1)} collective-permute-done((f32[26,2,1]{2,1,0:T(2,128)S(1)}, f32[26,2,1]{2,1,0:T(2,128)S(1)}, u32[]{:S(2)}, u32[]{:S(2)}) %collective-permute-start.1) | collective-permute-done | bytes 240 | tf_op jit(solution)/shard_map/ppermute | solution.py:22
  103.2 1.2 %fusion.12 = f32[26,2,1024]{2,1,0:T(2,128)} fusion(f32[26,2,1]{2,1,0:T(2,128)S(1)} %collective-permute-done.1, f32[26,2,1024]{2,1,0:T(2,128)S(1)} %broadcast_multiply_fusion.1, f32[26,2,1]{2,1,0:T(2,128)S(1)} %collective-permute-done, f32[1024]{0:T(1024)S(1)} %copy-done), kind=kLoop, calls=%fused_computation.20 | loop fusion | flops 372736 | bytes 430496 | tf_op jit(solution)/shard_map/mul | solution.py:81
  (3 shorter events, 0.0 us)
Async XLA Ops:
  6.5 58.5 %reduce-scatter.2.cloned.1.call-start = ((), (), s32[]{:S(2)}) async-start(), calls=%async_computation.3 | async-start | bytes 1310720 | tf_op jit(solution)/shard_map/reduce_scatter | solution.py:64
  34.2 1.8 %copy-start.1 = (f32[16]{0:T(128)S(1)}, f32[16]{0:T(128)}, u32[]{:S(2)}) copy-start(f32[16]{0:T(128)} %param.6) | copy-start | bytes 196
  67.5 24.0 %copy-start = (f32[1024]{0:T(1024)S(1)}, f32[1024]{0:T(1024)}, u32[]{:S(2)}) copy-start(f32[1024]{0:T(1024)} %param.7) | copy-start | bytes 12292
  71.0 7.5 %all-to-all-start = ((f32[2,1,32768]{2,1,0:T(1,128)}), f32[2,1,32768]{2,1,0:T(1,128)S(1)}, u32[]{:S(2)}, u32[]{:S(2)}) async-start(f32[2,1,32768]{2,1,0:T(1,128)} %reshape.26), calls=%async_computation.1 | async-start | bytes 524288 | tf_op jit(solution)/shard_map/all_to_all | solution.py:67
  91.6 8.3 %collective-permute-start = (f32[26,2,1]{2,1,0:T(2,128)S(1)}, f32[26,2,1]{2,1,0:T(2,128)S(1)}, u32[]{:S(2)}, u32[]{:S(2)}) collective-permute-start(f32[26,2,1]{2,1,0:T(2,128)S(1)} %get-tuple-element.9), channel_id=1, source_target_pairs={{0,4},{4,8},{8,12},{1,5},{5,9},{9,13},{2,6},{6,10},{10,14},{3,7},{... | collective-permute-start | bytes 632 | tf_op jit(solution)/shard_map/ppermute | solution.py:20
  98.0 5.2 %collective-permute-start.1 = (f32[26,2,1]{2,1,0:T(2,128)S(1)}, f32[26,2,1]{2,1,0:T(2,128)S(1)}, u32[]{:S(2)}, u32[]{:S(2)}) collective-permute-start(f32[26,2,1]{2,1,0:T(2,128)S(1)} %get-tuple-element.10), channel_id=1, source_target_pairs={{4,0},{8,4},{12,8},{5,1},{9,5},{13,9},{6,2},{10,6},{14,10},{7,3},{... | collective-permute-start | bytes 632 | tf_op jit(solution)/shard_map/ppermute | solution.py:22
Sparse Core Ops, SparseCore 0:
  36.1 28.8 reduce-scatter.1
where the time goes:
time: 112 us; the launch traced here: 111 us
  waiting for transfers between devices  36.2 us (32%)
  local copies, waits for them, and re-layouts  19.8 us (18%)
  matrix products  14 us (12%)
  between operations  13.6 us (12%)
  starting transfers between devices  11.7 us (10%)
  blocking collectives  11.7 us (10%)
  other arithmetic  4.27 us (4%)
    reduce_scatter x1, waiting for transfers between devices, local(): lax.psum_scatter(partial_value, 'sens', scatter_dimension=2, tiled=True)  29 us
    dot_general x2, matrix products, contract(): jnp.einsum('bsr,bsp->brp', spectrum, operator, preferred_element_type=jnp...  13.4 us
    slice x1, local copies, waits for them, and re-layouts, local(): with_real = contract(both_parts, kernel[0])  7.77 us
    unnamed x6, local copies, waits for them, and re-layouts  6.39 us
    ppermute x1, starting transfers between devices, extended(): lax.ppermute(tail, axis, [(i, (i + 1) % count) for i in range(ends)])  6.36 us
    all_to_all x1, blocking collectives, local(): lax.all_to_all(arranged, 'freq', split_axis=0, concat_axis=2, tiled=True)  6.12 us
    all_gather x1, blocking collectives, local(): series_piece = lax.all_gather(series, 'freq', axis=2, tiled=True)  5.63 us
    all_to_all x1, waiting for transfers between devices, local(): lax.all_to_all(scaled_spec, 'freq', split_axis=3, concat_axis=1, tiled=True)  3.86 us
  transfers between devices with their start and end apart: 4, of which 3 were waited for; matrix products, arithmetic and copies ran while one was open for 0% of the time, Pallas kernels for 0%

commit v1 on v0

v1 whole, which is shorter than its diff:
```python
import functools
import math

import jax
import jax.numpy as jnp
from jax import lax
from jax.experimental import pallas as pl
from jax.experimental.pallas import tpu as pltpu
from jax.sharding import PartitionSpec as P

LEN = 840
BF = jnp.bfloat16
F32 = jnp.float32


def vmem():
    return pl.BlockSpec(memory_space=pltpu.VMEM)


def call(body, name, out_shape, *args, limit=40 << 20):
    return pl.pallas_call(
        body,
        in_specs=[vmem()] * len(args),
        out_specs=jax.tree.map(lambda _: vmem(), out_shape),
        out_shape=out_shape,
        compiler_params=pltpu.CompilerParams(vmem_limit_bytes=limit),
        name=name,
    )(*args)


def wave(product, part):
    angle = ((product + part * (LEN // 4)) % LEN).astype(F32) * (2.0 * math.pi / LEN)
    return jnp.cos(angle)


def split_index(flat, sizes):
    out = []
    for size in reversed(sizes):
        out.append(flat % size)
        flat = flat // size
    return out[::-1]


def iota(shape, dim):
    return lax.broadcasted_iota(jnp.int32, shape, dim)


def forward_table(piece, bins, times, probes, group):
    freq, sens = lax.axis_index("freq"), lax.axis_index("sens")
    freqs, senss = lax.axis_size("freq"), lax.axis_size("sens")
    shape = (senss * 2 * bins * group, times * probes)
    shift, part, bin_at, inner = split_index(iota(shape, 0), (senss, 2, bins, group))
    time, probe = split_index(iota(shape, 1), (times, probes))
    time = time + (freq + piece) % freqs * times
    hit = probe == (sens + shift) % senss * group + inner
    value = wave((freq * bins + bin_at) * time, part) * (1.0 / math.sqrt(times * freqs))
    return jnp.where(hit, value, 0.0)


def inverse_table(weights, bins, times, group, rows):
    freq, freqs = lax.axis_index("freq"), lax.axis_size("freq")
    shape = (freqs * rows, 2 * bins * group)
    shift, row = split_index(iota(shape, 0), (freqs, rows))
    time, outer = split_index(row, (times + 1, group))
    part, bin_at, inner = split_index(iota(shape, 1), (2, bins, group))
    hit = (outer == inner) & (row < times * group)
    time = time + (freq + shift) % freqs * times
    value = wave((freq * bins + bin_at) * time, part)
    weight = jnp.broadcast_to(weights[None, :, None], (2, bins, group)).reshape(1, -1)
    return jnp.where(hit, value * weight, 0.0)


def contract_body(bins, blocks, pieces, *refs):
    tables = refs[: 2 * pieces]
    series = refs[2 * pieces : 3 * pieces]
    spread, operator = refs[3 * pieces : 3 * pieces + 2]
    outs = refs[3 * pieces + 2 :]
    spec = None
    for i in range(2 * pieces):
        term = jnp.dot(tables[i][...], series[i // 2][...], preferred_element_type=F32)
        spec = term if spec is None else spec + term
    rows = spec.shape[0]
    inner = operator.shape[0] // 2
    block = rows // blocks
    half = block // 2
    group = half // bins
    wide = jnp.dot(spec.astype(BF), spread[...], preferred_element_type=F32)
    keep = iota(wide.shape, 0) // group % bins == iota(wide.shape, 1) % bins
    wide = jnp.where(keep, wide, 0.0).astype(BF)
    turned = []
    for i in range(blocks):
        turned += [wide[i * block + half : (i + 1) * block], -wide[i * block : i * block + half]]
    total = jnp.dot(wide, operator[:inner], preferred_element_type=F32)
    total = total + jnp.dot(
        jnp.concatenate(turned, axis=0), operator[inner:], preferred_element_type=F32
    )
    for i, out in enumerate(outs):
        out[...] = total[i * block : (i + 1) * block].astype(out.dtype)


def image_body(rows, *refs):
    table, own = refs[:2]
    count = table.shape[0] // rows
    outs = refs[len(refs) - count :]
    total = own[...]
    for other in refs[2 : len(refs) - count]:
        total = total + other[...].astype(F32)
    image = jnp.dot(
        table[...], total, precision=lax.Precision.HIGHEST, preferred_element_type=F32
    )
    for i, out in enumerate(outs):
        out[...] = image[i * rows : (i + 1) * rows].astype(out.dtype)


def rotate(value, axis, shift):
    size = lax.axis_size(axis)
    return lax.ppermute(value, axis, [(i, (i + shift) % size) for i in range(size)])


def local(series, kernel, prior_spectrum, prior_scale):
    freqs, senss, params = (lax.axis_size(a) for a in ("freq", "sens", "param"))
    probes, sens_dev, times = series.shape
    bins, cols = kernel.shape[1], kernel.shape[3]
    group = probes // senss
    block = 2 * bins * group
    own_series = series.transpose(2, 0, 1).reshape(times * probes, sens_dev)
    pieces = [own_series] + [rotate(own_series, "freq", -j) for j in range(1, freqs)]
    tables = []
    for j in range(freqs):
        full = forward_table(j, bins, times, probes, group)
        high = lax.reduce_precision(full, 8, 7)
        tables += [high.astype(BF), (full - high).astype(BF)]
    operator = kernel.transpose(0, 2, 1, 3).reshape(2 * sens_dev * bins, cols)
    spread_shape = (sens_dev, sens_dev * bins)
    spread = (iota(spread_shape, 0) == iota(spread_shape, 1) // bins).astype(BF)
    partial = call(
        functools.partial(contract_body, bins, senss, freqs),
        "contract",
        [jax.ShapeDtypeStruct((block, cols), BF if i else F32) for i in range(senss)],
        *tables, *pieces, spread, operator,
    )
    order = sorted(range(1, senss), key=lambda d: -min(d, senss - d))
    arrived = [rotate(partial[d], "sens", d) for d in order]
    rows = -(-times * group // 8) * 8
    weights = prior_spectrum * (1.0 / math.sqrt(bins * freqs))
    image = call(
        functools.partial(image_body, rows),
        "image",
        [jax.ShapeDtypeStruct((rows, cols), BF if i else F32) for i in range(freqs)],
        inverse_table(weights, bins, times, group, rows), partial[0], *arrived,
    )
    total = image[0]
    for j in range(1, freqs):
        total = total + rotate(image[j], "freq", j).astype(F32)
    weighted = total[: times * group].reshape(times, group, cols) * prior_scale
    right = [(i, i + 1) for i in range(params - 1)]
    left = [(i + 1, i) for i in range(params - 1)]
    before = lax.ppermute(weighted[:, :, cols - 1 :], "param", right)
    after = lax.ppermute(weighted[:, :, :1], "param", left)
    padded = jnp.concatenate([before, weighted, after], axis=2)
    smooth = 0.5 * weighted + 0.25 * (padded[:, :, :-2] + padded[:, :, 2:])
    return smooth * prior_scale


def solution(mesh):
    placed = (P(None, "sens", "freq"), P(None, "freq", "sens", "param"), P("freq"), P("param"))
    return jax.shard_map(
        local, mesh=mesh, in_specs=placed, out_specs=P("freq", "sens", "param"), check_vma=False
    )
```

time: 112 us -> 44 us (0.39)
  waiting for transfers between devices: 36.2 us -> 12.2 us
  local copies, waits for them, and re-layouts: 19.8 us -> 4.19 us
  matrix products: 14 us -> 0 us
  between operations: 13.6 us -> 0.22 us
  blocking collectives: 11.7 us -> 0 us
  starting transfers between devices: 11.7 us -> 16.4 us
  Pallas kernels: 0 us -> 4.36 us
  other arithmetic: 4.27 us -> 5.71 us
    reduce_scatter x1 -> x0, waiting for transfers between devices: 29 us -> none  [local(): lax.psum_scatter(partial_value, 'sens', scatter_dimension=2, tiled=True)]
    dot_general x4 -> x0, matrix products: 14 us -> none  [the longest x2 13.4 us: contract(): jnp.einsum('bsr,bsp->brp', spectrum, operator, preferred_element_type=jnp...]
    ppermute x2 -> x7, waiting for transfers between devices: 3.23 us -> 12.2 us  [the longest x5 9.01 us: rotate(): lax.ppermute(value, axis, [(i, (i + shift) % size) for i in range(size)])]
    ppermute x2 -> x7, starting transfers between devices: 8.28 us -> 16.4 us  [the longest x5 7.74 us: rotate(): lax.ppermute(value, axis, [(i, (i + shift) % size) for i in range(size)])]
    slice x2 -> x1, local copies, waits for them, and re-layouts: 7.86 us -> 0.09 us  [local(): before = lax.ppermute(weighted[:, :, cols - 1:], 'param', right)]
    all_to_all x1 -> x0, blocking collectives: 6.12 us -> none  [local(): lax.all_to_all(arranged, 'freq', split_axis=0, concat_axis=2, tiled=True)]
    all_gather x1 -> x0, blocking collectives: 5.63 us -> none  [local(): series_piece = lax.all_gather(series, 'freq', axis=2, tiled=True)]
    pallas_call x0 -> x2, Pallas kernels: none -> 4.36 us  [call(): pl.pallas_call(body, in_specs=[vmem()] * len(args), out_specs=jax.tree.ma...]
  transfers between devices with their start and end apart: 4 -> 7, of which waited for: 3 -> 4; matrix products, arithmetic and copies ran while one was open for 0% -> 11% of each run, Pallas kernels for 0% -> 0%
where the time goes in v1:
time: 44 us; the launch traced here: 43.1 us
  starting transfers between devices  16.4 us (37%)
  waiting for transfers between devices  12.2 us (28%)
  other arithmetic  5.71 us (13%)
  Pallas kernels  4.36 us (10%)
  local copies, waits for them, and re-layouts  4.19 us (10%)
    ppermute x5, waiting for transfers between devices, rotate(): lax.ppermute(value, axis, [(i, (i + shift) % size) for i in range(size)])  9.01 us
    ppermute x5, starting transfers between devices, rotate(): lax.ppermute(value, axis, [(i, (i + shift) % size) for i in range(size)])  7.74 us
    ppermute x1, starting transfers between devices, local(): before = lax.ppermute(weighted[:, :, cols - 1:], 'param', right)  6.77 us
    pallas_call x2, Pallas kernels, call(): pl.pallas_call(body, in_specs=[vmem()] * len(args), out_specs=jax.tree.ma...  4.36 us
    unnamed x6, local copies, waits for them, and re-layouts  3.8 us
    ppermute x1, waiting for transfers between devices, local(): after = lax.ppermute(weighted[:, :, :1], 'param', left)  3.23 us
    convert_element_type x1, other arithmetic, local(): tables += [high.astype(BF), (full - high).astype(BF)]  3.01 us
    ppermute x1, starting transfers between devices, local(): after = lax.ppermute(weighted[:, :, :1], 'param', left)  1.92 us
  transfers between devices with their start and end apart: 7, of which 4 were waited for; matrix products, arithmetic and copies ran while one was open for 11% of the time, Pallas kernels for 0%

profile of v1, /device:TPU:1, one launch (start us, length us, event | category | flops | bytes accessed | tf_op | source)
XLA Modules:
  0.0 43.1 jit_solution(8882422494139577984)
XLA Ops:
  0.0 0.0 copy-start.1
  0.0 2.0 %collective-permute-start = (bf16[208,150]{1,0:T(8,128)(2,1)}, bf16[208,150]{1,0:T(8,128)(2,1)S(1)}, u32[]{:S(2)}, u32[]{:S(2)}) collective-permute-start(bf16[208,150]{1,0:T(8,128)(2,1)} %bitcast.7), channel_id=1, source_target_pairs={{0,16},{16,0},{1,17},{17,1},{2,18},{18,2},{3,19},{19,3},{4,20},{20... | collective-permute-start | bytes 187208 | tf_op jit(solution)/shard_map/ppermute | solution.py:117
  2.2 0.7 %broadcast_multiply_fusion.1 = f32[16]{0:T(128)S(1)} fusion(f32[16]{0:T(128)} %param.6), kind=kLoop, calls=%fused_computation.160 | loop fusion | flops 16 | bytes 128 | tf_op jit(solution)/shard_map/mul | solution.py:145
  2.9 0.1 broadcast_in_dim.17
  2.9 0.1 mul.108
  3.0 0.1 fusion.refs_6_
  3.2 3.0 %fusion.2 = (bf16[256,208]{1,0:T(8,128)(2,1)S(1)}, bf16[256,208]{1,0:T(8,128)(2,1)S(1)}, bf16[256,208]{1,0:T(8,128)(2,1)S(1)}, bf16[256,208]{1,0:T(8,128)(2,1)S(1)}) fusion(s32[]{:T(128)S(6)} %mul.117, s32[208]{0:T(256)S(1)} %get-tuple-element.41, s32[208]{0:T(256)S(1)} %get-tuple-element.44, pred[208]{0:T(512)(128)(4,1)S(1)} %get-tuple-element.37, ...), kind=kLoop, calls=%fused_computation.29 | loop fusion | flops 5857280 | bytes 434352 | tf_op jit(solution)/shard_map/convert_element_type | solution.py:132
  6.2 0.0 collective-permute-done.refs_5_
  6.2 0.0 copy-done.1
  6.2 0.0 copy-start
  6.2 3.8 %copy-done = bf16[2,16,150,1024]{3,1,2,0:T(8,128)(2,1)S(1)} copy-done((bf16[2,16,150,1024]{3,1,2,0:T(8,128)(2,1)S(1)}, bf16[2,16,150,1024]{3,1,2,0:T(8,128)(2,1)}, u32[]{:S(2)}) %copy-start) | copy-done | bytes 9830424
  10.0 3.8 %contract.1 = (f32[64,1024]{1,0:T(8,128)S(1)}, bf16[64,1024]{1,0:T(8,128)(2,1)S(1)}, bf16[64,1024]{1,0:T(8,128)(2,1)S(1)}, bf16[64,1024]{1,0:T(8,128)(2,1)S(1)}) custom-call(bf16[256,208]{1,0:T(8,128)(2,1)S(1)} %get-tuple-element.21.refs_0_, bf16[256,208]{1,0:T(8,128)(2,1)S(1)} %get-tuple-element.20.refs_1_, bf16[256,208]{1,0:T(8,128)(2,1)S(1)} %get-tuple-element.22.refs_2_, ...), custom_call_target="tpu_custom_call" | custom-call | tf_op jit(solution)/shard_map/contract/pallas_call | solution.py:21
  13.9 0.0 copy-start.2
  13.9 2.4 %collective-permute-start.1 = (bf16[64,1024]{1,0:T(8,128)(2,1)S(1)}, bf16[64,1024]{1,0:T(8,128)(2,1)S(1)}, u32[]{:S(2)}, u32[]{:S(2)}) collective-permute-start(bf16[64,1024]{1,0:T(8,128)(2,1)S(1)} %get-tuple-element.12), channel_id=1, source_target_pairs={{0,2},{1,3},{2,0},{3,1},{4,6},{5,7},{6,4},{7,5},{8,10},{9,11},{10,... | collective-permute-start | bytes 393224 | tf_op jit(solution)/shard_map/ppermute | solution.py:117
  16.2 1.3 %collective-permute-start.2 = (bf16[64,1024]{1,0:T(8,128)(2,1)S(1)}, bf16[64,1024]{1,0:T(8,128)(2,1)S(1)}, u32[]{:S(2)}, u32[]{:S(2)}) collective-permute-start(bf16[64,1024]{1,0:T(8,128)(2,1)S(1)} %get-tuple-element.13), channel_id=1, source_target_pairs={{0,1},{1,2},{2,3},{3,0},{4,5},{5,6},{6,7},{7,4},{8,9},{9,10},{10,1... | collective-permute-start | bytes 393224 | tf_op jit(solution)/shard_map/ppermute | solution.py:117
  17.5 2.0 %collective-permute-start.3 = (bf16[64,1024]{1,0:T(8,128)(2,1)S(1)}, bf16[64,1024]{1,0:T(8,128)(2,1)S(1)}, u32[]{:S(2)}, u32[]{:S(2)}) collective-permute-start(bf16[64,1024]{1,0:T(8,128)(2,1)S(1)} %get-tuple-element.14), channel_id=1, source_target_pairs={{0,3},{1,0},{2,1},{3,2},{4,7},{5,4},{6,5},{7,6},{8,11},{9,8},{10,9... | collective-permute-start | bytes 393224 | tf_op jit(solution)/shard_map/ppermute | solution.py:117
  19.5 0.5 %fusion.51.refs_0_ = f32[112,64]{1,0:T(8,128)S(1)} fusion(f32[64]{0:T(128)S(1)} %mul.108, s32[112]{0:T(128)S(1)} %get-tuple-element.27, s32[112]{0:T(128)S(1)} %get-tuple-element.31, s32[]{:T(128)S(6)} %axis_index.15, s32[64]{0:T(128)S(1)} %get-tuple-element.29, s32[64]{0:T(128)S(1)} %get-tuple-element.33, s32[]{:T(128)S(6)} %mul.99, ...), kind=kLoop, calls=%fused_computation.116 | loop fusion | flops 723968 | bytes 32104 | tf_op jit(solution)/shard_map/jit(_where)/select_n | solution.py:70
  20.0 4.5 %collective-permute-done.1.refs_2_ = bf16[64,1024]{1,0:T(8,128)(2,1)S(1)} collective-permute-done((bf16[64,1024]{1,0:T(8,128)(2,1)S(1)}, bf16[64,1024]{1,0:T(8,128)(2,1)S(1)}, u32[]{:S(2)}, u32[]{:S(2)}) %collective-permute-start.1) | collective-permute-done | bytes 131104 | tf_op jit(solution)/shard_map/ppermute | solution.py:117
  24.5 0.0 collective-permute-done.2.refs_3_
  24.5 0.8 %collective-permute-done.3.refs_4_ = bf16[64,1024]{1,0:T(8,128)(2,1)S(1)} collective-permute-done((bf16[64,1024]{1,0:T(8,128)(2,1)S(1)}, bf16[64,1024]{1,0:T(8,128)(2,1)S(1)}, u32[]{:S(2)}, u32[]{:S(2)}) %collective-permute-start.3) | collective-permute-done | bytes 131104 | tf_op jit(solution)/shard_map/ppermute | solution.py:117
  25.4 0.5 %image.1 = (f32[56,1024]{1,0:T(8,128)S(1)}, bf16[56,1024]{1,0:T(8,128)(2,1)S(1)}) custom-call(f32[112,64]{1,0:T(8,128)S(1)} %fusion.51.refs_0_, f32[64,1024]{1,0:T(8,128)S(1)} %get-tuple-element.11.refs_1_, bf16[64,1024]{1,0:T(8,128)(2,1)S(1)} %collective-permute-done.1.refs_2_, bf16[64,1024]{1,0:T(8,128)(2,1)S(1)} %collective-permute-done.2.refs_3_, ...), custom_call_target="tpu_custom_call" | custom-call | tf_op jit(solution)/shard_map/image/pallas_call | solution.py:21
  25.9 0.1 collective-permute-start.4
  26.0 3.6 %collective-permute-done.4 = bf16[56,1024]{1,0:T(8,128)(2,1)S(1)} collective-permute-done((bf16[56,1024]{1,0:T(8,128)(2,1)S(1)}, bf16[56,1024]{1,0:T(8,128)(2,1)S(1)}, u32[]{:S(2)}, u32[]{:S(2)}) %collective-permute-start.4) | collective-permute-done | bytes 114720 | tf_op jit(solution)/shard_map/ppermute | solution.py:117
  29.7 0.1 reshape.15
  29.8 0.0 copy-done.2
  29.8 0.1 broadcast_multiply_fusion
  29.9 0.1 fusion.69
  30.0 6.8 %collective-permute-start.5 = (f32[26,2,1]{2,1,0:T(2,128)S(1)}, f32[26,2,1]{2,1,0:T(2,128)S(1)}, u32[]{:S(2)}, u32[]{:S(2)}) collective-permute-start(f32[26,2,1]{2,1,0:T(2,128)S(1)} %get-tuple-element.17), channel_id=1, source_target_pairs={{0,4},{4,8},{8,12},{1,5},{5,9},{9,13},{2,6},{6,10},{10,14},{3,7},{... | collective-permute-start | bytes 632 | tf_op jit(solution)/shard_map/ppermute | solution.py:158
  36.8 1.9 %collective-permute-start.6 = (f32[26,2,1]{2,1,0:T(2,128)S(1)}, f32[26,2,1]{2,1,0:T(2,128)S(1)}, u32[]{:S(2)}, u32[]{:S(2)}) collective-permute-start(f32[26,2,1]{2,1,0:T(2,128)S(1)} %get-tuple-element.18), channel_id=1, source_target_pairs={{4,0},{8,4},{12,8},{5,1},{9,5},{13,9},{6,2},{10,6},{14,10},{7,3},{... | collective-permute-start | bytes 632 | tf_op jit(solution)/shard_map/ppermute | solution.py:159
  38.7 0.0 collective-permute-done.5
  38.7 3.2 %collective-permute-done.6 = f32[26,2,1]{2,1,0:T(2,128)S(1)} collective-permute-done((f32[26,2,1]{2,1,0:T(2,128)S(1)}, f32[26,2,1]{2,1,0:T(2,128)S(1)}, u32[]{:S(2)}, u32[]{:S(2)}) %collective-permute-start.6) | collective-permute-done | bytes 240 | tf_op jit(solution)/shard_map/ppermute | solution.py:159
  41.9 1.2 %fusion.33 = f32[26,2,1024]{2,1,0:T(2,128)} fusion(f32[26,2,1]{2,1,0:T(2,128)S(1)} %collective-permute-done.6, f32[26,2,1024]{2,1,0:T(2,128)S(1)} %broadcast_multiply_fusion, f32[26,2,1]{2,1,0:T(2,128)S(1)} %collective-permute-done.5, f32[1024]{0:T(1024)S(1)} %copy-done.2), kind=kLoop, calls=%fused_computation.67 | loop fusion | flops 372736 | bytes 430496 | tf_op jit(solution)/shard_map/mul | solution.py:162
  (15 shorter events, 0.1 us)
Async XLA Ops:
  0.0 6.2 %copy-start.1 = (bf16[8,150,26]{1,0,2:T(8,128)(2,1)S(1)}, bf16[8,150,26]{1,0,2:T(8,128)(2,1)}, u32[]{:S(2)}) copy-start(bf16[8,150,26]{1,0,2:T(8,128)(2,1)} %param.4) | copy-start | bytes 187204
  0.0 6.2 %collective-permute-start = (bf16[208,150]{1,0:T(8,128)(2,1)}, bf16[208,150]{1,0:T(8,128)(2,1)S(1)}, u32[]{:S(2)}, u32[]{:S(2)}) collective-permute-start(bf16[208,150]{1,0:T(8,128)(2,1)} %bitcast.7), channel_id=1, source_target_pairs={{0,16},{16,0},{1,17},{17,1},{2,18},{18,2},{3,19},{19,3},{4,20},{20... | collective-permute-start | bytes 187208 | tf_op jit(solution)/shard_map/ppermute | solution.py:117
  6.2 3.8 %copy-start = (bf16[2,16,150,1024]{3,1,2,0:T(8,128)(2,1)S(1)}, bf16[2,16,150,1024]{3,1,2,0:T(8,128)(2,1)}, u32[]{:S(2)}) copy-start(bf16[2,16,150,1024]{3,1,2,0:T(8,128)(2,1)} %param.5) | copy-start | bytes 29491204
  13.9 15.9 %copy-start.2 = (f32[1024]{0:T(1024)S(1)}, f32[1024]{0:T(1024)}, u32[]{:S(2)}) copy-start(f32[1024]{0:T(1024)} %param.7) | copy-start | bytes 12292
  13.9 10.7 %collective-permute-start.1 = (bf16[64,1024]{1,0:T(8,128)(2,1)S(1)}, bf16[64,1024]{1,0:T(8,128)(2,1)S(1)}, u32[]{:S(2)}, u32[]{:S(2)}) collective-permute-start(bf16[64,1024]{1,0:T(8,128)(2,1)S(1)} %get-tuple-element.12), channel_id=1, source_target_pairs={{0,2},{1,3},{2,0},{3,1},{4,6},{5,7},{6,4},{7,5},{8,10},{9,11},{10,... | collective-permute-start | bytes 393224 | tf_op jit(solution)/shard_map/ppermute | solution.py:117
  16.2 8.3 %collective-permute-start.2 = (bf16[64,1024]{1,0:T(8,128)(2,1)S(1)}, bf16[64,1024]{1,0:T(8,128)(2,1)S(1)}, u32[]{:S(2)}, u32[]{:S(2)}) collective-permute-start(bf16[64,1024]{1,0:T(8,128)(2,1)S(1)} %get-tuple-element.13), channel_id=1, source_target_pairs={{0,1},{1,2},{2,3},{3,0},{4,5},{5,6},{6,7},{7,4},{8,9},{9,10},{10,1... | collective-permute-start | bytes 393224 | tf_op jit(solution)/shard_map/ppermute | solution.py:117
  17.5 7.8 %collective-permute-start.3 = (bf16[64,1024]{1,0:T(8,128)(2,1)S(1)}, bf16[64,1024]{1,0:T(8,128)(2,1)S(1)}, u32[]{:S(2)}, u32[]{:S(2)}) collective-permute-start(bf16[64,1024]{1,0:T(8,128)(2,1)S(1)} %get-tuple-element.14), channel_id=1, source_target_pairs={{0,3},{1,0},{2,1},{3,2},{4,7},{5,4},{6,5},{7,6},{8,11},{9,8},{10,9... | collective-permute-start | bytes 393224 | tf_op jit(solution)/shard_map/ppermute | solution.py:117
  25.9 3.7 %collective-permute-start.4 = (bf16[56,1024]{1,0:T(8,128)(2,1)S(1)}, bf16[56,1024]{1,0:T(8,128)(2,1)S(1)}, u32[]{:S(2)}, u32[]{:S(2)}) collective-permute-start(bf16[56,1024]{1,0:T(8,128)(2,1)S(1)} %get-tuple-element.16), channel_id=1, source_target_pairs={{0,16},{16,0},{1,17},{17,1},{2,18},{18,2},{3,19},{19,3},{4,20},{20... | collective-permute-start | bytes 344072 | tf_op jit(solution)/shard_map/ppermute | solution.py:117
  30.0 8.7 %collective-permute-start.5 = (f32[26,2,1]{2,1,0:T(2,128)S(1)}, f32[26,2,1]{2,1,0:T(2,128)S(1)}, u32[]{:S(2)}, u32[]{:S(2)}) collective-permute-start(f32[26,2,1]{2,1,0:T(2,128)S(1)} %get-tuple-element.17), channel_id=1, source_target_pairs={{0,4},{4,8},{8,12},{1,5},{5,9},{9,13},{2,6},{6,10},{10,14},{3,7},{... | collective-permute-start | bytes 632 | tf_op jit(solution)/shard_map/ppermute | solution.py:158
  36.8 5.2 %collective-permute-start.6 = (f32[26,2,1]{2,1,0:T(2,128)S(1)}, f32[26,2,1]{2,1,0:T(2,128)S(1)}, u32[]{:S(2)}, u32[]{:S(2)}) collective-permute-start(f32[26,2,1]{2,1,0:T(2,128)S(1)} %get-tuple-element.18), channel_id=1, source_target_pairs={{4,0},{8,4},{12,8},{5,1},{9,5},{13,9},{6,2},{10,6},{14,10},{7,3},{... | collective-permute-start | bytes 632 | tf_op jit(solution)/shard_map/ppermute | solution.py:159

commit v2 on v1

v2 whole, which is shorter than its diff:
```python
import functools
import math

import jax
import jax.numpy as jnp
from jax import lax
from jax.experimental import pallas as pl
from jax.experimental.pallas import tpu as pltpu
from jax.sharding import PartitionSpec as P

LEN = 840
PREP = 10**10
BF = jnp.bfloat16
F32 = jnp.float32


def vmem():
    return pl.BlockSpec(memory_space=pltpu.VMEM)


def call(body, name, out_shape, *args, flops=0, limit=4 << 20):
    moved = sum(a.size * a.dtype.itemsize for a in [*args, *jax.tree.leaves(out_shape)])
    return pl.pallas_call(
        body,
        in_specs=[vmem()] * len(args),
        out_specs=jax.tree.map(lambda _: vmem(), out_shape),
        out_shape=out_shape,
        compiler_params=pltpu.CompilerParams(vmem_limit_bytes=limit),
        cost_estimate=pl.CostEstimate(flops=flops, transcendentals=0, bytes_accessed=moved),
        name=name,
    )(*args)


def split_index(flat, sizes):
    out = []
    for size in reversed(sizes):
        out.append(flat % size)
        flat = flat // size
    return out[::-1]


def iota(shape, dim):
    return lax.broadcasted_iota(jnp.int32, shape, dim)


def onehot(shape, hit):
    return jnp.where(hit, jnp.ones(shape, F32), jnp.zeros(shape, F32)).astype(BF)


def dot(a, b, precision=None):
    return jnp.dot(a, b, precision=precision, preferred_element_type=F32)


def wave(product, part):
    angle = ((product + part * (LEN // 4)) % LEN).astype(F32) * (2.0 * math.pi / LEN)
    return jnp.cos(angle)


def prepare_body(dims, weights, *refs):
    bins, times, probes, group, freqs, senss, rows = dims
    freq, sens = lax.axis_index("freq"), lax.axis_index("sens")
    tables, spread, inverse = refs[: 2 * freqs], refs[2 * freqs], refs[2 * freqs + 1]
    small = (2 * bins, times)
    part, bin_at = split_index(iota(small, 0), (2, bins))
    tall = (senss * 2 * bins * group, 2 * bins)
    up = onehot(tall, iota(tall, 0) // group % (2 * bins) == iota(tall, 1))
    flat = (times, times * probes)
    out = onehot(flat, iota(flat, 1) // probes == iota(flat, 0))
    full = (tall[0], flat[1])
    shift = iota(full, 0) // (2 * bins * group)
    probe = (sens + shift) % senss * group + iota(full, 0) % group
    hit = iota(full, 1) % probes == probe
    for j in range(freqs):
        time = iota(small, 1) + (freq + j) % freqs * times
        value = wave((freq * bins + bin_at) * time, part) * (1.0 / math.sqrt(times * freqs))
        high = value.astype(BF)
        low = (value - high.astype(F32)).astype(BF)
        for i, piece in enumerate((high, low)):
            wide = dot(dot(up, piece).astype(BF), out)
            tables[2 * j + i][...] = jnp.where(hit, wide, 0.0).astype(BF)
    spread[...] = onehot(spread.shape, iota(spread.shape, 1) // bins == iota(spread.shape, 0))
    shape = inverse.shape
    shift, row = split_index(iota(shape, 0), (freqs, rows))
    part, bin_at, inner = split_index(iota(shape, 1), (2, bins, group))
    time = row // group + (freq + shift) % freqs * times
    value = wave((freq * bins + bin_at) * time, part)
    pick = (bins, shape[1])
    chosen = jnp.where(iota(pick, 1) // group % bins == iota(pick, 0), 1.0, 0.0)
    weight = dot(weights[...], chosen, lax.Precision.HIGHEST) * (1.0 / math.sqrt(bins * freqs))
    hit = (row % group == inner) & (row < times * group)
    inverse[...] = jnp.where(hit, value * weight[:1], 0.0)


def contract_body(bins, blocks, pieces, *refs):
    tables = refs[: 2 * pieces]
    series = refs[2 * pieces : 3 * pieces]
    spread, operator = refs[3 * pieces : 3 * pieces + 2]
    lhs_re, lhs_im = refs[3 * pieces + 2 : 3 * pieces + 4]
    spec = None
    for i in range(2 * pieces):
        term = dot(tables[i][...], series[i // 2][...])
        spec = term if spec is None else spec + term
    rows = spec.shape[0]
    block = rows // blocks
    half = block // 2
    group = half // bins
    wide = dot(spec.astype(BF), spread[...])
    keep = iota(wide.shape, 0) // group % bins == iota(wide.shape, 1) % bins
    wide = jnp.where(keep, wide, 0.0).astype(BF)
    lhs_re[...] = wide
    for i in range(blocks):
        lhs_im[i * block : i * block + half, :] = wide[i * block + half : (i + 1) * block]
        lhs_im[i * block + half : (i + 1) * block, :] = -wide[i * block : i * block + half]
    outer_body(lhs_re, lhs_im, operator, *refs[3 * pieces + 4 :])


def product(lhs_re, lhs_im, operator, first, count):
    inner = operator.shape[0] // 2
    at = pl.ds(first, count)
    return dot(lhs_re[...], operator[:inner, at]) + dot(lhs_im[...], operator[inner:, at])


def outer_body(lhs_re, lhs_im, operator, *outs):
    cols = operator.shape[1]
    edge = cols // 4
    block = lhs_re.shape[0] // len(outs)
    for at, first in ((0, 0), (edge, cols - edge)):
        total = product(lhs_re, lhs_im, operator, first, edge)
        for i, out in enumerate(outs):
            out[:, at : at + edge] = total[i * block : (i + 1) * block].astype(out.dtype)


def inner_body(lhs_re, lhs_im, operator, *outs):
    cols = operator.shape[1]
    block = lhs_re.shape[0] // len(outs)
    total = product(lhs_re, lhs_im, operator, cols // 4, cols // 2)
    for i, out in enumerate(outs):
        out[...] = total[i * block : (i + 1) * block].astype(out.dtype)


def image_body(rows, *refs):
    table, own = refs[:2]
    count = table.shape[0] // rows
    outs = refs[len(refs) - count :]
    total = own[...]
    for other in refs[2 : len(refs) - count]:
        total = total + other[...].astype(F32)
    image = dot(table[...], total, lax.Precision.HIGHEST)
    for i, out in enumerate(outs):
        out[...] = image[i * rows : (i + 1) * rows].astype(out.dtype)


def edge_body(lanes, scale, *refs):
    first, last = refs[-2:]
    cols, width = scale.shape[1], refs[0].shape[1]
    for out, at, scale_at in ((first, 0, 0), (last, width - lanes, cols - lanes)):
        total = None
        for ref in refs[:-2]:
            term = ref[:, at : at + lanes].astype(F32)
            total = term if total is None else total + term
        out[...] = total * scale[:, scale_at : scale_at + lanes]


def smooth_body(count, scale, before, after, *refs):
    out = refs[-1]
    def total(parts):
        value = parts[0][...]
        for ref in parts[1:]:
            value = value + ref[...].astype(F32)
        return value
    outer, inner = total(refs[:count]), total(refs[count:-1])
    times, group, cols = out.shape
    edge = cols // 4
    value = jnp.concatenate([outer[:, :edge], inner, outer[:, edge:]], axis=1)
    value = value * scale[...]
    lane = iota(value.shape, 1)
    width = before.shape[1]
    left = jnp.where(lane == 0, before[:, width - 1 :], pltpu.roll(value, 1, 1))
    right = jnp.where(lane == cols - 1, after[:, :1], pltpu.roll(value, cols - 1, 1))
    value = (0.5 * value + 0.25 * (left + right)) * scale[...]
    out[...] = value[: times * group].reshape(times, group, cols)


def rotate(value, axis, shift):
    size = lax.axis_size(axis)
    return lax.ppermute(value, axis, [(i, (i + shift) % size) for i in range(size)])


def local(series, kernel, prior_spectrum, prior_scale):
    freqs, senss, params = (lax.axis_size(a) for a in ("freq", "sens", "param"))
    probes, sens_dev, times = series.shape
    bins, cols = kernel.shape[1], kernel.shape[3]
    group = probes // senss
    block = 2 * bins * group
    rows = -(-times * group // 8) * 8
    shape = jax.ShapeDtypeStruct
    own_series = series.transpose(2, 0, 1).reshape(times * probes, sens_dev)
    pieces = [own_series] + [rotate(own_series, "freq", -j) for j in range(1, freqs)]
    *tables, spread, inverse = call(
        functools.partial(prepare_body, (bins, times, probes, group, freqs, senss, rows)),
        "prepare",
        [shape((senss * block, times * probes), BF)] * (2 * freqs)
        + [shape((sens_dev, sens_dev * bins), BF), shape((freqs * rows, block), F32)],
        prior_spectrum.reshape(1, bins),
        flops=PREP,
    )
    operator = kernel.transpose(0, 2, 1, 3).reshape(2 * sens_dev * bins, cols)
    half = [shape((block, cols // 2), BF if i else F32) for i in range(senss)]
    lhs_re, lhs_im, *outer = call(
        functools.partial(contract_body, bins, senss, freqs),
        "contract_outer",
        [shape((senss * block, sens_dev * bins), BF)] * 2 + half,
        *tables, *pieces, spread, operator,
    )
    inner = call(inner_body, "contract_inner", half, lhs_re, lhs_im, operator)
    order = sorted(range(1, senss), key=lambda d: -min(d, senss - d))
    outer_parts = [outer[0]] + [rotate(outer[d], "sens", d) for d in order]
    inner_parts = [inner[0]] + [rotate(inner[d], "sens", d) for d in order]
    image = [shape((rows, cols // 2), BF if i else F32) for i in range(freqs)]
    as_image = functools.partial(image_body, rows)
    outer = call(as_image, "image_outer", image, inverse, *outer_parts)
    outer = [outer[0]] + [rotate(outer[j], "freq", j) for j in range(1, freqs)]
    inner = call(as_image, "image_inner", image, inverse, *inner_parts)
    inner = [inner[0]] + [rotate(inner[j], "freq", j) for j in range(1, freqs)]
    scale = prior_scale.reshape(1, cols)
    lanes = min(128, cols // 4)
    first, last = call(
        functools.partial(edge_body, lanes), "edge", [shape((rows, lanes), F32)] * 2, scale, *outer
    )
    before = lax.ppermute(last, "param", [(i, i + 1) for i in range(params - 1)])
    after = lax.ppermute(first, "param", [(i + 1, i) for i in range(params - 1)])
    return call(
        functools.partial(smooth_body, freqs),
        "smooth",
        shape((times, group, cols), F32),
        scale, before, after, *outer, *inner,
    )


def solution(mesh):
    placed = (P(None, "sens", "freq"), P(None, "freq", "sens", "param"), P("freq"), P("param"))
    return jax.shard_map(
        local, mesh=mesh, in_specs=placed, out_specs=P("freq", "sens", "param"), check_vma=False
    )
```

time: 44 us -> 35.3 us (0.80); the launches traced: 43.1 us -> 35.1 us
  other arithmetic: 5.71 us -> 0.01 us
  waiting for transfers between devices: 12.2 us -> 6.53 us
  starting transfers between devices: 16.4 us -> 20.1 us
  local copies, waits for them, and re-layouts: 4.19 us -> 1.97 us
  Pallas kernels: 4.36 us -> 6.41 us
    ppermute x5 -> x9, waiting for transfers between devices: 9.01 us -> 3.28 us  [rotate(): lax.ppermute(value, axis, [(i, (i + shift) % size) for i in range(size)])]
    ppermute x5 -> x9, starting transfers between devices: 7.74 us -> 11.9 us  [rotate(): lax.ppermute(value, axis, [(i, (i + shift) % size) for i in range(size)])]
    convert_element_type x2 -> x0, other arithmetic: 3.15 us -> none  [the longest x1 3.01 us: local(): tables += [high.astype(BF), (full - high).astype(BF)]]
    pallas_call x2 -> x7, Pallas kernels: 4.36 us -> 6.41 us  [call(): pl.pallas_call(body, in_specs=[vmem()] * len(args), out_specs=jax.tree.ma...]
    mul x3 -> x0, other arithmetic: 1.96 us -> none  [the longest x1 1.22 us: local(): return smooth * prior_scale]
    unnamed x6 -> x12, local copies, waits for them, and re-layouts: 3.8 us -> 1.97 us
    ppermute x2, starting transfers between devices: 8.69 us -> 8.16 us  [the longest x1 6.24 us: local(): lax.ppermute(last, 'param', [(i, i + 1) for i in range(params - 1)])]
    select_n x1 -> x0, other arithmetic: 0.48 us -> none  [inverse_table(): return jnp.where(hit, value * weight, 0.0)]
  transfers between devices with their start and end apart: 7 -> 11, of which waited for: 4 -> 5; matrix products, arithmetic and copies ran while one was open for 11% -> 0% of each run, Pallas kernels for 0% -> 9%
where the time goes in v2:
time: 35.3 us; the launch traced here: 35.1 us
  starting transfers between devices  20.1 us (57%)
  waiting for transfers between devices  6.53 us (18%)
  Pallas kernels  6.41 us (18%)
  local copies, waits for them, and re-layouts  1.97 us (6%)
    ppermute x9, starting transfers between devices, rotate(): lax.ppermute(value, axis, [(i, (i + shift) % size) for i in range(size)])  11.9 us
    pallas_call x7, Pallas kernels, call(): pl.pallas_call(body, in_specs=[vmem()] * len(args), out_specs=jax.tree.ma...  6.41 us
    ppermute x1, starting transfers between devices, local(): lax.ppermute(last, 'param', [(i, i + 1) for i in range(params - 1)])  6.24 us
    ppermute x9, waiting for transfers between devices, rotate(): lax.ppermute(value, axis, [(i, (i + shift) % size) for i in range(size)])  3.28 us
    ppermute x1, waiting for transfers between devices, local(): lax.ppermute(first, 'param', [(i + 1, i) for i in range(params - 1)])  3.24 us
    unnamed x12, local copies, waits for them, and re-layouts  1.97 us
    ppermute x1, starting transfers between devices, local(): lax.ppermute(first, 'param', [(i + 1, i) for i in range(params - 1)])  1.92 us
  transfers between devices with their start and end apart: 11, of which 5 were waited for; matrix products, arithmetic and copies ran while one was open for 0% of the time, Pallas kernels for 9%

profile of v2, /device:TPU:1, one launch (start us, length us, event | category | flops | bytes accessed | tf_op | source)
XLA Modules:
  0.0 35.1 jit_solution(16783821149501277086)
XLA Ops:
  0.0 2.0 %collective-permute-start = (bf16[208,150]{1,0:T(8,128)(2,1)}, bf16[208,150]{1,0:T(8,128)(2,1)S(1)}, u32[]{:S(2)}, u32[]{:S(2)}) collective-permute-start(bf16[208,150]{1,0:T(8,128)(2,1)} %bitcast.12), channel_id=1, source_target_pairs={{0,16},{16,0},{1,17},{17,1},{2,18},{18,2},{3,19},{19,3},{4,20},{20... | collective-permute-start | bytes 187208 | tf_op jit(solution)/shard_map/ppermute | solution.py:186
  2.0 0.0 slice-start
  2.0 0.0 copy-start.2
  2.0 0.8 %copy-done.2 = f32[16]{0:T(128)S(1)} copy-done((f32[16]{0:T(128)S(1)}, f32[16]{0:T(128)}, u32[]{:S(2)}) %copy-start.2) | copy-done | bytes 88
  2.8 0.0 slice-start.1
  2.8 0.0 slice-start.2
  2.8 0.0 copy-start
  2.8 0.9 %prepare.1 = (bf16[256,208]{1,0:T(8,128)(2,1)S(1)}, bf16[256,208]{1,0:T(8,128)(2,1)S(1)}, bf16[256,208]{1,0:T(8,128)(2,1)S(1)}, bf16[256,208]{1,0:T(8,128)(2,1)S...) custom-call(f32[1,16]{1,0:T(1,128)S(1)} %bitcast.16), custom_call_target="tpu_custom_call" | custom-call | flops 10000000000 | bytes 1174720 | tf_op jit(solution)/shard_map/prepare/pallas_call | solution.py:23
  3.8 1.1 %collective-permute-done.refs_5_ = bf16[208,150]{1,0:T(8,128)(2,1)S(1)} collective-permute-done((bf16[208,150]{1,0:T(8,128)(2,1)}, bf16[208,150]{1,0:T(8,128)(2,1)S(1)}, u32[]{:S(2)}, u32[]{:S(2)}) %collective-permute-start) | collective-permute-done | bytes 62432 | tf_op jit(solution)/shard_map/ppermute | solution.py:186
  4.9 0.0 slice-done
  4.9 0.8 %slice-done.1 = s8[4194304]{0:T(1024)(128)(4,1)S(1)} async-done(((s8[9830400]{0:T(1024)(128)(4,1)}), s8[4194304]{0:T(1024)(128)(4,1)S(1)}, s32[]{:S(2)}) %slice-start.1) | async-done | bytes 4194328
  5.7 0.4 %slice-done.2 = s8[1441792]{0:T(1024)(128)(4,1)S(1)} async-done(((s8[9830400]{0:T(1024)(128)(4,1)}), s8[1441792]{0:T(1024)(128)(4,1)S(1)}, s32[]{:S(2)}) %slice-start.2) | async-done | bytes 1441816
  6.1 0.0 copy-done
  6.1 2.3 %contract_outer.1 = (bf16[256,2400]{1,0:T(8,128)(2,1)S(1)}, bf16[256,2400]{1,0:T(8,128)(2,1)S(1)}, f32[64,512]{1,0:T(8,128)S(1)}, bf16[64,512]{1,0:T(8,128)(2,1)...) custom-call(bf16[256,208]{1,0:T(8,128)(2,1)S(1)} %get-tuple-element.28.refs_0_, ...), custom_call_target="tpu_custom_call" | custom-call | bytes 13886464 | tf_op jit(solution)/shard_map/contract_outer/pallas_call | solution.py:23
  8.4 2.4 %collective-permute-start.1 = (bf16[64,512]{1,0:T(8,128)(2,1)S(1)}, bf16[64,512]{1,0:T(8,128)(2,1)S(1)}, u32[]{:S(2)}, u32[]{:S(2)}) collective-permute-start(bf16[64,512]{1,0:T(8,128)(2,1)S(1)} %get-tuple-element.34), channel_id=1, source_target_pairs={{0,2},{1,3},{2,0},{3,1},{4,6},{5,7},{6,4},{7,5},{8,10},{9,11},{10,... | collective-permute-start | bytes 196616 | tf_op jit(solution)/shard_map/ppermute | solution.py:186
  10.8 1.3 %collective-permute-start.2 = (bf16[64,512]{1,0:T(8,128)(2,1)S(1)}, bf16[64,512]{1,0:T(8,128)(2,1)S(1)}, u32[]{:S(2)}, u32[]{:S(2)}) collective-permute-start(bf16[64,512]{1,0:T(8,128)(2,1)S(1)} %get-tuple-element.35), channel_id=1, source_target_pairs={{0,1},{1,2},{2,3},{3,0},{4,5},{5,6},{6,7},{7,4},{8,9},{9,10},{10,1... | collective-permute-start | bytes 196616 | tf_op jit(solution)/shard_map/ppermute | solution.py:186
  12.1 2.0 %collective-permute-start.3 = (bf16[64,512]{1,0:T(8,128)(2,1)S(1)}, bf16[64,512]{1,0:T(8,128)(2,1)S(1)}, u32[]{:S(2)}, u32[]{:S(2)}) collective-permute-start(bf16[64,512]{1,0:T(8,128)(2,1)S(1)} %get-tuple-element.36), channel_id=1, source_target_pairs={{0,3},{1,0},{2,1},{3,2},{4,7},{5,4},{6,5},{7,6},{8,11},{9,8},{10,9... | collective-permute-start | bytes 196616 | tf_op jit(solution)/shard_map/ppermute | solution.py:186
  14.1 0.0 copy-start.1
  14.1 1.5 %contract_inner.1 = (f32[64,512]{1,0:T(8,128)S(1)}, bf16[64,512]{1,0:T(8,128)(2,1)S(1)}, bf16[64,512]{1,0:T(8,128)(2,1)S(1)}, bf16[64,512]{1,0:T(8,128)(2,1)S(1)}) custom-call(bf16[256,2400]{1,0:T(8,128)(2,1)S(1)} %get-tuple-element.41.lhs_re, bf16[256,2400]{1,0:T(8,128)(2,1)S(1)} %get-tuple-element.42.lhs_im, bf16[4800,1024]{1,0:T(8,128)(2,1)S(1)} %bitcast.11), custom_call_target="tpu_custom_call" | custom-call | bytes 12615680 | tf_op jit(solution)/shard_map/contract_inner/pallas_call | solution.py:23
  15.6 0.1 collective-permute-start.7
  15.6 0.3 collective-permute-start.8
  15.9 0.0 collective-permute-done.1.refs_2_
  15.9 3.0 %collective-permute-start.9 = (bf16[64,512]{1,0:T(8,128)(2,1)S(1)}, bf16[64,512]{1,0:T(8,128)(2,1)S(1)}, u32[]{:S(2)}, u32[]{:S(2)}) collective-permute-start(bf16[64,512]{1,0:T(8,128)(2,1)S(1)} %get-tuple-element.46), channel_id=1, source_target_pairs={{0,3},{1,0},{2,1},{3,2},{4,7},{5,4},{6,5},{7,6},{8,11},{9,8},{10,9... | collective-permute-start | bytes 196616 | tf_op jit(solution)/shard_map/ppermute | solution.py:186
  19.0 0.0 collective-permute-done.2.refs_3_
  19.0 0.0 collective-permute-done.3.refs_4_
  19.0 0.4 %image_outer.1 = (f32[56,512]{1,0:T(8,128)S(1)}, bf16[56,512]{1,0:T(8,128)(2,1)S(1)}) custom-call(f32[112,64]{1,0:T(8,128)S(1)} %get-tuple-element.27.refs_0_, f32[64,512]{1,0:T(8,128)S(1)} %get-tuple-element.33.refs_1_, bf16[64,512]{1,0:T(8,128)(2,1)S(1)} %collective-permute-done.1.refs_2_, bf16[64,512]{1,0:T(8,128)(2,1)S(1)} %collective-permute-done.2.refs_3_, ...), custom_call_target="tpu_custom_call" | custom-call | bytes 528384 | tf_op jit(solution)/shard_map/image_outer/pallas_call | solution.py:23
  19.3 0.3 collective-permute-start.4
  19.7 0.0 collective-permute-done.7.refs_2_
  19.7 1.2 %collective-permute-done.8.refs_3_ = bf16[64,512]{1,0:T(8,128)(2,1)S(1)} collective-permute-done((bf16[64,512]{1,0:T(8,128)(2,1)S(1)}, bf16[64,512]{1,0:T(8,128)(2,1)S(1)}, u32[]{:S(2)}, u32[]{:S(2)}) %collective-permute-start.8) | collective-permute-done | bytes 65568 | tf_op jit(solution)/shard_map/ppermute | solution.py:186
  20.9 0.2 collective-permute-done.9.refs_4_
  21.1 0.4 %image_inner.1 = (f32[56,512]{1,0:T(8,128)S(1)}, bf16[56,512]{1,0:T(8,128)(2,1)S(1)}) custom-call(f32[112,64]{1,0:T(8,128)S(1)} %get-tuple-element.27.refs_0_, f32[64,512]{1,0:T(8,128)S(1)} %get-tuple-element.43.refs_1_, bf16[64,512]{1,0:T(8,128)(2,1)S(1)} %collective-permute-done.7.refs_2_, bf16[64,512]{1,0:T(8,128)(2,1)S(1)} %collective-permute-done.8.refs_3_, ...), custom_call_target="tpu_custom_call" | custom-call | bytes 528384 | tf_op jit(solution)/shard_map/image_inner/pallas_call | solution.py:23
  21.4 0.5 %collective-permute-start.10 = (bf16[56,512]{1,0:T(8,128)(2,1)S(1)}, bf16[56,512]{1,0:T(8,128)(2,1)S(1)}, u32[]{:S(2)}, u32[]{:S(2)}) collective-permute-start(bf16[56,512]{1,0:T(8,128)(2,1)S(1)} %get-tuple-element.48), channel_id=1, source_target_pairs={{0,16},{16,0},{1,17},{17,1},{2,18},{18,2},{3,19},{19,3},{4,20},{20... | collective-permute-start | bytes 172040 | tf_op jit(solution)/shard_map/ppermute | solution.py:186
  22.0 0.8 %collective-permute-done.4.refs_1_ = bf16[56,512]{1,0:T(8,128)(2,1)S(1)} collective-permute-done((bf16[56,512]{1,0:T(8,128)(2,1)S(1)}, bf16[56,512]{1,0:T(8,128)(2,1)S(1)}, u32[]{:S(2)}, u32[]{:S(2)}) %collective-permute-start.4) | collective-permute-done | bytes 57376 | tf_op jit(solution)/shard_map/ppermute | solution.py:186
  22.7 0.0 copy-done.1
  22.7 6.2 %collective-permute-start.5 = (f32[56,128]{1,0:T(8,128)S(1)}, f32[56,128]{1,0:T(8,128)S(1)}, u32[]{:S(2)}, u32[]{:S(2)}) collective-permute-start(f32[56,128]{1,0:T(8,128)S(1)} %get-tuple-element.39), channel_id=1, source_target_pairs={{0,4},{4,8},{8,12},{1,5},{5,9},{9,13},{2,6},{6,10},{10,14},{3,7},{... | collective-permute-start | bytes 86024 | tf_op jit(solution)/shard_map/ppermute | solution.py:230
  29.0 1.9 %collective-permute-start.6 = (f32[56,128]{1,0:T(8,128)S(1)}, f32[56,128]{1,0:T(8,128)S(1)}, u32[]{:S(2)}, u32[]{:S(2)}) collective-permute-start(f32[56,128]{1,0:T(8,128)S(1)} %get-tuple-element.40), channel_id=1, source_target_pairs={{4,0},{8,4},{12,8},{5,1},{9,5},{13,9},{6,2},{10,6},{14,10},{7,3},{... | collective-permute-start | bytes 86024 | tf_op jit(solution)/shard_map/ppermute | solution.py:231
  30.9 0.0 collective-permute-done.10.refs_3_
  30.9 0.0 collective-permute-done.5.before
  30.9 3.2 %collective-permute-done.6.after = f32[56,128]{1,0:T(8,128)S(1)} collective-permute-done((f32[56,128]{1,0:T(8,128)S(1)}, f32[56,128]{1,0:T(8,128)S(1)}, u32[]{:S(2)}, u32[]{:S(2)}) %collective-permute-start.6) | collective-permute-done | bytes 28704 | tf_op jit(solution)/shard_map/ppermute | solution.py:231
  34.2 0.9 %smooth.1 = f32[26,2,1024]{2,1,0:T(2,128)} custom-call(f32[1,1024]{1,0:T(1,128)S(1)} %bitcast.15, f32[56,128]{1,0:T(8,128)S(1)} %collective-permute-done.5.before, f32[56,128]{1,0:T(8,128)S(1)} %collective-permute-done.6.after, f32[56,512]{1,0:T(8,128)S(1)} %get-tuple-element.37.refs_0_, bf16[56,512]{1,0:T(8,128)(2,1)S(1)} %collective-permute-done.4.refs_1_, ...), custom_call_target="tpu_custom_call" | custom-call | bytes 618496 | tf_op jit(solution)/shard_map/smooth/pallas_call | solution.py:23
  (2 shorter events, 0.0 us)
Async XLA Ops:
  0.0 4.9 %collective-permute-start = (bf16[208,150]{1,0:T(8,128)(2,1)}, bf16[208,150]{1,0:T(8,128)(2,1)S(1)}, u32[]{:S(2)}, u32[]{:S(2)}) collective-permute-start(bf16[208,150]{1,0:T(8,128)(2,1)} %bitcast.12), channel_id=1, source_target_pairs={{0,16},{16,0},{1,17},{17,1},{2,18},{18,2},{3,19},{19,3},{4,20},{20... | collective-permute-start | bytes 187208 | tf_op jit(solution)/shard_map/ppermute | solution.py:186
  2.0 2.9 %slice-start = ((s8[9830400]{0:T(1024)(128)(4,1)}), s8[4194304]{0:T(1024)(128)(4,1)S(1)}, s32[]{:S(2)}) async-start(s8[9830400]{0:T(1024)(128)(4,1)} %bitcast.8), calls=%async_computation | async-start | bytes 8388608
  2.0 0.8 %copy-start.2 = (f32[16]{0:T(128)S(1)}, f32[16]{0:T(128)}, u32[]{:S(2)}) copy-start(f32[16]{0:T(128)} %param.6) | copy-start | bytes 196
  2.8 2.9 %slice-start.1 = ((s8[9830400]{0:T(1024)(128)(4,1)}), s8[4194304]{0:T(1024)(128)(4,1)S(1)}, s32[]{:S(2)}) async-start(s8[9830400]{0:T(1024)(128)(4,1)} %bitcast.8), calls=%async_computation.1 | async-start | bytes 8388608
  2.8 3.2 %slice-start.2 = ((s8[9830400]{0:T(1024)(128)(4,1)}), s8[1441792]{0:T(1024)(128)(4,1)S(1)}, s32[]{:S(2)}) async-start(s8[9830400]{0:T(1024)(128)(4,1)} %bitcast.8), calls=%async_computation.2 | async-start | bytes 2883584
  2.8 3.2 %copy-start = (bf16[8,150,26]{1,0,2:T(8,128)(2,1)S(1)}, bf16[8,150,26]{1,0,2:T(8,128)(2,1)}, u32[]{:S(2)}) copy-start(bf16[8,150,26]{1,0,2:T(8,128)(2,1)} %param.4) | copy-start | bytes 187204
  8.4 7.5 %collective-permute-start.1 = (bf16[64,512]{1,0:T(8,128)(2,1)S(1)}, bf16[64,512]{1,0:T(8,128)(2,1)S(1)}, u32[]{:S(2)}, u32[]{:S(2)}) collective-permute-start(bf16[64,512]{1,0:T(8,128)(2,1)S(1)} %get-tuple-element.34), channel_id=1, source_target_pairs={{0,2},{1,3},{2,0},{3,1},{4,6},{5,7},{6,4},{7,5},{8,10},{9,11},{10,... | collective-permute-start | bytes 196616 | tf_op jit(solution)/shard_map/ppermute | solution.py:186
  10.8 8.2 %collective-permute-start.2 = (bf16[64,512]{1,0:T(8,128)(2,1)S(1)}, bf16[64,512]{1,0:T(8,128)(2,1)S(1)}, u32[]{:S(2)}, u32[]{:S(2)}) collective-permute-start(bf16[64,512]{1,0:T(8,128)(2,1)S(1)} %get-tuple-element.35), channel_id=1, source_target_pairs={{0,1},{1,2},{2,3},{3,0},{4,5},{5,6},{6,7},{7,4},{8,9},{9,10},{10,1... | collective-permute-start | bytes 196616 | tf_op jit(solution)/shard_map/ppermute | solution.py:186
  12.1 6.9 %collective-permute-start.3 = (bf16[64,512]{1,0:T(8,128)(2,1)S(1)}, bf16[64,512]{1,0:T(8,128)(2,1)S(1)}, u32[]{:S(2)}, u32[]{:S(2)}) collective-permute-start(bf16[64,512]{1,0:T(8,128)(2,1)S(1)} %get-tuple-element.36), channel_id=1, source_target_pairs={{0,3},{1,0},{2,1},{3,2},{4,7},{5,4},{6,5},{7,6},{8,11},{9,8},{10,9... | collective-permute-start | bytes 196616 | tf_op jit(solution)/shard_map/ppermute | solution.py:186
  14.1 8.7 %copy-start.1 = (f32[1024]{0:T(1024)S(1)}, f32[1024]{0:T(1024)}, u32[]{:S(2)}) copy-start(f32[1024]{0:T(1024)} %param.7) | copy-start | bytes 12292
  15.6 4.1 %collective-permute-start.7 = (bf16[64,512]{1,0:T(8,128)(2,1)S(1)}, bf16[64,512]{1,0:T(8,128)(2,1)S(1)}, u32[]{:S(2)}, u32[]{:S(2)}) collective-permute-start(bf16[64,512]{1,0:T(8,128)(2,1)S(1)} %get-tuple-element.44), channel_id=1, source_target_pairs={{0,2},{1,3},{2,0},{3,1},{4,6},{5,7},{6,4},{7,5},{8,10},{9,11},{10,... | collective-permute-start | bytes 196616 | tf_op jit(solution)/shard_map/ppermute | solution.py:186
  15.6 5.2 %collective-permute-start.8 = (bf16[64,512]{1,0:T(8,128)(2,1)S(1)}, bf16[64,512]{1,0:T(8,128)(2,1)S(1)}, u32[]{:S(2)}, u32[]{:S(2)}) collective-permute-start(bf16[64,512]{1,0:T(8,128)(2,1)S(1)} %get-tuple-element.45), channel_id=1, source_target_pairs={{0,1},{1,2},{2,3},{3,0},{4,5},{5,6},{6,7},{7,4},{8,9},{9,10},{10,1... | collective-permute-start | bytes 196616 | tf_op jit(solution)/shard_map/ppermute | solution.py:186
  15.9 5.1 %collective-permute-start.9 = (bf16[64,512]{1,0:T(8,128)(2,1)S(1)}, bf16[64,512]{1,0:T(8,128)(2,1)S(1)}, u32[]{:S(2)}, u32[]{:S(2)}) collective-permute-start(bf16[64,512]{1,0:T(8,128)(2,1)S(1)} %get-tuple-element.46), channel_id=1, source_target_pairs={{0,3},{1,0},{2,1},{3,2},{4,7},{5,4},{6,5},{7,6},{8,11},{9,8},{10,9... | collective-permute-start | bytes 196616 | tf_op jit(solution)/shard_map/ppermute | solution.py:186
  19.3 3.4 %collective-permute-start.4 = (bf16[56,512]{1,0:T(8,128)(2,1)S(1)}, bf16[56,512]{1,0:T(8,128)(2,1)S(1)}, u32[]{:S(2)}, u32[]{:S(2)}) collective-permute-start(bf16[56,512]{1,0:T(8,128)(2,1)S(1)} %get-tuple-element.38), channel_id=1, source_target_pairs={{0,16},{16,0},{1,17},{17,1},{2,18},{18,2},{3,19},{19,3},{4,20},{20... | collective-permute-start | bytes 172040 | tf_op jit(solution)/shard_map/ppermute | solution.py:186
  21.4 9.5 %collective-permute-start.10 = (bf16[56,512]{1,0:T(8,128)(2,1)S(1)}, bf16[56,512]{1,0:T(8,128)(2,1)S(1)}, u32[]{:S(2)}, u32[]{:S(2)}) collective-permute-start(bf16[56,512]{1,0:T(8,128)(2,1)S(1)} %get-tuple-element.48), channel_id=1, source_target_pairs={{0,16},{16,0},{1,17},{17,1},{2,18},{18,2},{3,19},{19,3},{4,20},{20... | collective-permute-start | bytes 172040 | tf_op jit(solution)/shard_map/ppermute | solution.py:186
  22.7 8.2 %collective-permute-start.5 = (f32[56,128]{1,0:T(8,128)S(1)}, f32[56,128]{1,0:T(8,128)S(1)}, u32[]{:S(2)}, u32[]{:S(2)}) collective-permute-start(f32[56,128]{1,0:T(8,128)S(1)} %get-tuple-element.39), channel_id=1, source_target_pairs={{0,4},{4,8},{8,12},{1,5},{5,9},{9,13},{2,6},{6,10},{10,14},{3,7},{... | collective-permute-start | bytes 86024 | tf_op jit(solution)/shard_map/ppermute | solution.py:230
  29.0 5.2 %collective-permute-start.6 = (f32[56,128]{1,0:T(8,128)S(1)}, f32[56,128]{1,0:T(8,128)S(1)}, u32[]{:S(2)}, u32[]{:S(2)}) collective-permute-start(f32[56,128]{1,0:T(8,128)S(1)} %get-tuple-element.40), channel_id=1, source_target_pairs={{4,0},{8,4},{12,8},{5,1},{9,5},{13,9},{6,2},{10,6},{14,10},{7,3},{... | collective-permute-start | bytes 86024 | tf_op jit(solution)/shard_map/ppermute | solution.py:231

commit v3 on v2

--- a/solution.py
+++ b/solution.py
@@ -9,6 +9,7 @@
 from jax.sharding import PartitionSpec as P
 
 LEN = 840
+OUTER = 4
 PREP = 10**10
 BF = jnp.bfloat16
 F32 = jnp.float32
@@ -56,10 +57,10 @@
     return jnp.cos(angle)
 
 
-def prepare_body(dims, weights, *refs):
-    bins, times, probes, group, freqs, senss, rows = dims
+def prepare_body(dims, *refs):
+    bins, times, probes, group, freqs, senss = dims
     freq, sens = lax.axis_index("freq"), lax.axis_index("sens")
-    tables, spread, inverse = refs[: 2 * freqs], refs[2 * freqs], refs[2 * freqs + 1]
+    tables, spread = refs[: 2 * freqs], refs[2 * freqs]
     small = (2 * bins, times)
     part, bin_at = split_index(iota(small, 0), (2, bins))
     tall = (senss * 2 * bins * group, 2 * bins)
@@ -79,6 +80,11 @@
             wide = dot(dot(up, piece).astype(BF), out)
             tables[2 * j + i][...] = jnp.where(hit, wide, 0.0).astype(BF)
     spread[...] = onehot(spread.shape, iota(spread.shape, 1) // bins == iota(spread.shape, 0))
+
+
+def inverse_body(dims, weights, after, inverse):
+    bins, times, group, freqs, rows = dims
+    freq = lax.axis_index("freq")
     shape = inverse.shape
     shift, row = split_index(iota(shape, 0), (freqs, rows))
     part, bin_at, inner = split_index(iota(shape, 1), (2, bins, group))
@@ -121,8 +127,7 @@
 
 
 def outer_body(lhs_re, lhs_im, operator, *outs):
-    cols = operator.shape[1]
-    edge = cols // 4
+    cols, edge = operator.shape[1], outs[0].shape[1] // 2
     block = lhs_re.shape[0] // len(outs)
     for at, first in ((0, 0), (edge, cols - edge)):
         total = product(lhs_re, lhs_im, operator, first, edge)
@@ -131,9 +136,9 @@
 
 
 def inner_body(lhs_re, lhs_im, operator, *outs):
-    cols = operator.shape[1]
+    width = outs[0].shape[1]
     block = lhs_re.shape[0] // len(outs)
-    total = product(lhs_re, lhs_im, operator, cols // 4, cols // 2)
+    total = product(lhs_re, lhs_im, operator, (operator.shape[1] - width) // 2, width)
     for i, out in enumerate(outs):
         out[...] = total[i * block : (i + 1) * block].astype(out.dtype)
 
@@ -151,32 +156,43 @@
 
 
 def edge_body(lanes, scale, *refs):
-    first, last = refs[-2:]
+    within, across = refs[-2:]
     cols, width = scale.shape[1], refs[0].shape[1]
-    for out, at, scale_at in ((first, 0, 0), (last, width - lanes, cols - lanes)):
+
+    def scaled(at, scale_at):
         total = None
         for ref in refs[:-2]:
             term = ref[:, at : at + lanes].astype(F32)
             total = term if total is None else total + term
-        out[...] = total * scale[:, scale_at : scale_at + lanes]
-
-
-def smooth_body(count, scale, before, after, *refs):
+        return total * scale[:, scale_at : scale_at + lanes]
+
+    first, last = scaled(0, 0), scaled(width - lanes, cols - lanes)
+    even = lax.axis_index("param") % 2 == 0
+    within[...] = jnp.where(even, last, first)
+    across[...] = jnp.where(even, first, last)
+
+
+def smooth_body(count, scale, within, across, *refs):
     out = refs[-1]
+
     def total(parts):
         value = parts[0][...]
         for ref in parts[1:]:
             value = value + ref[...].astype(F32)
         return value
+
     outer, inner = total(refs[:count]), total(refs[count:-1])
     times, group, cols = out.shape
-    edge = cols // 4
+    edge = outer.shape[1] // 2
     value = jnp.concatenate([outer[:, :edge], inner, outer[:, edge:]], axis=1)
     value = value * scale[...]
     lane = iota(value.shape, 1)
-    width = before.shape[1]
-    left = jnp.where(lane == 0, before[:, width - 1 :], pltpu.roll(value, 1, 1))
-    right = jnp.where(lane == cols - 1, after[:, :1], pltpu.roll(value, cols - 1, 1))
+    width = within.shape[1]
+    even = lax.axis_index("param") % 2 == 0
+    before = jnp.where(even, across[:, width - 1 :], within[:, width - 1 :])
+    after = jnp.where(even, within[:, :1], across[:, :1])
+    left = jnp.where(lane == 0, before, pltpu.roll(value, 1, 1))
+    right = jnp.where(lane == cols - 1, after, pltpu.roll(value, cols - 1, 1))
     value = (0.5 * value + 0.25 * (left + right)) * scale[...]
     out[...] = value[: times * group].reshape(times, group, cols)
 
@@ -196,44 +212,54 @@
     shape = jax.ShapeDtypeStruct
     own_series = series.transpose(2, 0, 1).reshape(times * probes, sens_dev)
     pieces = [own_series] + [rotate(own_series, "freq", -j) for j in range(1, freqs)]
-    *tables, spread, inverse = call(
-        functools.partial(prepare_body, (bins, times, probes, group, freqs, senss, rows)),
+    *tables, spread = call(
+        functools.partial(prepare_body, (bins, times, probes, group, freqs, senss)),
         "prepare",
         [shape((senss * block, times * probes), BF)] * (2 * freqs)
-        + [shape((sens_dev, sens_dev * bins), BF), shape((freqs * rows, block), F32)],
-        prior_spectrum.reshape(1, bins),
+        + [shape((sens_dev, sens_dev * bins), BF)],
         flops=PREP,
     )
     operator = kernel.transpose(0, 2, 1, 3).reshape(2 * sens_dev * bins, cols)
-    half = [shape((block, cols // 2), BF if i else F32) for i in range(senss)]
+    edge = cols // OUTER
+    blocks = lambda width: [shape((block, width), BF if i else F32) for i in range(senss)]
     lhs_re, lhs_im, *outer = call(
         functools.partial(contract_body, bins, senss, freqs),
         "contract_outer",
-        [shape((senss * block, sens_dev * bins), BF)] * 2 + half,
+        [shape((senss * block, sens_dev * bins), BF)] * 2 + blocks(2 * edge),
         *tables, *pieces, spread, operator,
     )
-    inner = call(inner_body, "contract_inner", half, lhs_re, lhs_im, operator)
+    inner = call(
+        inner_body, "contract_inner", blocks(cols - 2 * edge), lhs_re, lhs_im, operator
+    )
+    inverse = call(
+        functools.partial(inverse_body, (bins, times, group, freqs, rows)),
+        "inverse",
+        shape((freqs * rows, block), F32),
+        prior_spectrum.reshape(1, bins), outer[0],
+    )
     order = sorted(range(1, senss), key=lambda d: -min(d, senss - d))
-    outer_parts = [outer[0]] + [rotate(outer[d], "sens", d) for d in order]
-    inner_parts = [inner[0]] + [rotate(inner[d], "sens", d) for d in order]
-    image = [shape((rows, cols // 2), BF if i else F32) for i in range(freqs)]
+    outer = [outer[0]] + [rotate(outer[d], "sens", d) for d in order]
+    inner = [inner[0]] + [rotate(inner[d], "sens", d) for d in order]
+    images = lambda width: [shape((rows, width), BF if i else F32) for i in range(freqs)]
     as_image = functools.partial(image_body, rows)
-    outer = call(as_image, "image_outer", image, inverse, *outer_parts)
+    outer = call(as_image, "image_outer", images(2 * edge), inverse, *outer)
     outer = [outer[0]] + [rotate(outer[j], "freq", j) for j in range(1, freqs)]
-    inner = call(as_image, "image_inner", image, inverse, *inner_parts)
+    inner = call(as_image, "image_inner", images(cols - 2 * edge), inverse, *inner)
     inner = [inner[0]] + [rotate(inner[j], "freq", j) for j in range(1, freqs)]
     scale = prior_scale.reshape(1, cols)
-    lanes = min(128, cols // 4)
-    first, last = call(
+    lanes = min(128, edge)
+    swaps = call(
         functools.partial(edge_body, lanes), "edge", [shape((rows, lanes), F32)] * 2, scale, *outer
     )
-    before = lax.ppermute(last, "param", [(i, i + 1) for i in range(params - 1)])
-    after = lax.ppermute(first, "param", [(i + 1, i) for i in range(params - 1)])
+    swaps = [
+        lax.ppermute(swaps[i], "param", [(a + d, a + 1 - d) for a in range(i, params - 1, 2) for d in (0, 1)])
+        for i in (0, 1)
+    ]
     return call(
         functools.partial(smooth_body, freqs),
         "smooth",
         shape((times, group, cols), F32),
-        scale, before, after, *outer, *inner,
+        scale, *swaps, *outer, *inner,
     )
 
 

time: 35.3 us -> 32.2 us (0.912)
  local copies, waits for them, and re-layouts: 1.97 us -> 0.02 us
  waiting for transfers between devices: 6.53 us -> 4.74 us
  starting transfers between devices: 20.1 us -> 20.6 us
    unnamed x12, local copies, waits for them, and re-layouts: 1.97 us -> 0.02 us
    ppermute x9, starting transfers between devices: 11.9 us -> 13.7 us  [rotate(): lax.ppermute(value, axis, [(i, (i + shift) % size) for i in range(size)])]
    ppermute x2, starting transfers between devices: 8.16 us -> 6.9 us  [local(): lax.ppermute(swaps[i], 'param', [(a + d, a + 1 - d) for a in range(i, par...]
    ppermute x2, waiting for transfers between devices: 3.24 us -> 2.11 us  [local(): lax.ppermute(swaps[i], 'param', [(a + d, a + 1 - d) for a in range(i, par...]
    ppermute x9, waiting for transfers between devices: 3.28 us -> 2.63 us  [rotate(): lax.ppermute(value, axis, [(i, (i + shift) % size) for i in range(size)])]
    pallas_call x7 -> x8, Pallas kernels: 6.41 us -> 6.54 us  [call(): pl.pallas_call(body, in_specs=[vmem()] * len(args), out_specs=jax.tree.ma...]
  transfers between devices with their start and end apart: 11 -> 11, of which waited for: 5 -> 4; matrix products, arithmetic and copies ran while one was open for 0% -> 0% of each run, Pallas kernels for 9% -> 10%
where the time goes in v3:
time: 32.2 us; the launch traced here: 32 us
  starting transfers between devices  20.6 us (64%)
  Pallas kernels  6.54 us (20%)
  waiting for transfers between devices  4.74 us (15%)
    ppermute x9, starting transfers between devices, rotate(): lax.ppermute(value, axis, [(i, (i + shift) % size) for i in range(size)])  13.7 us
    ppermute x2, starting transfers between devices, local(): lax.ppermute(swaps[i], 'param', [(a + d, a + 1 - d) for a in range(i, par...  6.9 us
    pallas_call x8, Pallas kernels, call(): pl.pallas_call(body, in_specs=[vmem()] * len(args), out_specs=jax.tree.ma...  6.54 us
    ppermute x9, waiting for transfers between devices, rotate(): lax.ppermute(value, axis, [(i, (i + shift) % size) for i in range(size)])  2.63 us
    ppermute x2, waiting for transfers between devices, local(): lax.ppermute(swaps[i], 'param', [(a + d, a + 1 - d) for a in range(i, par...  2.11 us
  transfers between devices with their start and end apart: 11, of which 4 were waited for; matrix products, arithmetic and copies ran while one was open for 0% of the time, Pallas kernels for 10%

profile of v3, /device:TPU:1, one launch (start us, length us, event | category | flops | bytes accessed | tf_op | source)
XLA Modules:
  0.0 32.0 jit_solution(12896899749877231711)
XLA Ops:
  0.0 0.0 slice-start
  0.0 0.0 slice-start.1
  0.0 0.0 slice-start.2
  0.0 0.0 copy-start
  0.0 2.1 %collective-permute-start = (bf16[208,150]{1,0:T(8,128)(2,1)}, bf16[208,150]{1,0:T(8,128)(2,1)S(1)}, u32[]{:S(2)}, u32[]{:S(2)}) collective-permute-start(bf16[208,150]{1,0:T(8,128)(2,1)} %bitcast.12), channel_id=1, source_target_pairs={{0,16},{16,0},{1,17},{17,1},{2,18},{18,2},{3,19},{19,3},{4,20},{20... | collective-permute-start | bytes 187208 | tf_op jit(solution)/shard_map/ppermute | solution.py:202
  2.1 0.7 %prepare.1 = (bf16[256,208]{1,0:T(8,128)(2,1)S(1)}, bf16[256,208]{1,0:T(8,128)(2,1)S(1)}, bf16[256,208]{1,0:T(8,128)(2,1)S(1)}, bf16[256,208]{1,0:T(8,128)(2,1)S(1)}, bf16[150,2400]{1,0:T(8,128)(2,1)S(1)}) custom-call(), custom_call_target="tpu_custom_call" | custom-call | flops 10000000000 | bytes 1145984 | tf_op jit(solution)/shard_map/prepare/pallas_call | solution.py:24
  2.8 2.2 %collective-permute-done.refs_5_ = bf16[208,150]{1,0:T(8,128)(2,1)S(1)} collective-permute-done((bf16[208,150]{1,0:T(8,128)(2,1)}, bf16[208,150]{1,0:T(8,128)(2,1)S(1)}, u32[]{:S(2)}, u32[]{:S(2)}) %collective-permute-start) | collective-permute-done | bytes 62432 | tf_op jit(solution)/shard_map/ppermute | solution.py:202
  5.0 0.0 slice-done
  5.0 0.0 slice-done.1
  5.0 0.0 slice-done.2
  5.0 0.0 copy-done
  5.0 2.3 %contract_outer.1 = (bf16[256,2400]{1,0:T(8,128)(2,1)S(1)}, bf16[256,2400]{1,0:T(8,128)(2,1)S(1)}, f32[64,512]{1,0:T(8,128)S(1)}, bf16[64,512]{1,0:T(8,128)(2,1)...) custom-call(bf16[256,208]{1,0:T(8,128)(2,1)S(1)} %get-tuple-element.26.refs_0_, ...), custom_call_target="tpu_custom_call" | custom-call | bytes 13886464 | tf_op jit(solution)/shard_map/contract_outer/pallas_call | solution.py:24
  7.4 2.3 %collective-permute-start.1 = (bf16[64,512]{1,0:T(8,128)(2,1)S(1)}, bf16[64,512]{1,0:T(8,128)(2,1)S(1)}, u32[]{:S(2)}, u32[]{:S(2)}) collective-permute-start(bf16[64,512]{1,0:T(8,128)(2,1)S(1)} %get-tuple-element.32), channel_id=1, source_target_pairs={{0,2},{1,3},{2,0},{3,1},{4,6},{5,7},{6,4},{7,5},{8,10},{9,11},{10,... | collective-permute-start | bytes 196616 | tf_op jit(solution)/shard_map/ppermute | solution.py:202
  9.7 1.3 %collective-permute-start.2 = (bf16[64,512]{1,0:T(8,128)(2,1)S(1)}, bf16[64,512]{1,0:T(8,128)(2,1)S(1)}, u32[]{:S(2)}, u32[]{:S(2)}) collective-permute-start(bf16[64,512]{1,0:T(8,128)(2,1)S(1)} %get-tuple-element.33), channel_id=1, source_target_pairs={{0,1},{1,2},{2,3},{3,0},{4,5},{5,6},{6,7},{7,4},{8,9},{9,10},{10,1... | collective-permute-start | bytes 196616 | tf_op jit(solution)/shard_map/ppermute | solution.py:202
  11.0 2.0 %collective-permute-start.3 = (bf16[64,512]{1,0:T(8,128)(2,1)S(1)}, bf16[64,512]{1,0:T(8,128)(2,1)S(1)}, u32[]{:S(2)}, u32[]{:S(2)}) collective-permute-start(bf16[64,512]{1,0:T(8,128)(2,1)S(1)} %get-tuple-element.34), channel_id=1, source_target_pairs={{0,3},{1,0},{2,1},{3,2},{4,7},{5,4},{6,5},{7,6},{8,11},{9,8},{10,9... | collective-permute-start | bytes 196616 | tf_op jit(solution)/shard_map/ppermute | solution.py:202
  13.0 0.0 copy-start.2
  13.0 0.0 copy-start.1
  13.0 1.5 %contract_inner.1 = (f32[64,512]{1,0:T(8,128)S(1)}, bf16[64,512]{1,0:T(8,128)(2,1)S(1)}, bf16[64,512]{1,0:T(8,128)(2,1)S(1)}, bf16[64,512]{1,0:T(8,128)(2,1)S(1)}) custom-call(bf16[256,2400]{1,0:T(8,128)(2,1)S(1)} %get-tuple-element.39.lhs_re, bf16[256,2400]{1,0:T(8,128)(2,1)S(1)} %get-tuple-element.40.lhs_im, bf16[4800,1024]{1,0:T(8,128)(2,1)S(1)} %bitcast.11), custom_call_target="tpu_custom_call" | custom-call | bytes 12615680 | tf_op jit(solution)/shard_map/contract_inner/pallas_call | solution.py:24
  14.5 0.1 collective-permute-start.7
  14.6 0.3 collective-permute-start.8
  14.9 0.0 collective-permute-done.1.refs_2_
  14.9 3.0 %collective-permute-start.9 = (bf16[64,512]{1,0:T(8,128)(2,1)S(1)}, bf16[64,512]{1,0:T(8,128)(2,1)S(1)}, u32[]{:S(2)}, u32[]{:S(2)}) collective-permute-start(bf16[64,512]{1,0:T(8,128)(2,1)S(1)} %get-tuple-element.44), channel_id=1, source_target_pairs={{0,3},{1,0},{2,1},{3,2},{4,7},{5,4},{6,5},{7,6},{8,11},{9,8},{10,9... | collective-permute-start | bytes 196616 | tf_op jit(solution)/shard_map/ppermute | solution.py:202
  17.9 0.0 copy-done.2
  17.9 0.4 %inverse.1.refs_0_ = f32[112,64]{1,0:T(8,128)S(1)} custom-call(f32[1,16]{1,0:T(1,128)S(1)} %bitcast.16, f32[64,512]{1,0:T(8,128)S(1)} %get-tuple-element.31.after.refs_1_), custom_call_target="tpu_custom_call" | custom-call | bytes 159808 | tf_op jit(solution)/shard_map/inverse/pallas_call | solution.py:24
  18.3 0.0 collective-permute-done.2.refs_3_
  18.3 0.0 collective-permute-done.3.refs_4_
  18.3 0.4 %image_outer.1 = (f32[56,512]{1,0:T(8,128)S(1)}, bf16[56,512]{1,0:T(8,128)(2,1)S(1)}) custom-call(f32[112,64]{1,0:T(8,128)S(1)} %inverse.1.refs_0_, f32[64,512]{1,0:T(8,128)S(1)} %get-tuple-element.31.after.refs_1_, bf16[64,512]{1,0:T(8,128)(2,1)S(1)} %collective-permute-done.1.refs_2_, bf16[64,512]{1,0:T(8,128)(2,1)S(1)} %collective-permute-done.2.refs_3_, ...), custom_call_target="tpu_custom_call" | custom-call | bytes 528384 | tf_op jit(solution)/shard_map/image_outer/pallas_call | solution.py:24
  18.7 1.3 %collective-permute-start.4 = (bf16[56,512]{1,0:T(8,128)(2,1)S(1)}, bf16[56,512]{1,0:T(8,128)(2,1)S(1)}, u32[]{:S(2)}, u32[]{:S(2)}) collective-permute-start(bf16[56,512]{1,0:T(8,128)(2,1)S(1)} %get-tuple-element.36), channel_id=1, source_target_pairs={{0,16},{16,0},{1,17},{17,1},{2,18},{18,2},{3,19},{19,3},{4,20},{20... | collective-permute-start | bytes 172040 | tf_op jit(solution)/shard_map/ppermute | solution.py:202
  20.0 0.0 collective-permute-done.7.refs_2_
  20.0 0.0 collective-permute-done.8.refs_3_
  20.0 0.2 collective-permute-done.9.refs_4_
  20.1 0.4 %image_inner.1 = (f32[56,512]{1,0:T(8,128)S(1)}, bf16[56,512]{1,0:T(8,128)(2,1)S(1)}) custom-call(f32[112,64]{1,0:T(8,128)S(1)} %inverse.1.refs_0_, f32[64,512]{1,0:T(8,128)S(1)} %get-tuple-element.41.refs_1_, bf16[64,512]{1,0:T(8,128)(2,1)S(1)} %collective-permute-done.7.refs_2_, bf16[64,512]{1,0:T(8,128)(2,1)S(1)} %collective-permute-done.8.refs_3_, ...), custom_call_target="tpu_custom_call" | custom-call | bytes 528384 | tf_op jit(solution)/shard_map/image_inner/pallas_call | solution.py:24
  20.5 1.3 %collective-permute-start.10 = (bf16[56,512]{1,0:T(8,128)(2,1)S(1)}, bf16[56,512]{1,0:T(8,128)(2,1)S(1)}, u32[]{:S(2)}, u32[]{:S(2)}) collective-permute-start(bf16[56,512]{1,0:T(8,128)(2,1)S(1)} %get-tuple-element.46), channel_id=1, source_target_pairs={{0,16},{16,0},{1,17},{17,1},{2,18},{18,2},{3,19},{19,3},{4,20},{20... | collective-permute-start | bytes 172040 | tf_op jit(solution)/shard_map/ppermute | solution.py:202
  21.8 0.3 collective-permute-done.4.refs_1_
  22.1 0.0 copy-done.1
  22.1 3.9 %collective-permute-start.5 = (f32[56,128]{1,0:T(8,128)S(1)}, f32[56,128]{1,0:T(8,128)S(1)}, u32[]{:S(2)}, u32[]{:S(2)}) collective-permute-start(f32[56,128]{1,0:T(8,128)S(1)} %get-tuple-element.37), channel_id=1, source_target_pairs={{0,4},{4,0},{8,12},{12,8},{1,5},{5,1},{9,13},{13,9},{2,6},{6,2},{1... | collective-permute-start | bytes 86024 | tf_op jit(solution)/shard_map/ppermute | solution.py:255
  25.9 3.0 %collective-permute-start.6 = (f32[56,128]{1,0:T(8,128)S(1)}, f32[56,128]{1,0:T(8,128)S(1)}, u32[]{:S(2)}, u32[]{:S(2)}) collective-permute-start(f32[56,128]{1,0:T(8,128)S(1)} %get-tuple-element.38), channel_id=1, source_target_pairs={{4,8},{8,4},{5,9},{9,5},{6,10},{10,6},{7,11},{11,7},{20,24},{24,20... | collective-permute-start | bytes 86024 | tf_op jit(solution)/shard_map/ppermute | solution.py:255
  29.0 0.0 collective-permute-done.10.refs_3_
  29.0 0.0 collective-permute-done.5.within
  29.0 2.1 %collective-permute-done.6.across = f32[56,128]{1,0:T(8,128)S(1)} collective-permute-done((f32[56,128]{1,0:T(8,128)S(1)}, f32[56,128]{1,0:T(8,128)S(1)}, u32[]{:S(2)}, u32[]{:S(2)}) %collective-permute-start.6) | collective-permute-done | bytes 28704 | tf_op jit(solution)/shard_map/ppermute | solution.py:255
  31.1 0.9 %smooth.1 = f32[26,2,1024]{2,1,0:T(2,128)} custom-call(f32[1,1024]{1,0:T(1,128)S(1)} %bitcast.15, f32[56,128]{1,0:T(8,128)S(1)} %collective-permute-done.5.within, f32[56,128]{1,0:T(8,128)S(1)} %collective-permute-done.6.across, f32[56,512]{1,0:T(8,128)S(1)} %get-tuple-element.35.refs_0_, bf16[56,512]{1,0:T(8,128)(2,1)S(1)} %collective-permute-done.4.refs_1_, ...), custom_call_target="tpu_custom_call" | custom-call | bytes 618496 | tf_op jit(solution)/shard_map/smooth/pallas_call | solution.py:24
  (2 shorter events, 0.0 us)
Async XLA Ops:
  0.0 5.0 %slice-start = ((s8[9830400]{0:T(1024)(128)(4,1)}), s8[4194304]{0:T(1024)(128)(4,1)S(1)}, s32[]{:S(2)}) async-start(s8[9830400]{0:T(1024)(128)(4,1)} %bitcast.8), calls=%async_computation | async-start | bytes 8388608
  0.0 5.0 %slice-start.1 = ((s8[9830400]{0:T(1024)(128)(4,1)}), s8[4194304]{0:T(1024)(128)(4,1)S(1)}, s32[]{:S(2)}) async-start(s8[9830400]{0:T(1024)(128)(4,1)} %bitcast.8), calls=%async_computation.1 | async-start | bytes 8388608
  0.0 5.0 %slice-start.2 = ((s8[9830400]{0:T(1024)(128)(4,1)}), s8[1441792]{0:T(1024)(128)(4,1)S(1)}, s32[]{:S(2)}) async-start(s8[9830400]{0:T(1024)(128)(4,1)} %bitcast.8), calls=%async_computation.2 | async-start | bytes 2883584
  0.0 5.0 %copy-start = (bf16[8,150,26]{1,0,2:T(8,128)(2,1)S(1)}, bf16[8,150,26]{1,0,2:T(8,128)(2,1)}, u32[]{:S(2)}) copy-start(bf16[8,150,26]{1,0,2:T(8,128)(2,1)} %param.4) | copy-start | bytes 187204
  0.0 5.0 %collective-permute-start = (bf16[208,150]{1,0:T(8,128)(2,1)}, bf16[208,150]{1,0:T(8,128)(2,1)S(1)}, u32[]{:S(2)}, u32[]{:S(2)}) collective-permute-start(bf16[208,150]{1,0:T(8,128)(2,1)} %bitcast.12), channel_id=1, source_target_pairs={{0,16},{16,0},{1,17},{17,1},{2,18},{18,2},{3,19},{19,3},{4,20},{20... | collective-permute-start | bytes 187208 | tf_op jit(solution)/shard_map/ppermute | solution.py:202
  7.4 7.5 %collective-permute-start.1 = (bf16[64,512]{1,0:T(8,128)(2,1)S(1)}, bf16[64,512]{1,0:T(8,128)(2,1)S(1)}, u32[]{:S(2)}, u32[]{:S(2)}) collective-permute-start(bf16[64,512]{1,0:T(8,128)(2,1)S(1)} %get-tuple-element.32), channel_id=1, source_target_pairs={{0,2},{1,3},{2,0},{3,1},{4,6},{5,7},{6,4},{7,5},{8,10},{9,11},{10,... | collective-permute-start | bytes 196616 | tf_op jit(solution)/shard_map/ppermute | solution.py:202
  9.7 8.6 %collective-permute-start.2 = (bf16[64,512]{1,0:T(8,128)(2,1)S(1)}, bf16[64,512]{1,0:T(8,128)(2,1)S(1)}, u32[]{:S(2)}, u32[]{:S(2)}) collective-permute-start(bf16[64,512]{1,0:T(8,128)(2,1)S(1)} %get-tuple-element.33), channel_id=1, source_target_pairs={{0,1},{1,2},{2,3},{3,0},{4,5},{5,6},{6,7},{7,4},{8,9},{9,10},{10,1... | collective-permute-start | bytes 196616 | tf_op jit(solution)/shard_map/ppermute | solution.py:202
  11.0 7.3 %collective-permute-start.3 = (bf16[64,512]{1,0:T(8,128)(2,1)S(1)}, bf16[64,512]{1,0:T(8,128)(2,1)S(1)}, u32[]{:S(2)}, u32[]{:S(2)}) collective-permute-start(bf16[64,512]{1,0:T(8,128)(2,1)S(1)} %get-tuple-element.34), channel_id=1, source_target_pairs={{0,3},{1,0},{2,1},{3,2},{4,7},{5,4},{6,5},{7,6},{8,11},{9,8},{10,9... | collective-permute-start | bytes 196616 | tf_op jit(solution)/shard_map/ppermute | solution.py:202
  13.0 4.9 %copy-start.2 = (f32[16]{0:T(128)S(1)}, f32[16]{0:T(128)}, u32[]{:S(2)}) copy-start(f32[16]{0:T(128)} %param.6) | copy-start | bytes 196
  13.0 9.1 %copy-start.1 = (f32[1024]{0:T(1024)S(1)}, f32[1024]{0:T(1024)}, u32[]{:S(2)}) copy-start(f32[1024]{0:T(1024)} %param.7) | copy-start | bytes 12292
  14.5 5.4 %collective-permute-start.7 = (bf16[64,512]{1,0:T(8,128)(2,1)S(1)}, bf16[64,512]{1,0:T(8,128)(2,1)S(1)}, u32[]{:S(2)}, u32[]{:S(2)}) collective-permute-start(bf16[64,512]{1,0:T(8,128)(2,1)S(1)} %get-tuple-element.42), channel_id=1, source_target_pairs={{0,2},{1,3},{2,0},{3,1},{4,6},{5,7},{6,4},{7,5},{8,10},{9,11},{10,... | collective-permute-start | bytes 196616 | tf_op jit(solution)/shard_map/ppermute | solution.py:202
  14.6 5.4 %collective-permute-start.8 = (bf16[64,512]{1,0:T(8,128)(2,1)S(1)}, bf16[64,512]{1,0:T(8,128)(2,1)S(1)}, u32[]{:S(2)}, u32[]{:S(2)}) collective-permute-start(bf16[64,512]{1,0:T(8,128)(2,1)S(1)} %get-tuple-element.43), channel_id=1, source_target_pairs={{0,1},{1,2},{2,3},{3,0},{4,5},{5,6},{6,7},{7,4},{8,9},{9,10},{10,1... | collective-permute-start | bytes 196616 | tf_op jit(solution)/shard_map/ppermute | solution.py:202
  14.9 5.3 %collective-permute-start.9 = (bf16[64,512]{1,0:T(8,128)(2,1)S(1)}, bf16[64,512]{1,0:T(8,128)(2,1)S(1)}, u32[]{:S(2)}, u32[]{:S(2)}) collective-permute-start(bf16[64,512]{1,0:T(8,128)(2,1)S(1)} %get-tuple-element.44), channel_id=1, source_target_pairs={{0,3},{1,0},{2,1},{3,2},{4,7},{5,4},{6,5},{7,6},{8,11},{9,8},{10,9... | collective-permute-start | bytes 196616 | tf_op jit(solution)/shard_map/ppermute | solution.py:202
  18.7 3.4 %collective-permute-start.4 = (bf16[56,512]{1,0:T(8,128)(2,1)S(1)}, bf16[56,512]{1,0:T(8,128)(2,1)S(1)}, u32[]{:S(2)}, u32[]{:S(2)}) collective-permute-start(bf16[56,512]{1,0:T(8,128)(2,1)S(1)} %get-tuple-element.36), channel_id=1, source_target_pairs={{0,16},{16,0},{1,17},{17,1},{2,18},{18,2},{3,19},{19,3},{4,20},{20... | collective-permute-start | bytes 172040 | tf_op jit(solution)/shard_map/ppermute | solution.py:202
  20.5 8.5 %collective-permute-start.10 = (bf16[56,512]{1,0:T(8,128)(2,1)S(1)}, bf16[56,512]{1,0:T(8,128)(2,1)S(1)}, u32[]{:S(2)}, u32[]{:S(2)}) collective-permute-start(bf16[56,512]{1,0:T(8,128)(2,1)S(1)} %get-tuple-element.46), channel_id=1, source_target_pairs={{0,16},{16,0},{1,17},{17,1},{2,18},{18,2},{3,19},{19,3},{4,20},{20... | collective-permute-start | bytes 172040 | tf_op jit(solution)/shard_map/ppermute | solution.py:202
  22.1 6.9 %collective-permute-start.5 = (f32[56,128]{1,0:T(8,128)S(1)}, f32[56,128]{1,0:T(8,128)S(1)}, u32[]{:S(2)}, u32[]{:S(2)}) collective-permute-start(f32[56,128]{1,0:T(8,128)S(1)} %get-tuple-element.37), channel_id=1, source_target_pairs={{0,4},{4,0},{8,12},{12,8},{1,5},{5,1},{9,13},{13,9},{2,6},{6,2},{1... | collective-permute-start | bytes 86024 | tf_op jit(solution)/shard_map/ppermute | solution.py:255
  25.9 5.2 %collective-permute-start.6 = (f32[56,128]{1,0:T(8,128)S(1)}, f32[56,128]{1,0:T(8,128)S(1)}, u32[]{:S(2)}, u32[]{:S(2)}) collective-permute-start(f32[56,128]{1,0:T(8,128)S(1)} %get-tuple-element.38), channel_id=1, source_target_pairs={{4,8},{8,4},{5,9},{9,5},{6,10},{10,6},{7,11},{11,7},{20,24},{24,20... | collective-permute-start | bytes 86024 | tf_op jit(solution)/shard_map/ppermute | solution.py:255

commit v4 on v3

--- a/solution.py
+++ b/solution.py
@@ -8,6 +8,7 @@
 from jax.experimental.pallas import tpu as pltpu
 from jax.sharding import PartitionSpec as P
 
+
 LEN = 840
 OUTER = 4
 PREP = 10**10
@@ -19,7 +20,7 @@
     return pl.BlockSpec(memory_space=pltpu.VMEM)
 
 
-def call(body, name, out_shape, *args, flops=0, limit=4 << 20):
+def call(body, out_shape, *args, flops=0, limit=4 << 20):
     moved = sum(a.size * a.dtype.itemsize for a in [*args, *jax.tree.leaves(out_shape)])
     return pl.pallas_call(
         body,
@@ -28,7 +29,6 @@
         out_shape=out_shape,
         compiler_params=pltpu.CompilerParams(vmem_limit_bytes=limit),
         cost_estimate=pl.CostEstimate(flops=flops, transcendentals=0, bytes_accessed=moved),
-        name=name,
     )(*args)
 
 
@@ -202,7 +202,7 @@
     return lax.ppermute(value, axis, [(i, (i + shift) % size) for i in range(size)])
 
 
-def local(series, kernel, prior_spectrum, prior_scale):
+def steps(series, kernel, prior_spectrum, prior_scale):
     freqs, senss, params = (lax.axis_size(a) for a in ("freq", "sens", "param"))
     probes, sens_dev, times = series.shape
     bins, cols = kernel.shape[1], kernel.shape[3]
@@ -214,26 +214,21 @@
     pieces = [own_series] + [rotate(own_series, "freq", -j) for j in range(1, freqs)]
     *tables, spread = call(
         functools.partial(prepare_body, (bins, times, probes, group, freqs, senss)),
-        "prepare",
         [shape((senss * block, times * probes), BF)] * (2 * freqs)
         + [shape((sens_dev, sens_dev * bins), BF)],
         flops=PREP,
     )
     operator = kernel.transpose(0, 2, 1, 3).reshape(2 * sens_dev * bins, cols)
-    edge = cols // OUTER
+    edge = cols * OUTER // 16
     blocks = lambda width: [shape((block, width), BF if i else F32) for i in range(senss)]
     lhs_re, lhs_im, *outer = call(
         functools.partial(contract_body, bins, senss, freqs),
-        "contract_outer",
         [shape((senss * block, sens_dev * bins), BF)] * 2 + blocks(2 * edge),
         *tables, *pieces, spread, operator,
     )
-    inner = call(
-        inner_body, "contract_inner", blocks(cols - 2 * edge), lhs_re, lhs_im, operator
-    )
+    inner = call(inner_body, blocks(cols - 2 * edge), lhs_re, lhs_im, operator)
     inverse = call(
         functools.partial(inverse_body, (bins, times, group, freqs, rows)),
-        "inverse",
         shape((freqs * rows, block), F32),
         prior_spectrum.reshape(1, bins), outer[0],
     )
@@ -242,22 +237,20 @@
     inner = [inner[0]] + [rotate(inner[d], "sens", d) for d in order]
     images = lambda width: [shape((rows, width), BF if i else F32) for i in range(freqs)]
     as_image = functools.partial(image_body, rows)
-    outer = call(as_image, "image_outer", images(2 * edge), inverse, *outer)
+    outer = call(as_image, images(2 * edge), inverse, *outer)
     outer = [outer[0]] + [rotate(outer[j], "freq", j) for j in range(1, freqs)]
-    inner = call(as_image, "image_inner", images(cols - 2 * edge), inverse, *inner)
+    inner = call(as_image, images(cols - 2 * edge), inverse, *inner)
     inner = [inner[0]] + [rotate(inner[j], "freq", j) for j in range(1, freqs)]
     scale = prior_scale.reshape(1, cols)
     lanes = min(128, edge)
-    swaps = call(
-        functools.partial(edge_body, lanes), "edge", [shape((rows, lanes), F32)] * 2, scale, *outer
-    )
-    swaps = [
-        lax.ppermute(swaps[i], "param", [(a + d, a + 1 - d) for a in range(i, params - 1, 2) for d in (0, 1)])
-        for i in (0, 1)
-    ]
+    swaps = list(call(
+        functools.partial(edge_body, lanes), [shape((rows, lanes), F32)] * 2, scale, *outer)
+    )
+    for i in (0, 1):
+        pairs = [(a, a + 1) for a in range(i, params - 1, 2)]
+        swaps[i] = lax.ppermute(swaps[i], "param", pairs + [(b, a) for a, b in pairs])
     return call(
         functools.partial(smooth_body, freqs),
-        "smooth",
         shape((times, group, cols), F32),
         scale, *swaps, *outer, *inner,
     )
@@ -266,5 +259,5 @@
 def solution(mesh):
     placed = (P(None, "sens", "freq"), P(None, "freq", "sens", "param"), P("freq"), P("param"))
     return jax.shard_map(
-        local, mesh=mesh, in_specs=placed, out_specs=P("freq", "sens", "param"), check_vma=False
-    )
+        steps, mesh=mesh, in_specs=placed, out_specs=P("freq", "sens", "param"), check_vma=False
+    )

time: 32.2 us -> 32.2 us (level)
  no operation moved by 1% of the time
where the time goes in v4:
time: 32.2 us; the launch traced here: 32 us
  starting transfers between devices  20.6 us (64%)
  Pallas kernels  6.54 us (20%)
  waiting for transfers between devices  4.74 us (15%)
    ppermute x9, starting transfers between devices, rotate(): lax.ppermute(value, axis, [(i, (i + shift) % size) for i in range(size)])  13.7 us
    ppermute x2, starting transfers between devices, steps(): lax.ppermute(swaps[i], 'param', pairs + [(b, a) for a, b in pairs])  6.9 us
    pallas_call x8, Pallas kernels, call(): pl.pallas_call(body, in_specs=[vmem()] * len(args), out_specs=jax.tree.ma...  6.54 us
    ppermute x9, waiting for transfers between devices, rotate(): lax.ppermute(value, axis, [(i, (i + shift) % size) for i in range(size)])  2.63 us
    ppermute x2, waiting for transfers between devices, steps(): lax.ppermute(swaps[i], 'param', pairs + [(b, a) for a, b in pairs])  2.11 us
  transfers between devices with their start and end apart: 11, of which 4 were waited for; matrix products, arithmetic and copies ran while one was open for 0% of the time, Pallas kernels for 10%

profile of v4, /device:TPU:1, one launch (start us, length us, event | category | flops | bytes accessed | tf_op | source)
XLA Modules:
  0.0 32.0 jit_solution(12896899749877231711)
XLA Ops:
  0.0 0.0 slice-start
  0.0 0.0 slice-start.1
  0.0 0.0 slice-start.2
  0.0 0.0 copy-start
  0.0 2.1 %collective-permute-start = (bf16[208,150]{1,0:T(8,128)(2,1)}, bf16[208,150]{1,0:T(8,128)(2,1)S(1)}, u32[]{:S(2)}, u32[]{:S(2)}) collective-permute-start(bf16[208,150]{1,0:T(8,128)(2,1)} %bitcast.12), channel_id=1, source_target_pairs={{0,16},{16,0},{1,17},{17,1},{2,18},{18,2},{3,19},{19,3},{4,20},{20... | collective-permute-start | bytes 187208 | tf_op jit(solution)/shard_map/ppermute | solution.py:202
  2.1 0.7 %shard_map.46 = (bf16[256,208]{1,0:T(8,128)(2,1)S(1)}, bf16[256,208]{1,0:T(8,128)(2,1)S(1)}, bf16[256,208]{1,0:T(8,128)(2,1)S(1)}, bf16[256,208]{1,0:T(8,128)(2,1)S(1)}, bf16[150,2400]{1,0:T(8,128)(2,1)S(1)}) custom-call(), custom_call_target="tpu_custom_call" | custom-call | flops 10000000000 | bytes 1145984 | tf_op jit(solution)/shard_map/pallas_call | solution.py:25
  2.8 2.2 %collective-permute-done.refs_5_ = bf16[208,150]{1,0:T(8,128)(2,1)S(1)} collective-permute-done((bf16[208,150]{1,0:T(8,128)(2,1)}, bf16[208,150]{1,0:T(8,128)(2,1)S(1)}, u32[]{:S(2)}, u32[]{:S(2)}) %collective-permute-start) | collective-permute-done | bytes 62432 | tf_op jit(solution)/shard_map/ppermute | solution.py:202
  5.0 0.0 slice-done
  5.0 0.0 slice-done.1
  5.0 0.0 slice-done.2
  5.0 0.0 copy-done
  5.0 2.3 %shard_map.47 = (bf16[256,2400]{1,0:T(8,128)(2,1)S(1)}, bf16[256,2400]{1,0:T(8,128)(2,1)S(1)}, f32[64,512]{1,0:T(8,128)S(1)}, bf16[64,512]{1,0:T(8,128)(2,1)S(1)...) custom-call(bf16[256,208]{1,0:T(8,128)(2,1)S(1)} %get-tuple-element.26.refs_0_, ...), custom_call_target="tpu_custom_call" | custom-call | bytes 13886464 | tf_op jit(solution)/shard_map/pallas_call | solution.py:25
  7.4 2.3 %collective-permute-start.1 = (bf16[64,512]{1,0:T(8,128)(2,1)S(1)}, bf16[64,512]{1,0:T(8,128)(2,1)S(1)}, u32[]{:S(2)}, u32[]{:S(2)}) collective-permute-start(bf16[64,512]{1,0:T(8,128)(2,1)S(1)} %get-tuple-element.32), channel_id=1, source_target_pairs={{0,2},{1,3},{2,0},{3,1},{4,6},{5,7},{6,4},{7,5},{8,10},{9,11},{10,... | collective-permute-start | bytes 196616 | tf_op jit(solution)/shard_map/ppermute | solution.py:202
  9.7 1.3 %collective-permute-start.2 = (bf16[64,512]{1,0:T(8,128)(2,1)S(1)}, bf16[64,512]{1,0:T(8,128)(2,1)S(1)}, u32[]{:S(2)}, u32[]{:S(2)}) collective-permute-start(bf16[64,512]{1,0:T(8,128)(2,1)S(1)} %get-tuple-element.33), channel_id=1, source_target_pairs={{0,1},{1,2},{2,3},{3,0},{4,5},{5,6},{6,7},{7,4},{8,9},{9,10},{10,1... | collective-permute-start | bytes 196616 | tf_op jit(solution)/shard_map/ppermute | solution.py:202
  11.0 2.0 %collective-permute-start.3 = (bf16[64,512]{1,0:T(8,128)(2,1)S(1)}, bf16[64,512]{1,0:T(8,128)(2,1)S(1)}, u32[]{:S(2)}, u32[]{:S(2)}) collective-permute-start(bf16[64,512]{1,0:T(8,128)(2,1)S(1)} %get-tuple-element.34), channel_id=1, source_target_pairs={{0,3},{1,0},{2,1},{3,2},{4,7},{5,4},{6,5},{7,6},{8,11},{9,8},{10,9... | collective-permute-start | bytes 196616 | tf_op jit(solution)/shard_map/ppermute | solution.py:202
  13.0 0.0 copy-start.2
  13.0 0.0 copy-start.1
  13.0 1.5 %shard_map.51 = (f32[64,512]{1,0:T(8,128)S(1)}, bf16[64,512]{1,0:T(8,128)(2,1)S(1)}, bf16[64,512]{1,0:T(8,128)(2,1)S(1)}, bf16[64,512]{1,0:T(8,128)(2,1)S(1)}) custom-call(bf16[256,2400]{1,0:T(8,128)(2,1)S(1)} %get-tuple-element.39.lhs_re, bf16[256,2400]{1,0:T(8,128)(2,1)S(1)} %get-tuple-element.40.lhs_im, bf16[4800,1024]{1,0:T(8,128)(2,1)S(1)} %bitcast.11), custom_call_target="tpu_custom_call" | custom-call | bytes 12615680 | tf_op jit(solution)/shard_map/pallas_call | solution.py:25
  14.5 0.1 collective-permute-start.7
  14.6 0.3 collective-permute-start.8
  14.9 0.0 collective-permute-done.1.refs_2_
  14.9 3.0 %collective-permute-start.9 = (bf16[64,512]{1,0:T(8,128)(2,1)S(1)}, bf16[64,512]{1,0:T(8,128)(2,1)S(1)}, u32[]{:S(2)}, u32[]{:S(2)}) collective-permute-start(bf16[64,512]{1,0:T(8,128)(2,1)S(1)} %get-tuple-element.44), channel_id=1, source_target_pairs={{0,3},{1,0},{2,1},{3,2},{4,7},{5,4},{6,5},{7,6},{8,11},{9,8},{10,9... | collective-permute-start | bytes 196616 | tf_op jit(solution)/shard_map/ppermute | solution.py:202
  17.9 0.0 copy-done.2
  17.9 0.4 %shard_map.48.refs_0_ = f32[112,64]{1,0:T(8,128)S(1)} custom-call(f32[1,16]{1,0:T(1,128)S(1)} %bitcast.16, f32[64,512]{1,0:T(8,128)S(1)} %get-tuple-element.31.after.refs_1_), custom_call_target="tpu_custom_call" | custom-call | bytes 159808 | tf_op jit(solution)/shard_map/pallas_call | solution.py:25
  18.3 0.0 collective-permute-done.2.refs_3_
  18.3 0.0 collective-permute-done.3.refs_4_
  18.3 0.4 %shard_map.49 = (f32[56,512]{1,0:T(8,128)S(1)}, bf16[56,512]{1,0:T(8,128)(2,1)S(1)}) custom-call(f32[112,64]{1,0:T(8,128)S(1)} %shard_map.48.refs_0_, f32[64,512]{1,0:T(8,128)S(1)} %get-tuple-element.31.after.refs_1_, bf16[64,512]{1,0:T(8,128)(2,1)S(1)} %collective-permute-done.1.refs_2_, bf16[64,512]{1,0:T(8,128)(2,1)S(1)} %collective-permute-done.2.refs_3_, ...), custom_call_target="tpu_custom_call" | custom-call | bytes 528384 | tf_op jit(solution)/shard_map/pallas_call | solution.py:25
  18.7 1.3 %collective-permute-start.4 = (bf16[56,512]{1,0:T(8,128)(2,1)S(1)}, bf16[56,512]{1,0:T(8,128)(2,1)S(1)}, u32[]{:S(2)}, u32[]{:S(2)}) collective-permute-start(bf16[56,512]{1,0:T(8,128)(2,1)S(1)} %get-tuple-element.36), channel_id=1, source_target_pairs={{0,16},{16,0},{1,17},{17,1},{2,18},{18,2},{3,19},{19,3},{4,20},{20... | collective-permute-start | bytes 172040 | tf_op jit(solution)/shard_map/ppermute | solution.py:202
  20.0 0.0 collective-permute-done.7.refs_2_
  20.0 0.0 collective-permute-done.8.refs_3_
  20.0 0.2 collective-permute-done.9.refs_4_
  20.1 0.4 %shard_map.52 = (f32[56,512]{1,0:T(8,128)S(1)}, bf16[56,512]{1,0:T(8,128)(2,1)S(1)}) custom-call(f32[112,64]{1,0:T(8,128)S(1)} %shard_map.48.refs_0_, f32[64,512]{1,0:T(8,128)S(1)} %get-tuple-element.41.refs_1_, bf16[64,512]{1,0:T(8,128)(2,1)S(1)} %collective-permute-done.7.refs_2_, bf16[64,512]{1,0:T(8,128)(2,1)S(1)} %collective-permute-done.8.refs_3_, ...), custom_call_target="tpu_custom_call" | custom-call | bytes 528384 | tf_op jit(solution)/shard_map/pallas_call | solution.py:25
  20.5 1.3 %collective-permute-start.10 = (bf16[56,512]{1,0:T(8,128)(2,1)S(1)}, bf16[56,512]{1,0:T(8,128)(2,1)S(1)}, u32[]{:S(2)}, u32[]{:S(2)}) collective-permute-start(bf16[56,512]{1,0:T(8,128)(2,1)S(1)} %get-tuple-element.46), channel_id=1, source_target_pairs={{0,16},{16,0},{1,17},{17,1},{2,18},{18,2},{3,19},{19,3},{4,20},{20... | collective-permute-start | bytes 172040 | tf_op jit(solution)/shard_map/ppermute | solution.py:202
  21.8 0.3 collective-permute-done.4.refs_1_
  22.1 0.0 copy-done.1
  22.1 3.9 %collective-permute-start.5 = (f32[56,128]{1,0:T(8,128)S(1)}, f32[56,128]{1,0:T(8,128)S(1)}, u32[]{:S(2)}, u32[]{:S(2)}) collective-permute-start(f32[56,128]{1,0:T(8,128)S(1)} %get-tuple-element.37), channel_id=1, source_target_pairs={{0,4},{8,12},{4,0},{12,8},{1,5},{9,13},{5,1},{13,9},{2,6},{10,14},... | collective-permute-start | bytes 86024 | tf_op jit(solution)/shard_map/ppermute | solution.py:251
  25.9 3.0 %collective-permute-start.6 = (f32[56,128]{1,0:T(8,128)S(1)}, f32[56,128]{1,0:T(8,128)S(1)}, u32[]{:S(2)}, u32[]{:S(2)}) collective-permute-start(f32[56,128]{1,0:T(8,128)S(1)} %get-tuple-element.38), channel_id=1, source_target_pairs={{4,8},{8,4},{5,9},{9,5},{6,10},{10,6},{7,11},{11,7},{20,24},{24,20... | collective-permute-start | bytes 86024 | tf_op jit(solution)/shard_map/ppermute | solution.py:251
  29.0 0.0 collective-permute-done.10.refs_3_
  29.0 0.0 collective-permute-done.5.within
  29.0 2.1 %collective-permute-done.6.across = f32[56,128]{1,0:T(8,128)S(1)} collective-permute-done((f32[56,128]{1,0:T(8,128)S(1)}, f32[56,128]{1,0:T(8,128)S(1)}, u32[]{:S(2)}, u32[]{:S(2)}) %collective-permute-start.6) | collective-permute-done | bytes 28704 | tf_op jit(solution)/shard_map/ppermute | solution.py:251
  31.1 0.9 %shard_map.53 = f32[26,2,1024]{2,1,0:T(2,128)} custom-call(f32[1,1024]{1,0:T(1,128)S(1)} %bitcast.15, f32[56,128]{1,0:T(8,128)S(1)} %collective-permute-done.5.within, f32[56,128]{1,0:T(8,128)S(1)} %collective-permute-done.6.across, f32[56,512]{1,0:T(8,128)S(1)} %get-tuple-element.35.refs_0_, bf16[56,512]{1,0:T(8,128)(2,1)S(1)} %collective-permute-done.4.refs_1_, ...), custom_call_target="tpu_custom_call" | custom-call | bytes 618496 | tf_op jit(solution)/shard_map/pallas_call | solution.py:25
  (2 shorter events, 0.0 us)
Async XLA Ops:
  0.0 5.0 %slice-start = ((s8[9830400]{0:T(1024)(128)(4,1)}), s8[4194304]{0:T(1024)(128)(4,1)S(1)}, s32[]{:S(2)}) async-start(s8[9830400]{0:T(1024)(128)(4,1)} %bitcast.8), calls=%async_computation | async-start | bytes 8388608
  0.0 5.0 %slice-start.1 = ((s8[9830400]{0:T(1024)(128)(4,1)}), s8[4194304]{0:T(1024)(128)(4,1)S(1)}, s32[]{:S(2)}) async-start(s8[9830400]{0:T(1024)(128)(4,1)} %bitcast.8), calls=%async_computation.1 | async-start | bytes 8388608
  0.0 5.0 %slice-start.2 = ((s8[9830400]{0:T(1024)(128)(4,1)}), s8[1441792]{0:T(1024)(128)(4,1)S(1)}, s32[]{:S(2)}) async-start(s8[9830400]{0:T(1024)(128)(4,1)} %bitcast.8), calls=%async_computation.2 | async-start | bytes 2883584
  0.0 5.0 %copy-start = (bf16[8,150,26]{1,0,2:T(8,128)(2,1)S(1)}, bf16[8,150,26]{1,0,2:T(8,128)(2,1)}, u32[]{:S(2)}) copy-start(bf16[8,150,26]{1,0,2:T(8,128)(2,1)} %param.4) | copy-start | bytes 187204
  0.0 5.0 %collective-permute-start = (bf16[208,150]{1,0:T(8,128)(2,1)}, bf16[208,150]{1,0:T(8,128)(2,1)S(1)}, u32[]{:S(2)}, u32[]{:S(2)}) collective-permute-start(bf16[208,150]{1,0:T(8,128)(2,1)} %bitcast.12), channel_id=1, source_target_pairs={{0,16},{16,0},{1,17},{17,1},{2,18},{18,2},{3,19},{19,3},{4,20},{20... | collective-permute-start | bytes 187208 | tf_op jit(solution)/shard_map/ppermute | solution.py:202
  7.4 7.5 %collective-permute-start.1 = (bf16[64,512]{1,0:T(8,128)(2,1)S(1)}, bf16[64,512]{1,0:T(8,128)(2,1)S(1)}, u32[]{:S(2)}, u32[]{:S(2)}) collective-permute-start(bf16[64,512]{1,0:T(8,128)(2,1)S(1)} %get-tuple-element.32), channel_id=1, source_target_pairs={{0,2},{1,3},{2,0},{3,1},{4,6},{5,7},{6,4},{7,5},{8,10},{9,11},{10,... | collective-permute-start | bytes 196616 | tf_op jit(solution)/shard_map/ppermute | solution.py:202
  9.7 8.6 %collective-permute-start.2 = (bf16[64,512]{1,0:T(8,128)(2,1)S(1)}, bf16[64,512]{1,0:T(8,128)(2,1)S(1)}, u32[]{:S(2)}, u32[]{:S(2)}) collective-permute-start(bf16[64,512]{1,0:T(8,128)(2,1)S(1)} %get-tuple-element.33), channel_id=1, source_target_pairs={{0,1},{1,2},{2,3},{3,0},{4,5},{5,6},{6,7},{7,4},{8,9},{9,10},{10,1... | collective-permute-start | bytes 196616 | tf_op jit(solution)/shard_map/ppermute | solution.py:202
  11.0 7.3 %collective-permute-start.3 = (bf16[64,512]{1,0:T(8,128)(2,1)S(1)}, bf16[64,512]{1,0:T(8,128)(2,1)S(1)}, u32[]{:S(2)}, u32[]{:S(2)}) collective-permute-start(bf16[64,512]{1,0:T(8,128)(2,1)S(1)} %get-tuple-element.34), channel_id=1, source_target_pairs={{0,3},{1,0},{2,1},{3,2},{4,7},{5,4},{6,5},{7,6},{8,11},{9,8},{10,9... | collective-permute-start | bytes 196616 | tf_op jit(solution)/shard_map/ppermute | solution.py:202
  13.0 4.9 %copy-start.2 = (f32[16]{0:T(128)S(1)}, f32[16]{0:T(128)}, u32[]{:S(2)}) copy-start(f32[16]{0:T(128)} %param.6) | copy-start | bytes 196
  13.0 9.1 %copy-start.1 = (f32[1024]{0:T(1024)S(1)}, f32[1024]{0:T(1024)}, u32[]{:S(2)}) copy-start(f32[1024]{0:T(1024)} %param.7) | copy-start | bytes 12292
  14.5 5.4 %collective-permute-start.7 = (bf16[64,512]{1,0:T(8,128)(2,1)S(1)}, bf16[64,512]{1,0:T(8,128)(2,1)S(1)}, u32[]{:S(2)}, u32[]{:S(2)}) collective-permute-start(bf16[64,512]{1,0:T(8,128)(2,1)S(1)} %get-tuple-element.42), channel_id=1, source_target_pairs={{0,2},{1,3},{2,0},{3,1},{4,6},{5,7},{6,4},{7,5},{8,10},{9,11},{10,... | collective-permute-start | bytes 196616 | tf_op jit(solution)/shard_map/ppermute | solution.py:202
  14.6 5.4 %collective-permute-start.8 = (bf16[64,512]{1,0:T(8,128)(2,1)S(1)}, bf16[64,512]{1,0:T(8,128)(2,1)S(1)}, u32[]{:S(2)}, u32[]{:S(2)}) collective-permute-start(bf16[64,512]{1,0:T(8,128)(2,1)S(1)} %get-tuple-element.43), channel_id=1, source_target_pairs={{0,1},{1,2},{2,3},{3,0},{4,5},{5,6},{6,7},{7,4},{8,9},{9,10},{10,1... | collective-permute-start | bytes 196616 | tf_op jit(solution)/shard_map/ppermute | solution.py:202
  14.9 5.3 %collective-permute-start.9 = (bf16[64,512]{1,0:T(8,128)(2,1)S(1)}, bf16[64,512]{1,0:T(8,128)(2,1)S(1)}, u32[]{:S(2)}, u32[]{:S(2)}) collective-permute-start(bf16[64,512]{1,0:T(8,128)(2,1)S(1)} %get-tuple-element.44), channel_id=1, source_target_pairs={{0,3},{1,0},{2,1},{3,2},{4,7},{5,4},{6,5},{7,6},{8,11},{9,8},{10,9... | collective-permute-start | bytes 196616 | tf_op jit(solution)/shard_map/ppermute | solution.py:202
  18.7 3.4 %collective-permute-start.4 = (bf16[56,512]{1,0:T(8,128)(2,1)S(1)}, bf16[56,512]{1,0:T(8,128)(2,1)S(1)}, u32[]{:S(2)}, u32[]{:S(2)}) collective-permute-start(bf16[56,512]{1,0:T(8,128)(2,1)S(1)} %get-tuple-element.36), channel_id=1, source_target_pairs={{0,16},{16,0},{1,17},{17,1},{2,18},{18,2},{3,19},{19,3},{4,20},{20... | collective-permute-start | bytes 172040 | tf_op jit(solution)/shard_map/ppermute | solution.py:202
  20.5 8.5 %collective-permute-start.10 = (bf16[56,512]{1,0:T(8,128)(2,1)S(1)}, bf16[56,512]{1,0:T(8,128)(2,1)S(1)}, u32[]{:S(2)}, u32[]{:S(2)}) collective-permute-start(bf16[56,512]{1,0:T(8,128)(2,1)S(1)} %get-tuple-element.46), channel_id=1, source_target_pairs={{0,16},{16,0},{1,17},{17,1},{2,18},{18,2},{3,19},{19,3},{4,20},{20... | collective-permute-start | bytes 172040 | tf_op jit(solution)/shard_map/ppermute | solution.py:202
  22.1 6.9 %collective-permute-start.5 = (f32[56,128]{1,0:T(8,128)S(1)}, f32[56,128]{1,0:T(8,128)S(1)}, u32[]{:S(2)}, u32[]{:S(2)}) collective-permute-start(f32[56,128]{1,0:T(8,128)S(1)} %get-tuple-element.37), channel_id=1, source_target_pairs={{0,4},{8,12},{4,0},{12,8},{1,5},{9,13},{5,1},{13,9},{2,6},{10,14},... | collective-permute-start | bytes 86024 | tf_op jit(solution)/shard_map/ppermute | solution.py:251
  25.9 5.2 %collective-permute-start.6 = (f32[56,128]{1,0:T(8,128)S(1)}, f32[56,128]{1,0:T(8,128)S(1)}, u32[]{:S(2)}, u32[]{:S(2)}) collective-permute-start(f32[56,128]{1,0:T(8,128)S(1)} %get-tuple-element.38), channel_id=1, source_target_pairs={{4,8},{8,4},{5,9},{9,5},{6,10},{10,6},{7,11},{11,7},{20,24},{24,20... | collective-permute-start | bytes 86024 | tf_op jit(solution)/shard_map/ppermute | solution.py:251

commit v5 on v4

--- a/solution.py
+++ b/solution.py
@@ -188,9 +188,11 @@
     value = value * scale[...]
     lane = iota(value.shape, 1)
     width = within.shape[1]
-    even = lax.axis_index("param") % 2 == 0
+    at, ends = lax.axis_index("param"), lax.axis_size("param") - 1
+    even = at % 2 == 0
     before = jnp.where(even, across[:, width - 1 :], within[:, width - 1 :])
     after = jnp.where(even, within[:, :1], across[:, :1])
+    before, after = jnp.where(at > 0, before, 0.0), jnp.where(at < ends, after, 0.0)
     left = jnp.where(lane == 0, before, pltpu.roll(value, 1, 1))
     right = jnp.where(lane == cols - 1, after, pltpu.roll(value, cols - 1, 1))
     value = (0.5 * value + 0.25 * (left + right)) * scale[...]
@@ -247,7 +249,7 @@
         functools.partial(edge_body, lanes), [shape((rows, lanes), F32)] * 2, scale, *outer)
     )
     for i in (0, 1):
-        pairs = [(a, a + 1) for a in range(i, params - 1, 2)]
+        pairs = [(a, (a + 1) % params) for a in range(i, params // 2 * 2, 2)]
         swaps[i] = lax.ppermute(swaps[i], "param", pairs + [(b, a) for a, b in pairs])
     return call(
         functools.partial(smooth_body, freqs),

time: 32.2 us -> 30.4 us (0.944)
  starting transfers between devices: 20.6 us -> 18.7 us
    ppermute x2, starting transfers between devices: 6.9 us -> 5.05 us  [steps(): lax.ppermute(swaps[i], 'param', pairs + [(b, a) for a, b in pairs])]
  transfers between devices with their start and end apart: 11 -> 11, of which waited for: 4 -> 4; matrix products, arithmetic and copies ran while one was open for 0% -> 0% of each run, Pallas kernels for 10% -> 11%
where the time goes in v5:
time: 30.4 us; the launch traced here: 30.2 us
  starting transfers between devices  18.7 us (62%)
  Pallas kernels  6.55 us (22%)
  waiting for transfers between devices  4.72 us (16%)
    ppermute x9, starting transfers between devices, rotate(): lax.ppermute(value, axis, [(i, (i + shift) % size) for i in range(size)])  13.7 us
    pallas_call x8, Pallas kernels, call(): pl.pallas_call(body, in_specs=[vmem()] * len(args), out_specs=jax.tree.ma...  6.55 us
    ppermute x2, starting transfers between devices, steps(): lax.ppermute(swaps[i], 'param', pairs + [(b, a) for a, b in pairs])  5.05 us
    ppermute x9, waiting for transfers between devices, rotate(): lax.ppermute(value, axis, [(i, (i + shift) % size) for i in range(size)])  2.63 us
    ppermute x2, waiting for transfers between devices, steps(): lax.ppermute(swaps[i], 'param', pairs + [(b, a) for a, b in pairs])  2.09 us
  transfers between devices with their start and end apart: 11, of which 4 were waited for; matrix products, arithmetic and copies ran while one was open for 0% of the time, Pallas kernels for 11%

profile of v5, /device:TPU:1, one launch (start us, length us, event | category | flops | bytes accessed | tf_op | source)
XLA Modules:
  0.0 30.2 jit_solution(10581060211794837610)
XLA Ops:
  0.0 0.0 slice-start
  0.0 0.0 slice-start.1
  0.0 0.0 slice-start.2
  0.0 0.0 copy-start
  0.0 2.1 %collective-permute-start = (bf16[208,150]{1,0:T(8,128)(2,1)}, bf16[208,150]{1,0:T(8,128)(2,1)S(1)}, u32[]{:S(2)}, u32[]{:S(2)}) collective-permute-start(bf16[208,150]{1,0:T(8,128)(2,1)} %bitcast.12), channel_id=1, source_target_pairs={{0,16},{16,0},{1,17},{17,1},{2,18},{18,2},{3,19},{19,3},{4,20},{20... | collective-permute-start | bytes 187208 | tf_op jit(solution)/shard_map/ppermute | solution.py:204
  2.1 0.7 %shard_map.46 = (bf16[256,208]{1,0:T(8,128)(2,1)S(1)}, bf16[256,208]{1,0:T(8,128)(2,1)S(1)}, bf16[256,208]{1,0:T(8,128)(2,1)S(1)}, bf16[256,208]{1,0:T(8,128)(2,1)S(1)}, bf16[150,2400]{1,0:T(8,128)(2,1)S(1)}) custom-call(), custom_call_target="tpu_custom_call" | custom-call | flops 10000000000 | bytes 1145984 | tf_op jit(solution)/shard_map/pallas_call | solution.py:25
  2.8 2.2 %collective-permute-done.refs_5_ = bf16[208,150]{1,0:T(8,128)(2,1)S(1)} collective-permute-done((bf16[208,150]{1,0:T(8,128)(2,1)}, bf16[208,150]{1,0:T(8,128)(2,1)S(1)}, u32[]{:S(2)}, u32[]{:S(2)}) %collective-permute-start) | collective-permute-done | bytes 62432 | tf_op jit(solution)/shard_map/ppermute | solution.py:204
  5.0 0.0 slice-done
  5.0 0.0 slice-done.1
  5.0 0.0 slice-done.2
  5.0 0.0 copy-done
  5.0 2.3 %shard_map.47 = (bf16[256,2400]{1,0:T(8,128)(2,1)S(1)}, bf16[256,2400]{1,0:T(8,128)(2,1)S(1)}, f32[64,512]{1,0:T(8,128)S(1)}, bf16[64,512]{1,0:T(8,128)(2,1)S(1)...) custom-call(bf16[256,208]{1,0:T(8,128)(2,1)S(1)} %get-tuple-element.26.refs_0_, ...), custom_call_target="tpu_custom_call" | custom-call | bytes 13886464 | tf_op jit(solution)/shard_map/pallas_call | solution.py:25
  7.4 2.3 %collective-permute-start.1 = (bf16[64,512]{1,0:T(8,128)(2,1)S(1)}, bf16[64,512]{1,0:T(8,128)(2,1)S(1)}, u32[]{:S(2)}, u32[]{:S(2)}) collective-permute-start(bf16[64,512]{1,0:T(8,128)(2,1)S(1)} %get-tuple-element.32), channel_id=1, source_target_pairs={{0,2},{1,3},{2,0},{3,1},{4,6},{5,7},{6,4},{7,5},{8,10},{9,11},{10,... | collective-permute-start | bytes 196616 | tf_op jit(solution)/shard_map/ppermute | solution.py:204
  9.7 1.3 %collective-permute-start.2 = (bf16[64,512]{1,0:T(8,128)(2,1)S(1)}, bf16[64,512]{1,0:T(8,128)(2,1)S(1)}, u32[]{:S(2)}, u32[]{:S(2)}) collective-permute-start(bf16[64,512]{1,0:T(8,128)(2,1)S(1)} %get-tuple-element.33), channel_id=1, source_target_pairs={{0,1},{1,2},{2,3},{3,0},{4,5},{5,6},{6,7},{7,4},{8,9},{9,10},{10,1... | collective-permute-start | bytes 196616 | tf_op jit(solution)/shard_map/ppermute | solution.py:204
  11.0 2.0 %collective-permute-start.3 = (bf16[64,512]{1,0:T(8,128)(2,1)S(1)}, bf16[64,512]{1,0:T(8,128)(2,1)S(1)}, u32[]{:S(2)}, u32[]{:S(2)}) collective-permute-start(bf16[64,512]{1,0:T(8,128)(2,1)S(1)} %get-tuple-element.34), channel_id=1, source_target_pairs={{0,3},{1,0},{2,1},{3,2},{4,7},{5,4},{6,5},{7,6},{8,11},{9,8},{10,9... | collective-permute-start | bytes 196616 | tf_op jit(solution)/shard_map/ppermute | solution.py:204
  13.0 0.0 copy-start.2
  13.0 0.0 copy-start.1
  13.0 1.5 %shard_map.51 = (f32[64,512]{1,0:T(8,128)S(1)}, bf16[64,512]{1,0:T(8,128)(2,1)S(1)}, bf16[64,512]{1,0:T(8,128)(2,1)S(1)}, bf16[64,512]{1,0:T(8,128)(2,1)S(1)}) custom-call(bf16[256,2400]{1,0:T(8,128)(2,1)S(1)} %get-tuple-element.39.lhs_re, bf16[256,2400]{1,0:T(8,128)(2,1)S(1)} %get-tuple-element.40.lhs_im, bf16[4800,1024]{1,0:T(8,128)(2,1)S(1)} %bitcast.11), custom_call_target="tpu_custom_call" | custom-call | bytes 12615680 | tf_op jit(solution)/shard_map/pallas_call | solution.py:25
  14.5 0.1 collective-permute-start.7
  14.6 0.3 collective-permute-start.8
  14.9 0.0 collective-permute-done.1.refs_2_
  14.9 3.0 %collective-permute-start.9 = (bf16[64,512]{1,0:T(8,128)(2,1)S(1)}, bf16[64,512]{1,0:T(8,128)(2,1)S(1)}, u32[]{:S(2)}, u32[]{:S(2)}) collective-permute-start(bf16[64,512]{1,0:T(8,128)(2,1)S(1)} %get-tuple-element.44), channel_id=1, source_target_pairs={{0,3},{1,0},{2,1},{3,2},{4,7},{5,4},{6,5},{7,6},{8,11},{9,8},{10,9... | collective-permute-start | bytes 196616 | tf_op jit(solution)/shard_map/ppermute | solution.py:204
  17.9 0.0 copy-done.2
  17.9 0.4 %shard_map.48.refs_0_ = f32[112,64]{1,0:T(8,128)S(1)} custom-call(f32[1,16]{1,0:T(1,128)S(1)} %bitcast.16, f32[64,512]{1,0:T(8,128)S(1)} %get-tuple-element.31.after.refs_1_), custom_call_target="tpu_custom_call" | custom-call | bytes 159808 | tf_op jit(solution)/shard_map/pallas_call | solution.py:25
  18.3 0.0 collective-permute-done.2.refs_3_
  18.3 0.0 collective-permute-done.3.refs_4_
  18.3 0.4 %shard_map.49 = (f32[56,512]{1,0:T(8,128)S(1)}, bf16[56,512]{1,0:T(8,128)(2,1)S(1)}) custom-call(f32[112,64]{1,0:T(8,128)S(1)} %shard_map.48.refs_0_, f32[64,512]{1,0:T(8,128)S(1)} %get-tuple-element.31.after.refs_1_, bf16[64,512]{1,0:T(8,128)(2,1)S(1)} %collective-permute-done.1.refs_2_, bf16[64,512]{1,0:T(8,128)(2,1)S(1)} %collective-permute-done.2.refs_3_, ...), custom_call_target="tpu_custom_call" | custom-call | bytes 528384 | tf_op jit(solution)/shard_map/pallas_call | solution.py:25
  18.7 1.3 %collective-permute-start.4 = (bf16[56,512]{1,0:T(8,128)(2,1)S(1)}, bf16[56,512]{1,0:T(8,128)(2,1)S(1)}, u32[]{:S(2)}, u32[]{:S(2)}) collective-permute-start(bf16[56,512]{1,0:T(8,128)(2,1)S(1)} %get-tuple-element.36), channel_id=1, source_target_pairs={{0,16},{16,0},{1,17},{17,1},{2,18},{18,2},{3,19},{19,3},{4,20},{20... | collective-permute-start | bytes 172040 | tf_op jit(solution)/shard_map/ppermute | solution.py:204
  20.0 0.0 collective-permute-done.7.refs_2_
  20.0 0.0 collective-permute-done.8.refs_3_
  20.0 0.2 collective-permute-done.9.refs_4_
  20.1 0.4 %shard_map.52 = (f32[56,512]{1,0:T(8,128)S(1)}, bf16[56,512]{1,0:T(8,128)(2,1)S(1)}) custom-call(f32[112,64]{1,0:T(8,128)S(1)} %shard_map.48.refs_0_, f32[64,512]{1,0:T(8,128)S(1)} %get-tuple-element.41.refs_1_, bf16[64,512]{1,0:T(8,128)(2,1)S(1)} %collective-permute-done.7.refs_2_, bf16[64,512]{1,0:T(8,128)(2,1)S(1)} %collective-permute-done.8.refs_3_, ...), custom_call_target="tpu_custom_call" | custom-call | bytes 528384 | tf_op jit(solution)/shard_map/pallas_call | solution.py:25
  20.5 1.3 %collective-permute-start.10 = (bf16[56,512]{1,0:T(8,128)(2,1)S(1)}, bf16[56,512]{1,0:T(8,128)(2,1)S(1)}, u32[]{:S(2)}, u32[]{:S(2)}) collective-permute-start(bf16[56,512]{1,0:T(8,128)(2,1)S(1)} %get-tuple-element.46), channel_id=1, source_target_pairs={{0,16},{16,0},{1,17},{17,1},{2,18},{18,2},{3,19},{19,3},{4,20},{20... | collective-permute-start | bytes 172040 | tf_op jit(solution)/shard_map/ppermute | solution.py:204
  21.8 0.3 collective-permute-done.4.refs_1_
  22.1 0.0 copy-done.1
  22.1 3.9 %collective-permute-start.5 = (f32[56,128]{1,0:T(8,128)S(1)}, f32[56,128]{1,0:T(8,128)S(1)}, u32[]{:S(2)}, u32[]{:S(2)}) collective-permute-start(f32[56,128]{1,0:T(8,128)S(1)} %get-tuple-element.37), channel_id=1, source_target_pairs={{0,4},{8,12},{4,0},{12,8},{1,5},{9,13},{5,1},{13,9},{2,6},{10,14},... | collective-permute-start | bytes 86024 | tf_op jit(solution)/shard_map/ppermute | solution.py:253
  25.9 1.2 %collective-permute-start.6 = (f32[56,128]{1,0:T(8,128)S(1)}, f32[56,128]{1,0:T(8,128)S(1)}, u32[]{:S(2)}, u32[]{:S(2)}) collective-permute-start(f32[56,128]{1,0:T(8,128)S(1)} %get-tuple-element.38), channel_id=1, source_target_pairs={{4,8},{12,0},{8,4},{0,12},{5,9},{13,1},{9,5},{1,13},{6,10},{14,2},... | collective-permute-start | bytes 86024 | tf_op jit(solution)/shard_map/ppermute | solution.py:253
  27.1 0.0 collective-permute-done.10.refs_3_
  27.2 0.0 collective-permute-done.5.within
  27.2 2.1 %collective-permute-done.6.across = f32[56,128]{1,0:T(8,128)S(1)} collective-permute-done((f32[56,128]{1,0:T(8,128)S(1)}, f32[56,128]{1,0:T(8,128)S(1)}, u32[]{:S(2)}, u32[]{:S(2)}) %collective-permute-start.6) | collective-permute-done | bytes 28704 | tf_op jit(solution)/shard_map/ppermute | solution.py:253
  29.2 0.9 %shard_map.53 = f32[26,2,1024]{2,1,0:T(2,128)} custom-call(f32[1,1024]{1,0:T(1,128)S(1)} %bitcast.15, f32[56,128]{1,0:T(8,128)S(1)} %collective-permute-done.5.within, f32[56,128]{1,0:T(8,128)S(1)} %collective-permute-done.6.across, f32[56,512]{1,0:T(8,128)S(1)} %get-tuple-element.35.refs_0_, bf16[56,512]{1,0:T(8,128)(2,1)S(1)} %collective-permute-done.4.refs_1_, ...), custom_call_target="tpu_custom_call" | custom-call | bytes 618496 | tf_op jit(solution)/shard_map/pallas_call | solution.py:25
  (2 shorter events, 0.0 us)
Async XLA Ops:
  0.0 5.0 %slice-start = ((s8[9830400]{0:T(1024)(128)(4,1)}), s8[4194304]{0:T(1024)(128)(4,1)S(1)}, s32[]{:S(2)}) async-start(s8[9830400]{0:T(1024)(128)(4,1)} %bitcast.8), calls=%async_computation | async-start | bytes 8388608
  0.0 5.0 %slice-start.1 = ((s8[9830400]{0:T(1024)(128)(4,1)}), s8[4194304]{0:T(1024)(128)(4,1)S(1)}, s32[]{:S(2)}) async-start(s8[9830400]{0:T(1024)(128)(4,1)} %bitcast.8), calls=%async_computation.1 | async-start | bytes 8388608
  0.0 5.0 %slice-start.2 = ((s8[9830400]{0:T(1024)(128)(4,1)}), s8[1441792]{0:T(1024)(128)(4,1)S(1)}, s32[]{:S(2)}) async-start(s8[9830400]{0:T(1024)(128)(4,1)} %bitcast.8), calls=%async_computation.2 | async-start | bytes 2883584
  0.0 5.0 %copy-start = (bf16[8,150,26]{1,0,2:T(8,128)(2,1)S(1)}, bf16[8,150,26]{1,0,2:T(8,128)(2,1)}, u32[]{:S(2)}) copy-start(bf16[8,150,26]{1,0,2:T(8,128)(2,1)} %param.4) | copy-start | bytes 187204
  0.0 5.0 %collective-permute-start = (bf16[208,150]{1,0:T(8,128)(2,1)}, bf16[208,150]{1,0:T(8,128)(2,1)S(1)}, u32[]{:S(2)}, u32[]{:S(2)}) collective-permute-start(bf16[208,150]{1,0:T(8,128)(2,1)} %bitcast.12), channel_id=1, source_target_pairs={{0,16},{16,0},{1,17},{17,1},{2,18},{18,2},{3,19},{19,3},{4,20},{20... | collective-permute-start | bytes 187208 | tf_op jit(solution)/shard_map/ppermute | solution.py:204
  7.4 7.5 %collective-permute-start.1 = (bf16[64,512]{1,0:T(8,128)(2,1)S(1)}, bf16[64,512]{1,0:T(8,128)(2,1)S(1)}, u32[]{:S(2)}, u32[]{:S(2)}) collective-permute-start(bf16[64,512]{1,0:T(8,128)(2,1)S(1)} %get-tuple-element.32), channel_id=1, source_target_pairs={{0,2},{1,3},{2,0},{3,1},{4,6},{5,7},{6,4},{7,5},{8,10},{9,11},{10,... | collective-permute-start | bytes 196616 | tf_op jit(solution)/shard_map/ppermute | solution.py:204
  9.7 8.6 %collective-permute-start.2 = (bf16[64,512]{1,0:T(8,128)(2,1)S(1)}, bf16[64,512]{1,0:T(8,128)(2,1)S(1)}, u32[]{:S(2)}, u32[]{:S(2)}) collective-permute-start(bf16[64,512]{1,0:T(8,128)(2,1)S(1)} %get-tuple-element.33), channel_id=1, source_target_pairs={{0,1},{1,2},{2,3},{3,0},{4,5},{5,6},{6,7},{7,4},{8,9},{9,10},{10,1... | collective-permute-start | bytes 196616 | tf_op jit(solution)/shard_map/ppermute | solution.py:204
  11.0 7.3 %collective-permute-start.3 = (bf16[64,512]{1,0:T(8,128)(2,1)S(1)}, bf16[64,512]{1,0:T(8,128)(2,1)S(1)}, u32[]{:S(2)}, u32[]{:S(2)}) collective-permute-start(bf16[64,512]{1,0:T(8,128)(2,1)S(1)} %get-tuple-element.34), channel_id=1, source_target_pairs={{0,3},{1,0},{2,1},{3,2},{4,7},{5,4},{6,5},{7,6},{8,11},{9,8},{10,9... | collective-permute-start | bytes 196616 | tf_op jit(solution)/shard_map/ppermute | solution.py:204
  13.0 4.9 %copy-start.2 = (f32[16]{0:T(128)S(1)}, f32[16]{0:T(128)}, u32[]{:S(2)}) copy-start(f32[16]{0:T(128)} %param.6) | copy-start | bytes 196
  13.0 9.1 %copy-start.1 = (f32[1024]{0:T(1024)S(1)}, f32[1024]{0:T(1024)}, u32[]{:S(2)}) copy-start(f32[1024]{0:T(1024)} %param.7) | copy-start | bytes 12292
  14.5 5.4 %collective-permute-start.7 = (bf16[64,512]{1,0:T(8,128)(2,1)S(1)}, bf16[64,512]{1,0:T(8,128)(2,1)S(1)}, u32[]{:S(2)}, u32[]{:S(2)}) collective-permute-start(bf16[64,512]{1,0:T(8,128)(2,1)S(1)} %get-tuple-element.42), channel_id=1, source_target_pairs={{0,2},{1,3},{2,0},{3,1},{4,6},{5,7},{6,4},{7,5},{8,10},{9,11},{10,... | collective-permute-start | bytes 196616 | tf_op jit(solution)/shard_map/ppermute | solution.py:204
  14.6 5.4 %collective-permute-start.8 = (bf16[64,512]{1,0:T(8,128)(2,1)S(1)}, bf16[64,512]{1,0:T(8,128)(2,1)S(1)}, u32[]{:S(2)}, u32[]{:S(2)}) collective-permute-start(bf16[64,512]{1,0:T(8,128)(2,1)S(1)} %get-tuple-element.43), channel_id=1, source_target_pairs={{0,1},{1,2},{2,3},{3,0},{4,5},{5,6},{6,7},{7,4},{8,9},{9,10},{10,1... | collective-permute-start | bytes 196616 | tf_op jit(solution)/shard_map/ppermute | solution.py:204
  14.9 5.3 %collective-permute-start.9 = (bf16[64,512]{1,0:T(8,128)(2,1)S(1)}, bf16[64,512]{1,0:T(8,128)(2,1)S(1)}, u32[]{:S(2)}, u32[]{:S(2)}) collective-permute-start(bf16[64,512]{1,0:T(8,128)(2,1)S(1)} %get-tuple-element.44), channel_id=1, source_target_pairs={{0,3},{1,0},{2,1},{3,2},{4,7},{5,4},{6,5},{7,6},{8,11},{9,8},{10,9... | collective-permute-start | bytes 196616 | tf_op jit(solution)/shard_map/ppermute | solution.py:204
  18.7 3.4 %collective-permute-start.4 = (bf16[56,512]{1,0:T(8,128)(2,1)S(1)}, bf16[56,512]{1,0:T(8,128)(2,1)S(1)}, u32[]{:S(2)}, u32[]{:S(2)}) collective-permute-start(bf16[56,512]{1,0:T(8,128)(2,1)S(1)} %get-tuple-element.36), channel_id=1, source_target_pairs={{0,16},{16,0},{1,17},{17,1},{2,18},{18,2},{3,19},{19,3},{4,20},{20... | collective-permute-start | bytes 172040 | tf_op jit(solution)/shard_map/ppermute | solution.py:204
  20.5 6.7 %collective-permute-start.10 = (bf16[56,512]{1,0:T(8,128)(2,1)S(1)}, bf16[56,512]{1,0:T(8,128)(2,1)S(1)}, u32[]{:S(2)}, u32[]{:S(2)}) collective-permute-start(bf16[56,512]{1,0:T(8,128)(2,1)S(1)} %get-tuple-element.46), channel_id=1, source_target_pairs={{0,16},{16,0},{1,17},{17,1},{2,18},{18,2},{3,19},{19,3},{4,20},{20... | collective-permute-start | bytes 172040 | tf_op jit(solution)/shard_map/ppermute | solution.py:204
  22.1 5.1 %collective-permute-start.5 = (f32[56,128]{1,0:T(8,128)S(1)}, f32[56,128]{1,0:T(8,128)S(1)}, u32[]{:S(2)}, u32[]{:S(2)}) collective-permute-start(f32[56,128]{1,0:T(8,128)S(1)} %get-tuple-element.37), channel_id=1, source_target_pairs={{0,4},{8,12},{4,0},{12,8},{1,5},{9,13},{5,1},{13,9},{2,6},{10,14},... | collective-permute-start | bytes 86024 | tf_op jit(solution)/shard_map/ppermute | solution.py:253
  25.9 3.3 %collective-permute-start.6 = (f32[56,128]{1,0:T(8,128)S(1)}, f32[56,128]{1,0:T(8,128)S(1)}, u32[]{:S(2)}, u32[]{:S(2)}) collective-permute-start(f32[56,128]{1,0:T(8,128)S(1)} %get-tuple-element.38), channel_id=1, source_target_pairs={{4,8},{12,0},{8,4},{0,12},{5,9},{13,1},{9,5},{1,13},{6,10},{14,2},... | collective-permute-start | bytes 86024 | tf_op jit(solution)/shard_map/ppermute | solution.py:253

commit v6 on v5

--- a/solution.py
+++ b/solution.py
@@ -44,8 +44,16 @@
     return lax.broadcasted_iota(jnp.int32, shape, dim)
 
 
-def onehot(shape, hit):
-    return jnp.where(hit, jnp.ones(shape, F32), jnp.zeros(shape, F32)).astype(BF)
+def rows_of(count):
+    return iota((count, 1), 0)
+
+
+def cols_of(count):
+    return iota((1, count), 1)
+
+
+def onehot(hit):
+    return jnp.where(hit, 1.0, 0.0).astype(BF)
 
 
 def dot(a, b, precision=None):
@@ -61,57 +69,62 @@
     bins, times, probes, group, freqs, senss = dims
     freq, sens = lax.axis_index("freq"), lax.axis_index("sens")
     tables, spread = refs[: 2 * freqs], refs[2 * freqs]
-    small = (2 * bins, times)
-    part, bin_at = split_index(iota(small, 0), (2, bins))
-    tall = (senss * 2 * bins * group, 2 * bins)
-    up = onehot(tall, iota(tall, 0) // group % (2 * bins) == iota(tall, 1))
-    flat = (times, times * probes)
-    out = onehot(flat, iota(flat, 1) // probes == iota(flat, 0))
-    full = (tall[0], flat[1])
-    shift = iota(full, 0) // (2 * bins * group)
-    probe = (sens + shift) % senss * group + iota(full, 0) % group
-    hit = iota(full, 1) % probes == probe
+    part, bin_at = split_index(rows_of(2 * bins), (2, bins))
+    tall, wide = senss * 2 * bins * group, times * probes
+    up = onehot(rows_of(tall) // group % (2 * bins) == cols_of(2 * bins))
+    out = onehot(cols_of(wide) // probes == rows_of(times))
+    shift = rows_of(tall) // (2 * bins * group)
+    probe = (sens + shift) % senss * group + rows_of(tall) % group
+    hit = cols_of(wide) % probes == probe
     for j in range(freqs):
-        time = iota(small, 1) + (freq + j) % freqs * times
+        time = cols_of(times) + (freq + j) % freqs * times
         value = wave((freq * bins + bin_at) * time, part) * (1.0 / math.sqrt(times * freqs))
         high = value.astype(BF)
         low = (value - high.astype(F32)).astype(BF)
         for i, piece in enumerate((high, low)):
-            wide = dot(dot(up, piece).astype(BF), out)
-            tables[2 * j + i][...] = jnp.where(hit, wide, 0.0).astype(BF)
-    spread[...] = onehot(spread.shape, iota(spread.shape, 1) // bins == iota(spread.shape, 0))
-
-
-def inverse_body(dims, weights, after, inverse):
+            spaced = dot(dot(up, piece).astype(BF), out)
+            tables[2 * j + i][...] = jnp.where(hit, spaced, 0.0).astype(BF)
+    spread[...] = onehot(cols_of(spread.shape[1]) // bins == rows_of(spread.shape[0]))
+
+
+def inverse_body(dims, weights, high, low):
     bins, times, group, freqs, rows = dims
     freq = lax.axis_index("freq")
-    shape = inverse.shape
-    shift, row = split_index(iota(shape, 0), (freqs, rows))
-    part, bin_at, inner = split_index(iota(shape, 1), (2, bins, group))
+    shift, row = split_index(rows_of(freqs * rows), (freqs, rows))
+    part, bin_at, inner = split_index(cols_of(2 * bins * group), (2, bins, group))
     time = row // group + (freq + shift) % freqs * times
     value = wave((freq * bins + bin_at) * time, part)
-    pick = (bins, shape[1])
-    chosen = jnp.where(iota(pick, 1) // group % bins == iota(pick, 0), 1.0, 0.0)
+    chosen = jnp.where(bin_at == rows_of(bins), 1.0, 0.0)
     weight = dot(weights[...], chosen, lax.Precision.HIGHEST) * (1.0 / math.sqrt(bins * freqs))
     hit = (row % group == inner) & (row < times * group)
-    inverse[...] = jnp.where(hit, value * weight[:1], 0.0)
-
-
-def contract_body(bins, blocks, pieces, *refs):
+    value = jnp.where(hit, value * weight[:1], 0.0)
+    high[...] = value.astype(BF)
+    low[...] = (value - high[...].astype(F32)).astype(BF)
+
+
+def spectrum(tables, series, total=None):
+    for i, table in enumerate(tables):
+        term = dot(table[...], series[i // 2][...])
+        total = term if total is None else total + term
+    return total
+
+
+def own_body(high, low, series, out):
+    out[...] = spectrum((high, low), (series,))
+
+
+def contract_body(bins, blocks, pieces, own, *refs):
     tables = refs[: 2 * pieces]
     series = refs[2 * pieces : 3 * pieces]
     spread, operator = refs[3 * pieces : 3 * pieces + 2]
     lhs_re, lhs_im = refs[3 * pieces + 2 : 3 * pieces + 4]
-    spec = None
-    for i in range(2 * pieces):
-        term = dot(tables[i][...], series[i // 2][...])
-        spec = term if spec is None else spec + term
+    spec = spectrum(tables, series, own[...])
     rows = spec.shape[0]
     block = rows // blocks
     half = block // 2
     group = half // bins
     wide = dot(spec.astype(BF), spread[...])
-    keep = iota(wide.shape, 0) // group % bins == iota(wide.shape, 1) % bins
+    keep = rows_of(rows) // group % bins == cols_of(wide.shape[1]) % bins
     wide = jnp.where(keep, wide, 0.0).astype(BF)
     lhs_re[...] = wide
     for i in range(blocks):
@@ -143,33 +156,37 @@
         out[...] = total[i * block : (i + 1) * block].astype(out.dtype)
 
 
-def image_body(rows, *refs):
-    table, own = refs[:2]
-    count = table.shape[0] // rows
+def image_body(rows, high, low, own, *refs):
+    count = high.shape[0] // rows
     outs = refs[len(refs) - count :]
     total = own[...]
-    for other in refs[2 : len(refs) - count]:
+    for other in refs[: len(refs) - count]:
         total = total + other[...].astype(F32)
-    image = dot(table[...], total, lax.Precision.HIGHEST)
+    upper = total.astype(BF)
+    lower = (total - upper.astype(F32)).astype(BF)
+    image = dot(high[...], upper) + (dot(high[...], lower) + dot(low[...], upper))
     for i, out in enumerate(outs):
         out[...] = image[i * rows : (i + 1) * rows].astype(out.dtype)
 
 
-def edge_body(lanes, scale, *refs):
+def edge_body(scale, *refs):
     within, across = refs[-2:]
     cols, width = scale.shape[1], refs[0].shape[1]
-
-    def scaled(at, scale_at):
+    count = refs[0].shape[0]
+    eye = rows_of(count) == cols_of(within.shape[1])
+
+    def column(at, scale_at):
         total = None
         for ref in refs[:-2]:
-            term = ref[:, at : at + lanes].astype(F32)
+            term = ref[:, at : at + 1].astype(F32)
             total = term if total is None else total + term
-        return total * scale[:, scale_at : scale_at + lanes]
-
-    first, last = scaled(0, 0), scaled(width - lanes, cols - lanes)
+        total = total * scale[:, scale_at : scale_at + 1]
+        return jnp.sum(jnp.where(eye, total, 0.0), axis=0, keepdims=True)
+
+    first, last = column(0, 0), column(width - 1, cols - 1)
     even = lax.axis_index("param") % 2 == 0
-    within[...] = jnp.where(even, last, first)
-    across[...] = jnp.where(even, first, last)
+    within[...] = jnp.broadcast_to(jnp.where(even, last, first), within.shape)
+    across[...] = jnp.broadcast_to(jnp.where(even, first, last), across.shape)
 
 
 def smooth_body(count, scale, within, across, *refs):
@@ -186,13 +203,16 @@
     edge = outer.shape[1] // 2
     value = jnp.concatenate([outer[:, :edge], inner, outer[:, edge:]], axis=1)
     value = value * scale[...]
-    lane = iota(value.shape, 1)
-    width = within.shape[1]
+    lane = cols_of(cols)
     at, ends = lax.axis_index("param"), lax.axis_size("param") - 1
+    eye = rows_of(value.shape[0]) == cols_of(within.shape[1])
+    within, across = within[:1], across[:1]
     even = at % 2 == 0
-    before = jnp.where(even, across[:, width - 1 :], within[:, width - 1 :])
-    after = jnp.where(even, within[:, :1], across[:, :1])
-    before, after = jnp.where(at > 0, before, 0.0), jnp.where(at < ends, after, 0.0)
+    before = jnp.where(even & (at > 0), across, jnp.where(even, 0.0, within))
+    after = jnp.where(even, within, jnp.where(at < ends, across, 0.0))
+    before, after = (
+        jnp.sum(jnp.where(eye, row, 0.0), axis=1, keepdims=True) for row in (before, after)
+    )
     left = jnp.where(lane == 0, before, pltpu.roll(value, 1, 1))
     right = jnp.where(lane == cols - 1, after, pltpu.roll(value, cols - 1, 1))
     value = (0.5 * value + 0.25 * (left + right)) * scale[...]
@@ -223,31 +243,30 @@
     operator = kernel.transpose(0, 2, 1, 3).reshape(2 * sens_dev * bins, cols)
     edge = cols * OUTER // 16
     blocks = lambda width: [shape((block, width), BF if i else F32) for i in range(senss)]
+    own = call(own_body, shape((senss * block, sens_dev), F32), *tables[:2], own_series)
     lhs_re, lhs_im, *outer = call(
-        functools.partial(contract_body, bins, senss, freqs),
+        functools.partial(contract_body, bins, senss, freqs - 1),
         [shape((senss * block, sens_dev * bins), BF)] * 2 + blocks(2 * edge),
-        *tables, *pieces, spread, operator,
+        own, *tables[2:], *pieces[1:], spread, operator,
     )
     inner = call(inner_body, blocks(cols - 2 * edge), lhs_re, lhs_im, operator)
     inverse = call(
         functools.partial(inverse_body, (bins, times, group, freqs, rows)),
-        shape((freqs * rows, block), F32),
-        prior_spectrum.reshape(1, bins), outer[0],
+        [shape((freqs * rows, block), BF)] * 2,
+        prior_spectrum.reshape(1, bins),
     )
     order = sorted(range(1, senss), key=lambda d: -min(d, senss - d))
     outer = [outer[0]] + [rotate(outer[d], "sens", d) for d in order]
     inner = [inner[0]] + [rotate(inner[d], "sens", d) for d in order]
     images = lambda width: [shape((rows, width), BF if i else F32) for i in range(freqs)]
     as_image = functools.partial(image_body, rows)
-    outer = call(as_image, images(2 * edge), inverse, *outer)
+    outer = call(as_image, images(2 * edge), *inverse, *outer)
     outer = [outer[0]] + [rotate(outer[j], "freq", j) for j in range(1, freqs)]
-    inner = call(as_image, images(cols - 2 * edge), inverse, *inner)
+    inner = call(as_image, images(cols - 2 * edge), *inverse, *inner)
     inner = [inner[0]] + [rotate(inner[j], "freq", j) for j in range(1, freqs)]
     scale = prior_scale.reshape(1, cols)
-    lanes = min(128, edge)
-    swaps = list(call(
-        functools.partial(edge_body, lanes), [shape((rows, lanes), F32)] * 2, scale, *outer)
-    )
+    row = shape((8, -(-rows // 128) * 128), F32)
+    swaps = list(call(edge_body, [row] * 2, scale, *outer))
     for i in (0, 1):
         pairs = [(a, (a + 1) % params) for a in range(i, params // 2 * 2, 2)]
         swaps[i] = lax.ppermute(swaps[i], "param", pairs + [(b, a) for a, b in pairs])

time: 30.4 us -> 29.9 us (0.984)
  waiting for transfers between devices: 4.72 us -> 4.33 us
    pallas_call x8 -> x9, Pallas kernels: 6.55 us -> 6.47 us  [call(): pl.pallas_call(body, in_specs=[vmem()] * len(args), out_specs=jax.tree.ma...]
where the time goes in v6:
time: 29.9 us; the launch traced here: 29.7 us
  starting transfers between devices  18.7 us (63%)
  Pallas kernels  6.47 us (22%)
  waiting for transfers between devices  4.33 us (14%)
    ppermute x9, starting transfers between devices, rotate(): lax.ppermute(value, axis, [(i, (i + shift) % size) for i in range(size)])  13.7 us
    pallas_call x9, Pallas kernels, call(): pl.pallas_call(body, in_specs=[vmem()] * len(args), out_specs=jax.tree.ma...  6.47 us
    ppermute x2, starting transfers between devices, steps(): lax.ppermute(swaps[i], 'param', pairs + [(b, a) for a, b in pairs])  5.05 us
    ppermute x9, waiting for transfers between devices, rotate(): lax.ppermute(value, axis, [(i, (i + shift) % size) for i in range(size)])  2.5 us
    ppermute x2, waiting for transfers between devices, steps(): lax.ppermute(swaps[i], 'param', pairs + [(b, a) for a, b in pairs])  1.82 us
  transfers between devices with their start and end apart: 11, of which 4 were waited for; matrix products, arithmetic and copies ran while one was open for 0% of the time, Pallas kernels for 11%

profile of v6, /device:TPU:1, one launch (start us, length us, event | category | flops | bytes accessed | tf_op | source)
XLA Modules:
  0.0 29.7 jit_solution(12310452876571081380)
XLA Ops:
  0.0 0.0 slice-start
  0.0 0.0 copy-start
  0.0 0.0 slice-start.1
  0.0 0.0 slice-start.2
  0.0 2.1 %collective-permute-start = (bf16[208,150]{1,0:T(8,128)(2,1)}, bf16[208,150]{1,0:T(8,128)(2,1)S(1)}, u32[]{:S(2)}, u32[]{:S(2)}) collective-permute-start(bf16[208,150]{1,0:T(8,128)(2,1)} %bitcast.12), channel_id=1, source_target_pairs={{0,16},{16,0},{1,17},{17,1},{2,18},{18,2},{3,19},{19,3},{4,20},{20... | collective-permute-start | bytes 187208 | tf_op jit(solution)/shard_map/ppermute | solution.py:224
  2.1 0.7 %shard_map.47 = (bf16[256,208]{1,0:T(8,128)(2,1)S(1)}, bf16[256,208]{1,0:T(8,128)(2,1)S(1)}, bf16[256,208]{1,0:T(8,128)(2,1)S(1)}, bf16[256,208]{1,0:T(8,128)(2,1)S(1)}, bf16[150,2400]{1,0:T(8,128)(2,1)S(1)}) custom-call(), custom_call_target="tpu_custom_call" | custom-call | flops 10000000000 | bytes 1145984 | tf_op jit(solution)/shard_map/pallas_call | solution.py:25
  2.8 0.0 copy-done
  2.8 0.2 shard_map.48.own
  3.0 2.0 %collective-permute-done.refs_2_ = bf16[208,150]{1,0:T(8,128)(2,1)S(1)} collective-permute-done((bf16[208,150]{1,0:T(8,128)(2,1)}, bf16[208,150]{1,0:T(8,128)(2,1)S(1)}, u32[]{:S(2)}, u32[]{:S(2)}) %collective-permute-start) | collective-permute-done | bytes 62432 | tf_op jit(solution)/shard_map/ppermute | solution.py:224
  5.0 0.0 slice-done
  5.0 0.0 slice-done.1
  5.0 0.0 slice-done.2
  5.0 2.2 %shard_map.49 = (bf16[256,2400]{1,0:T(8,128)(2,1)S(1)}, bf16[256,2400]{1,0:T(8,128)(2,1)S(1)}, f32[64,512]{1,0:T(8,128)S(1)}, bf16[64,512]{1,0:T(8,128)(2,1)S(1)...) custom-call(f32[256,150]{1,0:T(8,128)S(1)} %shard_map.48.own, ...), custom_call_target="tpu_custom_call" | custom-call | bytes 13764672 | tf_op jit(solution)/shard_map/pallas_call | solution.py:25
  7.2 2.3 %collective-permute-start.1 = (bf16[64,512]{1,0:T(8,128)(2,1)S(1)}, bf16[64,512]{1,0:T(8,128)(2,1)S(1)}, u32[]{:S(2)}, u32[]{:S(2)}) collective-permute-start(bf16[64,512]{1,0:T(8,128)(2,1)S(1)} %get-tuple-element.36), channel_id=1, source_target_pairs={{0,2},{1,3},{2,0},{3,1},{4,6},{5,7},{6,4},{7,5},{8,10},{9,11},{10,... | collective-permute-start | bytes 196616 | tf_op jit(solution)/shard_map/ppermute | solution.py:224
  9.5 1.3 %collective-permute-start.2 = (bf16[64,512]{1,0:T(8,128)(2,1)S(1)}, bf16[64,512]{1,0:T(8,128)(2,1)S(1)}, u32[]{:S(2)}, u32[]{:S(2)}) collective-permute-start(bf16[64,512]{1,0:T(8,128)(2,1)S(1)} %get-tuple-element.37), channel_id=1, source_target_pairs={{0,1},{1,2},{2,3},{3,0},{4,5},{5,6},{6,7},{7,4},{8,9},{9,10},{10,1... | collective-permute-start | bytes 196616 | tf_op jit(solution)/shard_map/ppermute | solution.py:224
  10.8 2.0 %collective-permute-start.3 = (bf16[64,512]{1,0:T(8,128)(2,1)S(1)}, bf16[64,512]{1,0:T(8,128)(2,1)S(1)}, u32[]{:S(2)}, u32[]{:S(2)}) collective-permute-start(bf16[64,512]{1,0:T(8,128)(2,1)S(1)} %get-tuple-element.38), channel_id=1, source_target_pairs={{0,3},{1,0},{2,1},{3,2},{4,7},{5,4},{6,5},{7,6},{8,11},{9,8},{10,9... | collective-permute-start | bytes 196616 | tf_op jit(solution)/shard_map/ppermute | solution.py:224
  12.8 0.0 copy-start.2
  12.8 0.0 copy-start.1
  12.8 1.5 %shard_map.52 = (f32[64,512]{1,0:T(8,128)S(1)}, bf16[64,512]{1,0:T(8,128)(2,1)S(1)}, bf16[64,512]{1,0:T(8,128)(2,1)S(1)}, bf16[64,512]{1,0:T(8,128)(2,1)S(1)}) custom-call(bf16[256,2400]{1,0:T(8,128)(2,1)S(1)} %get-tuple-element.43.lhs_re, bf16[256,2400]{1,0:T(8,128)(2,1)S(1)} %get-tuple-element.44.lhs_im, bf16[4800,1024]{1,0:T(8,128)(2,1)S(1)} %bitcast.11), custom_call_target="tpu_custom_call" | custom-call | bytes 12615680 | tf_op jit(solution)/shard_map/pallas_call | solution.py:25
  14.3 0.1 collective-permute-start.7
  14.4 0.3 collective-permute-start.8
  14.7 0.0 collective-permute-done.1.refs_0_
  14.7 3.0 %collective-permute-start.9 = (bf16[64,512]{1,0:T(8,128)(2,1)S(1)}, bf16[64,512]{1,0:T(8,128)(2,1)S(1)}, u32[]{:S(2)}, u32[]{:S(2)}) collective-permute-start(bf16[64,512]{1,0:T(8,128)(2,1)S(1)} %get-tuple-element.48), channel_id=1, source_target_pairs={{0,3},{1,0},{2,1},{3,2},{4,7},{5,4},{6,5},{7,6},{8,11},{9,8},{10,9... | collective-permute-start | bytes 196616 | tf_op jit(solution)/shard_map/ppermute | solution.py:224
  17.7 0.0 copy-done.2
  17.7 0.4 %shard_map.46 = (bf16[112,64]{1,0:T(8,128)(2,1)S(1)}, bf16[112,64]{1,0:T(8,128)(2,1)S(1)}) custom-call(f32[1,16]{1,0:T(1,128)S(1)} %bitcast.16), custom_call_target="tpu_custom_call" | custom-call | bytes 28736 | tf_op jit(solution)/shard_map/pallas_call | solution.py:25
  18.1 0.0 collective-permute-done.2.refs_1_
  18.1 0.0 collective-permute-done.3.refs_2_
  18.1 0.3 shard_map.50
  18.4 1.3 %collective-permute-start.4 = (bf16[56,512]{1,0:T(8,128)(2,1)S(1)}, bf16[56,512]{1,0:T(8,128)(2,1)S(1)}, u32[]{:S(2)}, u32[]{:S(2)}) collective-permute-start(bf16[56,512]{1,0:T(8,128)(2,1)S(1)} %get-tuple-element.40), channel_id=1, source_target_pairs={{0,16},{16,0},{1,17},{17,1},{2,18},{18,2},{3,19},{19,3},{4,20},{20... | collective-permute-start | bytes 172040 | tf_op jit(solution)/shard_map/ppermute | solution.py:224
  19.7 0.0 collective-permute-done.7.refs_0_
  19.7 0.0 collective-permute-done.8.refs_1_
  19.7 0.3 collective-permute-done.9.refs_2_
  19.9 0.3 shard_map.53
  20.2 1.3 %collective-permute-start.10 = (bf16[56,512]{1,0:T(8,128)(2,1)S(1)}, bf16[56,512]{1,0:T(8,128)(2,1)S(1)}, u32[]{:S(2)}, u32[]{:S(2)}) collective-permute-start(bf16[56,512]{1,0:T(8,128)(2,1)S(1)} %get-tuple-element.50), channel_id=1, source_target_pairs={{0,16},{16,0},{1,17},{17,1},{2,18},{18,2},{3,19},{19,3},{4,20},{20... | collective-permute-start | bytes 172040 | tf_op jit(solution)/shard_map/ppermute | solution.py:224
  21.5 0.3 collective-permute-done.4.refs_1_
  21.8 0.0 copy-done.1
  21.8 0.1 shard_map.51
  21.9 3.8 %collective-permute-start.5 = (f32[8,128]{1,0:T(8,128)S(1)}, f32[8,128]{1,0:T(8,128)S(1)}, u32[]{:S(2)}, u32[]{:S(2)}) collective-permute-start(f32[8,128]{1,0:T(8,128)S(1)} %get-tuple-element.41), channel_id=1, source_target_pairs={{0,4},{8,12},{4,0},{12,8},{1,5},{9,13},{5,1},{13,9},{2,6},{10,14},... | collective-permute-start | bytes 12296 | tf_op jit(solution)/shard_map/ppermute | solution.py:272
  25.7 1.2 %collective-permute-start.6 = (f32[8,128]{1,0:T(8,128)S(1)}, f32[8,128]{1,0:T(8,128)S(1)}, u32[]{:S(2)}, u32[]{:S(2)}) collective-permute-start(f32[8,128]{1,0:T(8,128)S(1)} %get-tuple-element.42), channel_id=1, source_target_pairs={{4,8},{12,0},{8,4},{0,12},{5,9},{13,1},{9,5},{1,13},{6,10},{14,2},... | collective-permute-start | bytes 12296 | tf_op jit(solution)/shard_map/ppermute | solution.py:272
  26.9 0.0 collective-permute-done.10.refs_3_
  26.9 0.0 collective-permute-done.5.within
  26.9 1.8 %collective-permute-done.6.across = f32[8,128]{1,0:T(8,128)S(1)} collective-permute-done((f32[8,128]{1,0:T(8,128)S(1)}, f32[8,128]{1,0:T(8,128)S(1)}, u32[]{:S(2)}, u32[]{:S(2)}) %collective-permute-start.6) | collective-permute-done | bytes 4128 | tf_op jit(solution)/shard_map/ppermute | solution.py:272
  28.8 0.9 %shard_map.54 = f32[26,2,1024]{2,1,0:T(2,128)} custom-call(f32[1,1024]{1,0:T(1,128)S(1)} %bitcast.15, f32[8,128]{1,0:T(8,128)S(1)} %collective-permute-done.5.within, f32[8,128]{1,0:T(8,128)S(1)} %collective-permute-done.6.across, f32[56,512]{1,0:T(8,128)S(1)} %get-tuple-element.39.refs_0_, bf16[56,512]{1,0:T(8,128)(2,1)S(1)} %collective-permute-done.4.refs_1_, ...), custom_call_target="tpu_custom_call" | custom-call | bytes 569344 | tf_op jit(solution)/shard_map/pallas_call | solution.py:25
  (1 shorter events, 0.0 us)
Async XLA Ops:
  0.0 5.0 %slice-start = ((s8[9830400]{0:T(1024)(128)(4,1)}), s8[4194304]{0:T(1024)(128)(4,1)S(1)}, s32[]{:S(2)}) async-start(s8[9830400]{0:T(1024)(128)(4,1)} %bitcast.8), calls=%async_computation | async-start | bytes 8388608
  0.0 2.8 %copy-start = (bf16[8,150,26]{1,0,2:T(8,128)(2,1)S(1)}, bf16[8,150,26]{1,0,2:T(8,128)(2,1)}, u32[]{:S(2)}) copy-start(bf16[8,150,26]{1,0,2:T(8,128)(2,1)} %param.4) | copy-start | bytes 187204
  0.0 5.0 %slice-start.1 = ((s8[9830400]{0:T(1024)(128)(4,1)}), s8[4194304]{0:T(1024)(128)(4,1)S(1)}, s32[]{:S(2)}) async-start(s8[9830400]{0:T(1024)(128)(4,1)} %bitcast.8), calls=%async_computation.1 | async-start | bytes 8388608
  0.0 5.0 %slice-start.2 = ((s8[9830400]{0:T(1024)(128)(4,1)}), s8[1441792]{0:T(1024)(128)(4,1)S(1)}, s32[]{:S(2)}) async-start(s8[9830400]{0:T(1024)(128)(4,1)} %bitcast.8), calls=%async_computation.2 | async-start | bytes 2883584
  0.0 5.0 %collective-permute-start = (bf16[208,150]{1,0:T(8,128)(2,1)}, bf16[208,150]{1,0:T(8,128)(2,1)S(1)}, u32[]{:S(2)}, u32[]{:S(2)}) collective-permute-start(bf16[208,150]{1,0:T(8,128)(2,1)} %bitcast.12), channel_id=1, source_target_pairs={{0,16},{16,0},{1,17},{17,1},{2,18},{18,2},{3,19},{19,3},{4,20},{20... | collective-permute-start | bytes 187208 | tf_op jit(solution)/shard_map/ppermute | solution.py:224
  7.2 7.5 %collective-permute-start.1 = (bf16[64,512]{1,0:T(8,128)(2,1)S(1)}, bf16[64,512]{1,0:T(8,128)(2,1)S(1)}, u32[]{:S(2)}, u32[]{:S(2)}) collective-permute-start(bf16[64,512]{1,0:T(8,128)(2,1)S(1)} %get-tuple-element.36), channel_id=1, source_target_pairs={{0,2},{1,3},{2,0},{3,1},{4,6},{5,7},{6,4},{7,5},{8,10},{9,11},{10,... | collective-permute-start | bytes 196616 | tf_op jit(solution)/shard_map/ppermute | solution.py:224
  9.5 8.6 %collective-permute-start.2 = (bf16[64,512]{1,0:T(8,128)(2,1)S(1)}, bf16[64,512]{1,0:T(8,128)(2,1)S(1)}, u32[]{:S(2)}, u32[]{:S(2)}) collective-permute-start(bf16[64,512]{1,0:T(8,128)(2,1)S(1)} %get-tuple-element.37), channel_id=1, source_target_pairs={{0,1},{1,2},{2,3},{3,0},{4,5},{5,6},{6,7},{7,4},{8,9},{9,10},{10,1... | collective-permute-start | bytes 196616 | tf_op jit(solution)/shard_map/ppermute | solution.py:224
  10.8 7.3 %collective-permute-start.3 = (bf16[64,512]{1,0:T(8,128)(2,1)S(1)}, bf16[64,512]{1,0:T(8,128)(2,1)S(1)}, u32[]{:S(2)}, u32[]{:S(2)}) collective-permute-start(bf16[64,512]{1,0:T(8,128)(2,1)S(1)} %get-tuple-element.38), channel_id=1, source_target_pairs={{0,3},{1,0},{2,1},{3,2},{4,7},{5,4},{6,5},{7,6},{8,11},{9,8},{10,9... | collective-permute-start | bytes 196616 | tf_op jit(solution)/shard_map/ppermute | solution.py:224
  12.8 4.9 %copy-start.2 = (f32[16]{0:T(128)S(1)}, f32[16]{0:T(128)}, u32[]{:S(2)}) copy-start(f32[16]{0:T(128)} %param.6) | copy-start | bytes 196
  12.8 9.0 %copy-start.1 = (f32[1024]{0:T(1024)S(1)}, f32[1024]{0:T(1024)}, u32[]{:S(2)}) copy-start(f32[1024]{0:T(1024)} %param.7) | copy-start | bytes 12292
  14.3 5.4 %collective-permute-start.7 = (bf16[64,512]{1,0:T(8,128)(2,1)S(1)}, bf16[64,512]{1,0:T(8,128)(2,1)S(1)}, u32[]{:S(2)}, u32[]{:S(2)}) collective-permute-start(bf16[64,512]{1,0:T(8,128)(2,1)S(1)} %get-tuple-element.46), channel_id=1, source_target_pairs={{0,2},{1,3},{2,0},{3,1},{4,6},{5,7},{6,4},{7,5},{8,10},{9,11},{10,... | collective-permute-start | bytes 196616 | tf_op jit(solution)/shard_map/ppermute | solution.py:224
  14.4 5.3 %collective-permute-start.8 = (bf16[64,512]{1,0:T(8,128)(2,1)S(1)}, bf16[64,512]{1,0:T(8,128)(2,1)S(1)}, u32[]{:S(2)}, u32[]{:S(2)}) collective-permute-start(bf16[64,512]{1,0:T(8,128)(2,1)S(1)} %get-tuple-element.47), channel_id=1, source_target_pairs={{0,1},{1,2},{2,3},{3,0},{4,5},{5,6},{6,7},{7,4},{8,9},{9,10},{10,1... | collective-permute-start | bytes 196616 | tf_op jit(solution)/shard_map/ppermute | solution.py:224
  14.7 5.2 %collective-permute-start.9 = (bf16[64,512]{1,0:T(8,128)(2,1)S(1)}, bf16[64,512]{1,0:T(8,128)(2,1)S(1)}, u32[]{:S(2)}, u32[]{:S(2)}) collective-permute-start(bf16[64,512]{1,0:T(8,128)(2,1)S(1)} %get-tuple-element.48), channel_id=1, source_target_pairs={{0,3},{1,0},{2,1},{3,2},{4,7},{5,4},{6,5},{7,6},{8,11},{9,8},{10,9... | collective-permute-start | bytes 196616 | tf_op jit(solution)/shard_map/ppermute | solution.py:224
  18.4 3.4 %collective-permute-start.4 = (bf16[56,512]{1,0:T(8,128)(2,1)S(1)}, bf16[56,512]{1,0:T(8,128)(2,1)S(1)}, u32[]{:S(2)}, u32[]{:S(2)}) collective-permute-start(bf16[56,512]{1,0:T(8,128)(2,1)S(1)} %get-tuple-element.40), channel_id=1, source_target_pairs={{0,16},{16,0},{1,17},{17,1},{2,18},{18,2},{3,19},{19,3},{4,20},{20... | collective-permute-start | bytes 172040 | tf_op jit(solution)/shard_map/ppermute | solution.py:224
  20.2 6.8 %collective-permute-start.10 = (bf16[56,512]{1,0:T(8,128)(2,1)S(1)}, bf16[56,512]{1,0:T(8,128)(2,1)S(1)}, u32[]{:S(2)}, u32[]{:S(2)}) collective-permute-start(bf16[56,512]{1,0:T(8,128)(2,1)S(1)} %get-tuple-element.50), channel_id=1, source_target_pairs={{0,16},{16,0},{1,17},{17,1},{2,18},{18,2},{3,19},{19,3},{4,20},{20... | collective-permute-start | bytes 172040 | tf_op jit(solution)/shard_map/ppermute | solution.py:224
  21.9 5.1 %collective-permute-start.5 = (f32[8,128]{1,0:T(8,128)S(1)}, f32[8,128]{1,0:T(8,128)S(1)}, u32[]{:S(2)}, u32[]{:S(2)}) collective-permute-start(f32[8,128]{1,0:T(8,128)S(1)} %get-tuple-element.41), channel_id=1, source_target_pairs={{0,4},{8,12},{4,0},{12,8},{1,5},{9,13},{5,1},{13,9},{2,6},{10,14},... | collective-permute-start | bytes 12296 | tf_op jit(solution)/shard_map/ppermute | solution.py:272
  25.7 3.0 %collective-permute-start.6 = (f32[8,128]{1,0:T(8,128)S(1)}, f32[8,128]{1,0:T(8,128)S(1)}, u32[]{:S(2)}, u32[]{:S(2)}) collective-permute-start(f32[8,128]{1,0:T(8,128)S(1)} %get-tuple-element.42), channel_id=1, source_target_pairs={{4,8},{12,0},{8,4},{0,12},{5,9},{13,1},{9,5},{1,13},{6,10},{14,2},... | collective-permute-start | bytes 12296 | tf_op jit(solution)/shard_map/ppermute | solution.py:272

commit v7 on v6

--- a/solution.py
+++ b/solution.py
@@ -12,6 +12,7 @@
 LEN = 840
 OUTER = 4
 PREP = 10**10
+EARLY = 1
 BF = jnp.bfloat16
 F32 = jnp.float32
 
@@ -20,13 +21,14 @@
     return pl.BlockSpec(memory_space=pltpu.VMEM)
 
 
-def call(body, out_shape, *args, flops=0, limit=4 << 20):
+def call(body, out_shape, *args, flops=0, aliases={}, limit=4 << 20):
     moved = sum(a.size * a.dtype.itemsize for a in [*args, *jax.tree.leaves(out_shape)])
     return pl.pallas_call(
         body,
         in_specs=[vmem()] * len(args),
         out_specs=jax.tree.map(lambda _: vmem(), out_shape),
         out_shape=out_shape,
+        input_output_aliases=aliases,
         compiler_params=pltpu.CompilerParams(vmem_limit_bytes=limit),
         cost_estimate=pl.CostEstimate(flops=flops, transcendentals=0, bytes_accessed=moved),
     )(*args)
@@ -148,7 +150,13 @@
             out[:, at : at + edge] = total[i * block : (i + 1) * block].astype(out.dtype)
 
 
-def inner_body(lhs_re, lhs_im, operator, *outs):
+def inner_body(turn, blocks, lhs_re, lhs_im, operator, *refs):
+    @pl.when(lax.axis_index("param") % 2 == turn)
+    def _():
+        inner_product(lhs_re, lhs_im, operator, *refs[-blocks:])
+
+
+def inner_product(lhs_re, lhs_im, operator, *outs):
     width = outs[0].shape[1]
     block = lhs_re.shape[0] // len(outs)
     total = product(lhs_re, lhs_im, operator, (operator.shape[1] - width) // 2, width)
@@ -249,7 +257,14 @@
         [shape((senss * block, sens_dev * bins), BF)] * 2 + blocks(2 * edge),
         own, *tables[2:], *pieces[1:], spread, operator,
     )
-    inner = call(inner_body, blocks(cols - 2 * edge), lhs_re, lhs_im, operator)
+    factors = (lhs_re, lhs_im, operator)
+    inner = blocks(cols - 2 * edge)
+    early = call(functools.partial(inner_body, EARLY, senss), inner, *factors)
+    inner = call(
+        functools.partial(inner_body, 1 - EARLY, senss),
+        inner, *factors, *early,
+        aliases={len(factors) + i: i for i in range(senss)},
+    )
     inverse = call(
         functools.partial(inverse_body, (bins, times, group, freqs, rows)),
         [shape((freqs * rows, block), BF)] * 2,

time: 29.9 us -> 29.9 us (level)
    pallas_call x9 -> x10, Pallas kernels: 6.47 us -> 6.48 us  [call(): pl.pallas_call(body, in_specs=[vmem()] * len(args), out_specs=jax.tree.ma...]
where the time goes in v7:
time: 29.9 us; the launch traced here: 29.7 us
  starting transfers between devices  18.7 us (63%)
  Pallas kernels  6.48 us (22%)
  waiting for transfers between devices  4.31 us (14%)
    ppermute x9, starting transfers between devices, rotate(): lax.ppermute(value, axis, [(i, (i + shift) % size) for i in range(size)])  13.7 us
    pallas_call x10, Pallas kernels, call(): pl.pallas_call(body, in_specs=[vmem()] * len(args), out_specs=jax.tree.ma...  6.48 us
    ppermute x2, starting transfers between devices, steps(): lax.ppermute(swaps[i], 'param', pairs + [(b, a) for a, b in pairs])  5.01 us
    ppermute x9, waiting for transfers between devices, rotate(): lax.ppermute(value, axis, [(i, (i + shift) % size) for i in range(size)])  2.49 us
    ppermute x2, waiting for transfers between devices, steps(): lax.ppermute(swaps[i], 'param', pairs + [(b, a) for a, b in pairs])  1.82 us
  transfers between devices with their start and end apart: 11, of which 4 were waited for; matrix products, arithmetic and copies ran while one was open for 0% of the time, Pallas kernels for 11%

profile of v7, /device:TPU:1, one launch (start us, length us, event | category | flops | bytes accessed | tf_op | source)
XLA Modules:
  0.0 29.7 jit_solution(11866215412964142314)
XLA Ops:
  0.0 0.0 slice-start
  0.0 0.0 copy-start
  0.0 0.0 slice-start.1
  0.0 0.0 slice-start.2
  0.0 2.1 %collective-permute-start = (bf16[208,150]{1,0:T(8,128)(2,1)}, bf16[208,150]{1,0:T(8,128)(2,1)S(1)}, u32[]{:S(2)}, u32[]{:S(2)}) collective-permute-start(bf16[208,150]{1,0:T(8,128)(2,1)} %bitcast.13), channel_id=1, source_target_pairs={{0,16},{16,0},{1,17},{17,1},{2,18},{18,2},{3,19},{19,3},{4,20},{20... | collective-permute-start | bytes 187208 | tf_op jit(solution)/shard_map/ppermute | solution.py:232
  2.1 0.7 %shard_map.47 = (bf16[256,208]{1,0:T(8,128)(2,1)S(1)}, bf16[256,208]{1,0:T(8,128)(2,1)S(1)}, bf16[256,208]{1,0:T(8,128)(2,1)S(1)}, bf16[256,208]{1,0:T(8,128)(2,1)S(1)}, bf16[150,2400]{1,0:T(8,128)(2,1)S(1)}) custom-call(), custom_call_target="tpu_custom_call" | custom-call | flops 10000000000 | bytes 1145984 | tf_op jit(solution)/shard_map/pallas_call | solution.py:26
  2.8 0.0 copy-done
  2.8 0.2 shard_map.48.own
  3.0 2.0 %collective-permute-done.refs_2_ = bf16[208,150]{1,0:T(8,128)(2,1)S(1)} collective-permute-done((bf16[208,150]{1,0:T(8,128)(2,1)}, bf16[208,150]{1,0:T(8,128)(2,1)S(1)}, u32[]{:S(2)}, u32[]{:S(2)}) %collective-permute-start) | collective-permute-done | bytes 62432 | tf_op jit(solution)/shard_map/ppermute | solution.py:232
  5.0 0.0 slice-done
  5.0 0.0 slice-done.1
  5.0 0.0 slice-done.2
  5.0 2.2 %shard_map.49 = (bf16[256,2400]{1,0:T(8,128)(2,1)S(1)}, bf16[256,2400]{1,0:T(8,128)(2,1)S(1)}, f32[64,512]{1,0:T(8,128)S(1)}, bf16[64,512]{1,0:T(8,128)(2,1)S(1)...) custom-call(f32[256,150]{1,0:T(8,128)S(1)} %shard_map.48.own, ...), custom_call_target="tpu_custom_call" | custom-call | bytes 13764672 | tf_op jit(solution)/shard_map/pallas_call | solution.py:26
  7.2 2.3 %collective-permute-start.1 = (bf16[64,512]{1,0:T(8,128)(2,1)S(1)}, bf16[64,512]{1,0:T(8,128)(2,1)S(1)}, u32[]{:S(2)}, u32[]{:S(2)}) collective-permute-start(bf16[64,512]{1,0:T(8,128)(2,1)S(1)} %get-tuple-element.40), channel_id=1, source_target_pairs={{0,2},{1,3},{2,0},{3,1},{4,6},{5,7},{6,4},{7,5},{8,10},{9,11},{10,... | collective-permute-start | bytes 196616 | tf_op jit(solution)/shard_map/ppermute | solution.py:232
  9.5 1.3 %collective-permute-start.2 = (bf16[64,512]{1,0:T(8,128)(2,1)S(1)}, bf16[64,512]{1,0:T(8,128)(2,1)S(1)}, u32[]{:S(2)}, u32[]{:S(2)}) collective-permute-start(bf16[64,512]{1,0:T(8,128)(2,1)S(1)} %get-tuple-element.41), channel_id=1, source_target_pairs={{0,1},{1,2},{2,3},{3,0},{4,5},{5,6},{6,7},{7,4},{8,9},{9,10},{10,1... | collective-permute-start | bytes 196616 | tf_op jit(solution)/shard_map/ppermute | solution.py:232
  10.8 2.0 %collective-permute-start.3 = (bf16[64,512]{1,0:T(8,128)(2,1)S(1)}, bf16[64,512]{1,0:T(8,128)(2,1)S(1)}, u32[]{:S(2)}, u32[]{:S(2)}) collective-permute-start(bf16[64,512]{1,0:T(8,128)(2,1)S(1)} %get-tuple-element.42), channel_id=1, source_target_pairs={{0,3},{1,0},{2,1},{3,2},{4,7},{5,4},{6,5},{7,6},{8,11},{9,8},{10,9... | collective-permute-start | bytes 196616 | tf_op jit(solution)/shard_map/ppermute | solution.py:232
  12.8 1.5 %shard_map.52 = (f32[64,512]{1,0:T(8,128)S(1)}, bf16[64,512]{1,0:T(8,128)(2,1)S(1)}, bf16[64,512]{1,0:T(8,128)(2,1)S(1)}, bf16[64,512]{1,0:T(8,128)(2,1)S(1)}) custom-call(bf16[256,2400]{1,0:T(8,128)(2,1)S(1)} %get-tuple-element.47.lhs_re, bf16[256,2400]{1,0:T(8,128)(2,1)S(1)} %get-tuple-element.48.lhs_im, bf16[4800,1024]{1,0:T(8,128)(2,1)S(1)} %bitcast.11), custom_call_target="tpu_custom_call" | custom-call | bytes 12615680 | tf_op jit(solution)/shard_map/pallas_call | solution.py:26
  14.3 0.0 copy-start.2
  14.3 0.0 copy-start.1
  14.4 0.1 collective-permute-start.7
  14.4 0.3 collective-permute-start.8
  14.7 0.0 collective-permute-done.1.refs_0_
  14.7 3.0 %collective-permute-start.9 = (bf16[64,512]{1,0:T(8,128)(2,1)S(1)}, bf16[64,512]{1,0:T(8,128)(2,1)S(1)}, u32[]{:S(2)}, u32[]{:S(2)}) collective-permute-start(bf16[64,512]{1,0:T(8,128)(2,1)S(1)} %get-tuple-element.56), channel_id=1, source_target_pairs={{0,3},{1,0},{2,1},{3,2},{4,7},{5,4},{6,5},{7,6},{8,11},{9,8},{10,9... | collective-permute-start | bytes 196616 | tf_op jit(solution)/shard_map/ppermute | solution.py:232
  17.8 0.0 copy-done.2
  17.8 0.4 %shard_map.46 = (bf16[112,64]{1,0:T(8,128)(2,1)S(1)}, bf16[112,64]{1,0:T(8,128)(2,1)S(1)}) custom-call(f32[1,16]{1,0:T(1,128)S(1)} %bitcast.17), custom_call_target="tpu_custom_call" | custom-call | bytes 28736 | tf_op jit(solution)/shard_map/pallas_call | solution.py:26
  18.2 0.0 collective-permute-done.2.refs_1_
  18.2 0.0 collective-permute-done.3.refs_2_
  18.2 0.3 shard_map.50
  18.4 1.3 %collective-permute-start.4 = (bf16[56,512]{1,0:T(8,128)(2,1)S(1)}, bf16[56,512]{1,0:T(8,128)(2,1)S(1)}, u32[]{:S(2)}, u32[]{:S(2)}) collective-permute-start(bf16[56,512]{1,0:T(8,128)(2,1)S(1)} %get-tuple-element.44), channel_id=1, source_target_pairs={{0,16},{16,0},{1,17},{17,1},{2,18},{18,2},{3,19},{19,3},{4,20},{20... | collective-permute-start | bytes 172040 | tf_op jit(solution)/shard_map/ppermute | solution.py:232
  19.7 0.0 collective-permute-done.7.refs_0_
  19.7 0.0 collective-permute-done.8.refs_1_
  19.7 0.3 collective-permute-done.9.refs_2_
  20.0 0.2 shard_map.54
  20.2 1.4 %collective-permute-start.10 = (bf16[56,512]{1,0:T(8,128)(2,1)S(1)}, bf16[56,512]{1,0:T(8,128)(2,1)S(1)}, u32[]{:S(2)}, u32[]{:S(2)}) collective-permute-start(bf16[56,512]{1,0:T(8,128)(2,1)S(1)} %get-tuple-element.58), channel_id=1, source_target_pairs={{0,16},{16,0},{1,17},{17,1},{2,18},{18,2},{3,19},{19,3},{4,20},{20... | collective-permute-start | bytes 172040 | tf_op jit(solution)/shard_map/ppermute | solution.py:232
  21.6 0.2 collective-permute-done.4.refs_1_
  21.8 0.0 copy-done.1
  21.8 0.1 shard_map.51
  21.9 3.8 %collective-permute-start.5 = (f32[8,128]{1,0:T(8,128)S(1)}, f32[8,128]{1,0:T(8,128)S(1)}, u32[]{:S(2)}, u32[]{:S(2)}) collective-permute-start(f32[8,128]{1,0:T(8,128)S(1)} %get-tuple-element.45), channel_id=1, source_target_pairs={{0,4},{8,12},{4,0},{12,8},{1,5},{9,13},{5,1},{13,9},{2,6},{10,14},... | collective-permute-start | bytes 12296 | tf_op jit(solution)/shard_map/ppermute | solution.py:287
  25.7 1.2 %collective-permute-start.6 = (f32[8,128]{1,0:T(8,128)S(1)}, f32[8,128]{1,0:T(8,128)S(1)}, u32[]{:S(2)}, u32[]{:S(2)}) collective-permute-start(f32[8,128]{1,0:T(8,128)S(1)} %get-tuple-element.46), channel_id=1, source_target_pairs={{4,8},{12,0},{8,4},{0,12},{5,9},{13,1},{9,5},{1,13},{6,10},{14,2},... | collective-permute-start | bytes 12296 | tf_op jit(solution)/shard_map/ppermute | solution.py:287
  26.9 0.0 collective-permute-done.10.refs_3_
  26.9 0.0 collective-permute-done.5.within
  26.9 1.8 %collective-permute-done.6.across = f32[8,128]{1,0:T(8,128)S(1)} collective-permute-done((f32[8,128]{1,0:T(8,128)S(1)}, f32[8,128]{1,0:T(8,128)S(1)}, u32[]{:S(2)}, u32[]{:S(2)}) %collective-permute-start.6) | collective-permute-done | bytes 4128 | tf_op jit(solution)/shard_map/ppermute | solution.py:287
  28.8 0.9 %shard_map.55 = f32[26,2,1024]{2,1,0:T(2,128)} custom-call(f32[1,1024]{1,0:T(1,128)S(1)} %bitcast.16, f32[8,128]{1,0:T(8,128)S(1)} %collective-permute-done.5.within, f32[8,128]{1,0:T(8,128)S(1)} %collective-permute-done.6.across, f32[56,512]{1,0:T(8,128)S(1)} %get-tuple-element.43.refs_0_, bf16[56,512]{1,0:T(8,128)(2,1)S(1)} %collective-permute-done.4.refs_1_, ...), custom_call_target="tpu_custom_call" | custom-call | bytes 569344 | tf_op jit(solution)/shard_map/pallas_call | solution.py:26
  (2 shorter events, 0.0 us)
Async XLA Ops:
  0.0 5.0 %slice-start = ((s8[9830400]{0:T(1024)(128)(4,1)}), s8[4194304]{0:T(1024)(128)(4,1)S(1)}, s32[]{:S(2)}) async-start(s8[9830400]{0:T(1024)(128)(4,1)} %bitcast.8), calls=%async_computation | async-start | bytes 8388608
  0.0 2.8 %copy-start = (bf16[8,150,26]{1,0,2:T(8,128)(2,1)S(1)}, bf16[8,150,26]{1,0,2:T(8,128)(2,1)}, u32[]{:S(2)}) copy-start(bf16[8,150,26]{1,0,2:T(8,128)(2,1)} %param.4) | copy-start | bytes 187204
  0.0 5.0 %slice-start.1 = ((s8[9830400]{0:T(1024)(128)(4,1)}), s8[4194304]{0:T(1024)(128)(4,1)S(1)}, s32[]{:S(2)}) async-start(s8[9830400]{0:T(1024)(128)(4,1)} %bitcast.8), calls=%async_computation.1 | async-start | bytes 8388608
  0.0 5.0 %slice-start.2 = ((s8[9830400]{0:T(1024)(128)(4,1)}), s8[1441792]{0:T(1024)(128)(4,1)S(1)}, s32[]{:S(2)}) async-start(s8[9830400]{0:T(1024)(128)(4,1)} %bitcast.8), calls=%async_computation.2 | async-start | bytes 2883584
  0.0 5.0 %collective-permute-start = (bf16[208,150]{1,0:T(8,128)(2,1)}, bf16[208,150]{1,0:T(8,128)(2,1)S(1)}, u32[]{:S(2)}, u32[]{:S(2)}) collective-permute-start(bf16[208,150]{1,0:T(8,128)(2,1)} %bitcast.13), channel_id=1, source_target_pairs={{0,16},{16,0},{1,17},{17,1},{2,18},{18,2},{3,19},{19,3},{4,20},{20... | collective-permute-start | bytes 187208 | tf_op jit(solution)/shard_map/ppermute | solution.py:232
  7.2 7.5 %collective-permute-start.1 = (bf16[64,512]{1,0:T(8,128)(2,1)S(1)}, bf16[64,512]{1,0:T(8,128)(2,1)S(1)}, u32[]{:S(2)}, u32[]{:S(2)}) collective-permute-start(bf16[64,512]{1,0:T(8,128)(2,1)S(1)} %get-tuple-element.40), channel_id=1, source_target_pairs={{0,2},{1,3},{2,0},{3,1},{4,6},{5,7},{6,4},{7,5},{8,10},{9,11},{10,... | collective-permute-start | bytes 196616 | tf_op jit(solution)/shard_map/ppermute | solution.py:232
  9.5 8.6 %collective-permute-start.2 = (bf16[64,512]{1,0:T(8,128)(2,1)S(1)}, bf16[64,512]{1,0:T(8,128)(2,1)S(1)}, u32[]{:S(2)}, u32[]{:S(2)}) collective-permute-start(bf16[64,512]{1,0:T(8,128)(2,1)S(1)} %get-tuple-element.41), channel_id=1, source_target_pairs={{0,1},{1,2},{2,3},{3,0},{4,5},{5,6},{6,7},{7,4},{8,9},{9,10},{10,1... | collective-permute-start | bytes 196616 | tf_op jit(solution)/shard_map/ppermute | solution.py:232
  10.8 7.3 %collective-permute-start.3 = (bf16[64,512]{1,0:T(8,128)(2,1)S(1)}, bf16[64,512]{1,0:T(8,128)(2,1)S(1)}, u32[]{:S(2)}, u32[]{:S(2)}) collective-permute-start(bf16[64,512]{1,0:T(8,128)(2,1)S(1)} %get-tuple-element.42), channel_id=1, source_target_pairs={{0,3},{1,0},{2,1},{3,2},{4,7},{5,4},{6,5},{7,6},{8,11},{9,8},{10,9... | collective-permute-start | bytes 196616 | tf_op jit(solution)/shard_map/ppermute | solution.py:232
  14.3 3.5 %copy-start.2 = (f32[16]{0:T(128)S(1)}, f32[16]{0:T(128)}, u32[]{:S(2)}) copy-start(f32[16]{0:T(128)} %param.6) | copy-start | bytes 196
  14.3 7.5 %copy-start.1 = (f32[1024]{0:T(1024)S(1)}, f32[1024]{0:T(1024)}, u32[]{:S(2)}) copy-start(f32[1024]{0:T(1024)} %param.7) | copy-start | bytes 12292
  14.4 5.4 %collective-permute-start.7 = (bf16[64,512]{1,0:T(8,128)(2,1)S(1)}, bf16[64,512]{1,0:T(8,128)(2,1)S(1)}, u32[]{:S(2)}, u32[]{:S(2)}) collective-permute-start(bf16[64,512]{1,0:T(8,128)(2,1)S(1)} %get-tuple-element.54), channel_id=1, source_target_pairs={{0,2},{1,3},{2,0},{3,1},{4,6},{5,7},{6,4},{7,5},{8,10},{9,11},{10,... | collective-permute-start | bytes 196616 | tf_op jit(solution)/shard_map/ppermute | solution.py:232
  14.4 5.3 %collective-permute-start.8 = (bf16[64,512]{1,0:T(8,128)(2,1)S(1)}, bf16[64,512]{1,0:T(8,128)(2,1)S(1)}, u32[]{:S(2)}, u32[]{:S(2)}) collective-permute-start(bf16[64,512]{1,0:T(8,128)(2,1)S(1)} %get-tuple-element.55), channel_id=1, source_target_pairs={{0,1},{1,2},{2,3},{3,0},{4,5},{5,6},{6,7},{7,4},{8,9},{9,10},{10,1... | collective-permute-start | bytes 196616 | tf_op jit(solution)/shard_map/ppermute | solution.py:232
  14.7 5.3 %collective-permute-start.9 = (bf16[64,512]{1,0:T(8,128)(2,1)S(1)}, bf16[64,512]{1,0:T(8,128)(2,1)S(1)}, u32[]{:S(2)}, u32[]{:S(2)}) collective-permute-start(bf16[64,512]{1,0:T(8,128)(2,1)S(1)} %get-tuple-element.56), channel_id=1, source_target_pairs={{0,3},{1,0},{2,1},{3,2},{4,7},{5,4},{6,5},{7,6},{8,11},{9,8},{10,9... | collective-permute-start | bytes 196616 | tf_op jit(solution)/shard_map/ppermute | solution.py:232
  18.4 3.4 %collective-permute-start.4 = (bf16[56,512]{1,0:T(8,128)(2,1)S(1)}, bf16[56,512]{1,0:T(8,128)(2,1)S(1)}, u32[]{:S(2)}, u32[]{:S(2)}) collective-permute-start(bf16[56,512]{1,0:T(8,128)(2,1)S(1)} %get-tuple-element.44), channel_id=1, source_target_pairs={{0,16},{16,0},{1,17},{17,1},{2,18},{18,2},{3,19},{19,3},{4,20},{20... | collective-permute-start | bytes 172040 | tf_op jit(solution)/shard_map/ppermute | solution.py:232
  20.2 6.7 %collective-permute-start.10 = (bf16[56,512]{1,0:T(8,128)(2,1)S(1)}, bf16[56,512]{1,0:T(8,128)(2,1)S(1)}, u32[]{:S(2)}, u32[]{:S(2)}) collective-permute-start(bf16[56,512]{1,0:T(8,128)(2,1)S(1)} %get-tuple-element.58), channel_id=1, source_target_pairs={{0,16},{16,0},{1,17},{17,1},{2,18},{18,2},{3,19},{19,3},{4,20},{20... | collective-permute-start | bytes 172040 | tf_op jit(solution)/shard_map/ppermute | solution.py:232
  21.9 5.0 %collective-permute-start.5 = (f32[8,128]{1,0:T(8,128)S(1)}, f32[8,128]{1,0:T(8,128)S(1)}, u32[]{:S(2)}, u32[]{:S(2)}) collective-permute-start(f32[8,128]{1,0:T(8,128)S(1)} %get-tuple-element.45), channel_id=1, source_target_pairs={{0,4},{8,12},{4,0},{12,8},{1,5},{9,13},{5,1},{13,9},{2,6},{10,14},... | collective-permute-start | bytes 12296 | tf_op jit(solution)/shard_map/ppermute | solution.py:287
  25.7 3.0 %collective-permute-start.6 = (f32[8,128]{1,0:T(8,128)S(1)}, f32[8,128]{1,0:T(8,128)S(1)}, u32[]{:S(2)}, u32[]{:S(2)}) collective-permute-start(f32[8,128]{1,0:T(8,128)S(1)} %get-tuple-element.46), channel_id=1, source_target_pairs={{4,8},{12,0},{8,4},{0,12},{5,9},{13,1},{9,5},{1,13},{6,10},{14,2},... | collective-permute-start | bytes 12296 | tf_op jit(solution)/shard_map/ppermute | solution.py:287
